TPU v7x, 32 devices: a whole 2x2x4 slice. The times are simulated.
32 devices in a mesh: samp: 16 (over z, x, core), var: 2 (over y).
Axes of the slice: x: 2, y: 2, z: 4, core: 2. Of those that a mesh axis runs over, the one named last changes fastest.
Arguments:
- genotypes: bfloat16 [17280, 8192], P('samp', 'var'), may hold values from 0 to 2, as said below
- residual: float32 [17280, 256], P('samp'), may hold values from -6 to 6
- coefficients: float32 [256, 8192], P('samp', 'var'), may hold values from -0.06 to 0.06
- penalty: float32 [8192], P('var'), may hold values from 0.2 to 3
- colors: int32 [2, 2], P(None, 'var'), may hold values from 0 to 1
Outputs:
- coefficients_out: float32 [256, 8192], P('samp', 'var')
- residual_out: float32 [17280, 256], P('samp')
Inputs may be any that keep to these rules, and one draw needn't show every extreme that they name: `genotypes`: dosages of a genotype, whole numbers. `colors`: entry (r, v) names which of the 2 blocks of group v is updated in round r.
All inputs are finite; a program needn't handle non-finite values.
Results may differ from a plain program's by a relative error of at most 0.014.
Values may be sent and summed in bfloat16 or wider, within the bound.
No kernel may reach another device: no remote copies, remote signals or barrier semaphores. Data moves between devices by JAX's collectives and lax.ppermute only.
A program may use at most 64 MiB of HBM per device.

v0:
```python
import jax
import jax.numpy as jnp
from jax import lax
from jax.sharding import PartitionSpec as P

BS = 2048
ROUNDS = 2
F32 = jnp.float32
BF16 = jnp.bfloat16


def stage_radices(size):
    radices = []
    while len(radices) < 2 and size % 2 == 0:
        radices.append(2)
        size //= 2
    if size > 1:
        radices.append(size)
    return radices


class Stage:
    def __init__(self, size, radix, stride):
        self.size, self.radix, self.stride = size, radix, stride
        self.digit = (lax.axis_index("samp") // stride) % radix

    def partner(self, digit, step):
        if self.radix & (self.radix - 1) == 0:
            return digit ^ step
        return (digit + step) % self.radix

    def source(self, digit, step):
        if self.radix & (self.radix - 1) == 0:
            return digit ^ step
        return (digit - step) % self.radix

    def pairs(self, step):
        out = []
        for i in range(self.size):
            d = (i // self.stride) % self.radix
            out.append((i, i + (self.partner(d, step) - d) * self.stride))
        return out

    def send(self, value, step):
        return lax.ppermute(value, "samp", self.pairs(step))


def stages(size):
    out, stride = [], 1
    for radix in stage_radices(size):
        out.append(Stage(size, radix, stride))
        stride *= radix
    return out


def pick(parts, index):
    value = parts[0]
    for i in range(1, len(parts)):
        value = jnp.where(index == i, parts[i], value)
    return value


def split_cols(value, radix):
    width = value.shape[-1] // radix
    return [value[..., i * width : (i + 1) * width] for i in range(radix)]


def ordered(stage, own, received):
    by_step = [own] + received
    out = []
    for digit in range(stage.radix):
        value = by_step[0]
        for step in range(1, stage.radix):
            value = jnp.where(stage.source(stage.digit, step) == digit, by_step[step], value)
        out.append(value)
    return out


def rounded_to_bf16(value):
    return lax.reduce_precision(value, 8, 7)


def split_bf16(value, terms):
    out = []
    for _ in range(terms):
        top = rounded_to_bf16(value)
        out.append(top.astype(BF16))
        value = value - top
    return out


def after(value, *others):
    return lax.optimization_barrier((value, *others))[0]


def scatter_stage(value, stage):
    parts = split_cols(value, stage.radix)
    own = pick(parts, stage.digit)
    received = [
        stage.send(pick(parts, stage.partner(stage.digit, step)), step) for step in range(1, stage.radix)
    ]
    return jnp.concatenate(ordered(stage, own, received), axis=-2)


def return_stage(value, stage, rows_axis):
    parts = [
        lax.index_in_dim(value, i, rows_axis, keepdims=True) for i in range(stage.radix)
    ]
    own = pick(parts, stage.digit)
    received = [
        stage.send(pick(parts, stage.partner(stage.digit, step)), step) for step in range(1, stage.radix)
    ]
    return ordered(stage, own, received)


def gather_stage(value, stage):
    received = [stage.send(value, step) for step in range(1, stage.radix)]
    return jnp.concatenate(ordered(stage, value, received), axis=-1)


def pad_rows(rows):
    return jnp.pad(rows, ((0, -rows.shape[0] % 16), (0, 0)))


class Moments:
    def __init__(self, counts, twos, samples):
        self.counts, self.twos, self.samples = counts, twos, samples


def sum_rows(resid_sum, width):
    size = resid_sum.shape[0]
    fit = min(width, size)
    rows = [
        jnp.pad(row.reshape(-1, fit), ((0, 0), (0, width - fit))) for row in split_bf16(resid_sum, 3)
    ]
    return jnp.concatenate(rows, axis=0)


def read_sums(rows, width, size):
    fit = min(width, size)
    return jnp.sum(rows.astype(F32).reshape(3, size // fit, width)[:, :, :fit], axis=0).reshape(size)


def merge_stage(stage, partial, resid_sum, counts, twos, samples, known=None):
    size, width = partial.shape[0], partial.shape[1] // stage.radix
    parts = split_cols(partial, stage.radix)
    count_parts, two_parts = split_cols(counts, stage.radix), split_cols(twos, stage.radix)
    sums = sum_rows(resid_sum, width)
    n_sum = sums.shape[0]
    partials = [pick(parts, stage.digit)]
    resid_sums = [resid_sum]
    moments = [(pick(count_parts, stage.digit), pick(two_parts, stage.digit))] if known is None else known
    sent = []
    for step in range(1, stage.radix):
        to = stage.partner(stage.digit, step)
        extra = sums
        if known is None:
            stats = split_bf16(pick(count_parts, to), 2) + split_bf16(pick(two_parts, to), 2)
            extra = jnp.concatenate([sums] + [row[None, :] for row in stats], axis=0)
        message = jnp.concatenate([pick(parts, to).astype(BF16), pad_rows(extra)], axis=0)
        sent.append(message)
        message = stage.send(message, step)
        partials.append(message[:size].astype(F32))
        tail = message[size:]
        resid_sums.append(read_sums(tail[:n_sum], width, size))
        if known is None:
            stats = tail[n_sum : n_sum + 4].astype(F32)
            moments.append((stats[0] + stats[1], stats[2] + stats[3]))
    count_mean = sum(m[0] for m in moments) / stage.radix
    sum_mean = sum(resid_sums) / stage.radix
    total = sum(partials)
    for s, m in zip(resid_sums, moments):
        total = total + (s - sum_mean)[:, None] * ((m[0] - count_mean) / samples)[None, :]
    return total, sum(resid_sums), moments, sent


def over_var(value):
    size = lax.axis_size("var")
    if size & (size - 1):
        total = lax.psum(value, "var")
        return total, jnp.zeros_like(total)
    step, other = 1, jnp.zeros_like(value)
    while step < size:
        value = value + other
        other = lax.ppermute(value.astype(BF16), "var", [(i, i ^ step) for i in range(size)]).astype(F32)
        value = rounded_to_bf16(value)
        step *= 2
    return value, other


def descent(genotypes, residual, coefficients, penalty, colors):
    samp = lax.axis_size("samp")
    local_samples = genotypes.shape[0]
    rows_own = coefficients.shape[0]
    phenotypes = rows_own * samp
    blocks = genotypes.shape[1] // BS
    width = BS // samp
    all_stages = stages(samp)
    early, last = all_stages[:-1], all_stages[-1]
    chunks = 2 if phenotypes % 256 == 0 else 1
    size = phenotypes // chunks

    old_columns = jnp.stack(
        [lax.dynamic_slice_in_dim(coefficients, colors[r, 0] * BS, BS, 1) for r in range(ROUNDS)]
    )
    for stage in early:
        old_gate = old_columns
        old_columns = scatter_stage(old_columns, stage)

    first = jnp.int32(0)
    for stage in all_stages:
        first = first * stage.radix + stage.digit
    first = first * width

    residuals = [residual[:, c * size : (c + 1) * size] for c in range(chunks)]
    pending = None
    new_columns = []
    gate = None
    for r in range(ROUNDS):
        start = colors[r, 0] * BS
        values = lax.dynamic_slice_in_dim(genotypes, start, BS, 1)
        seen = values if gate is None else lax.dynamic_slice_in_dim(after(genotypes, gate), start, BS, 1)
        wide = seen.astype(F32)
        counts = jnp.sum(wide, axis=0)
        twos = 0.5 * (jnp.sum(wide * wide, axis=0) - counts)
        local_mean = counts / local_samples

        partials, resid_sums, learned = [], [], []
        for c in range(chunks):
            if pending is not None:
                own, other = pending[c]
                if c:
                    other = after(other, *ahead)
                residuals[c] = residuals[c] - (own + other)
            rounded = residuals[c].astype(BF16)
            if r == 0:
                rounded = after(rounded, *([old_gate] if c == 0 else ahead))
            resid_sum = jnp.sum(rounded.astype(F32), axis=0)
            product = lax.dot_general(
                rounded, values, (((0,), (0,)), ((), ())), preferred_element_type=F32
            )
            partial = product - resid_sum[:, None] * local_mean[None, :]
            col_counts, col_twos, samples = counts, twos, local_samples
            for i, stage in enumerate(early):
                partial, resid_sum, moments, ahead = merge_stage(
                    stage,
                    partial,
                    resid_sum,
                    col_counts,
                    col_twos,
                    samples,
                    learned[i] if c else None,
                )
                if not c:
                    learned.append(moments)
                col_counts = sum(m[0] for m in learned[i])
                col_twos = sum(m[1] for m in learned[i])
                samples = samples * stage.radix
            partials.append(partial)
            resid_sums.append(resid_sum)
        if r == 0:
            old_columns = scatter_stage(old_columns, last)
        gradient, _, moments, _ = merge_stage(
            last,
            jnp.concatenate(partials, axis=0),
            jnp.concatenate(resid_sums, axis=0),
            col_counts,
            col_twos,
            samples,
        )
        counts = sum(m[0] for m in moments)
        twos = sum(m[1] for m in moments)
        total = local_samples * samp
        mean = counts / total
        scale = (counts + 2.0 * twos) - counts * mean
        old = old_columns[r]
        for before in range(r):
            old = jnp.where(colors[before, 0] == colors[r, 0], new_columns[before], old)
        weight = lax.dynamic_slice_in_dim(penalty, start + first, width, 0)
        shifted = old + gradient / scale[None, :]
        norm = jnp.sqrt(jnp.sum(shifted * shifted, axis=0) + 1e-06)
        shrink = jnp.maximum(0.0, 1.0 - weight * jnp.sqrt(phenotypes / scale) / norm)
        new = shrink[None, :] * shifted
        new_columns.append(new)
        change = (new - old).astype(BF16)
        means = pad_rows(jnp.concatenate([row[None, :] for row in split_bf16(mean, 3)], axis=0))
        message = jnp.concatenate([means, change], axis=0)
        gate = message
        gathered = gather_stage(message, last)
        lead = means.shape[0]
        cuts = [0] + [lead + size * (c + 1) for c in range(chunks)]
        pieces = [gathered[cuts[c] : cuts[c + 1]] for c in range(chunks)]
        received = []
        top = len(early) - 1
        for c in range(chunks):
            received.append([early[top].send(pieces[c], step) for step in range(1, early[top].radix)])
        pending = []
        for c in range(chunks):
            if c:
                received[c] = [after(value, product) for value in received[c]]
            piece = jnp.concatenate(ordered(early[top], pieces[c], received[c]), axis=-1)
            for i in reversed(range(top)):
                piece = gather_stage(piece, early[i])
            if c == 0:
                mean_rows, piece = piece[:lead], piece[lead:]
            shift = jnp.sum(
                lax.dot_general(
                    mean_rows, piece, (((1,), (1,)), ((), ())), preferred_element_type=F32
                ),
                axis=0,
            )
            product = lax.dot_general(
                values, piece, (((1,), (1,)), ((), ())), preferred_element_type=F32
            )
            product = product - shift[None, :]
            pending.append(over_var(product))

    for c in range(chunks):
        own, other = pending[c]
        residuals[c] = residuals[c] - (own + other)
    digits = [stage.radix for stage in reversed(all_stages)]
    home = after(jnp.stack(new_columns), product)
    home = home.reshape([ROUNDS] + digits + [rows_own, width])
    pieces = [home]
    for i, stage in reversed(list(enumerate(all_stages))):
        axis = 1 + len(all_stages) - 1 - i
        pieces = [return_stage(piece, stage, axis) for piece in pieces][0]
        pieces = [jnp.concatenate(pieces, axis=-1)]
    new_rows = pieces[0].reshape(ROUNDS, rows_own, BS)
    out = []
    for block in range(blocks):
        piece = coefficients[:, block * BS : (block + 1) * BS]
        for r in range(ROUNDS):
            piece = jnp.where(colors[r, 0] == block, new_rows[r], piece)
        out.append(piece)
    return (jnp.concatenate(out, axis=1), jnp.concatenate(residuals, axis=1))


def solution(mesh):
    placed = (P("samp", "var"), P("samp", None), P("samp", "var"), P("var"), P(None, "var"))
    return jax.shard_map(
        descent,
        mesh=mesh,
        in_specs=placed,
        out_specs=(P("samp", "var"), P("samp", None)),
        check_vma=False,
    )
```

profile of v0, /device:TPU:0, one launch (start us, length us, event | category | flops | bytes accessed | tf_op | source)
XLA Modules:
  0.0 171.7 jit_solution(10363859753820378460)
XLA Ops:
  0.6 1.4 fusion.249
  3.4 1.0 dynamic-slice_bitcast_fusion.1
  4.9 1.3 fusion.248
  6.4 3.5 %fusion = (f32[2048]{0:T(1024)S(1)}, f32[2048]{0:T(1024)S(1)}) fusion(bf16[1080,4096]{1,0:T(8,128)(2,1)} %param.5, s32[]{:T(128)S(6)} %select_n.1136), kind=kLoop, calls=%fused_computation.4 | loop fusion | flops 8843264 | bytes 4440068 | tf_op jit(solution)/shard_map/reduce_sum | solution.py:225
  9.9 3.2 %convolution_subtract_fusion.3 = f32[128,2048]{1,0:T(8,128)S(1)} fusion(bf16[1080,128]{1,0:T(8,128)(2,1)S(1)} %get-tuple-element.9, bf16[1080,4096]{1,0:T(8,128)(2,1)} %param.5, s32[]{:T(128)S(6)} %select_n.1136, f32[2048]{0:T(1024)S(1)} %get-tuple-element.180, f32[128]{0:T(128)S(1)} %convert_reduce_fusion.5), kind=kOutput, calls=%fused_computation.21 | convolution fusion | flops 566755328 | bytes 5757444 | tf_op jit(solution)/shard_map/dot_general | solution.py:239
  13.3 2.6 %collective-permute-start.8 = (f32[2,32,512]{2,1,0:T(8,128)S(1)}, f32[2,32,512]{2,1,0:T(8,128)S(1)}, u32[]{:S(2)}, u32[]{:S(2)}) collective-permute-start(f32[2,32,512]{2,1,0:T(8,128)S(1)} %broadcast_select_fusion.19), channel_id=1, source_target_pairs={{0,4},{2,6},{4,0},{6,2},{8,12},{10,14},{12,8},{14,10},{16,20},{18,... | collective-permute-start | bytes 393224 | tf_op jit(solution)/shard_map/ppermute | solution.py:45
  16.3 3.7 %collective-permute-done.8 = f32[2,32,512]{2,1,0:T(8,128)S(1)} collective-permute-done((f32[2,32,512]{2,1,0:T(8,128)S(1)}, f32[2,32,512]{2,1,0:T(8,128)S(1)}, u32[]{:S(2)}, u32[]{:S(2)}) %collective-permute-start.8) | collective-permute-done | bytes 131104 | tf_op jit(solution)/shard_map/ppermute | solution.py:45
  20.1 3.9 %collective-permute-start.9 = (f32[2,64,128]{2,1,0:T(8,128)S(1)}, f32[2,64,128]{2,1,0:T(8,128)S(1)}, u32[]{:S(2)}, u32[]{:S(2)}) collective-permute-start(f32[2,64,128]{2,1,0:T(8,128)S(1)} %get-tuple-element.160), channel_id=1, source_target_pairs={{0,24},{2,26},{4,28},{6,30},{8,16},{10,18},{12,20},{14,22},{16,8},... | collective-permute-start | bytes 196616 | tf_op jit(solution)/shard_map/ppermute | solution.py:45
  25.3 3.2 %convolution_subtract_fusion.2 = f32[128,2048]{1,0:T(8,128)S(1)} fusion(bf16[1080,128]{1,0:T(8,128)(2,1)S(1)} %get-tuple-element.10, bf16[1080,4096]{1,0:T(8,128)(2,1)} %param.5, s32[]{:T(128)S(6)} %select_n.1136, f32[128]{0:T(128)S(1)} %convert_reduce_fusion.4, f32[2048]{0:T(1024)S(1)} %get-tuple-element.180), kind=kOutput, calls=%fused_computation.20 | convolution fusion | flops 566755328 | bytes 5757444 | tf_op jit(solution)/shard_map/dot_general | solution.py:239
  28.6 1.7 %collective-permute-start.2 = (bf16[144,512]{1,0:T(8,128)(2,1)S(1)}, bf16[144,512]{1,0:T(8,128)(2,1)S(1)}, u32[]{:S(2)}, u32[]{:S(2)}) collective-permute-start(bf16[144,512]{1,0:T(8,128)(2,1)S(1)} %fusion.40), channel_id=1, source_target_pairs={{0,4},{2,6},{4,0},{6,2},{8,12},{10,14},{12,8},{14,10},{16,20},{18,... | collective-permute-start | bytes 442376 | tf_op jit(solution)/shard_map/ppermute | solution.py:45
  30.6 3.2 %collective-permute-done.2 = bf16[144,512]{1,0:T(8,128)(2,1)S(1)} collective-permute-done((bf16[144,512]{1,0:T(8,128)(2,1)S(1)}, bf16[144,512]{1,0:T(8,128)(2,1)S(1)}, u32[]{:S(2)}, u32[]{:S(2)}) %collective-permute-start.2) | collective-permute-done | bytes 147488 | tf_op jit(solution)/shard_map/ppermute | solution.py:45
  34.4 1.7 %collective-permute-start.4 = (bf16[144,512]{1,0:T(8,128)(2,1)S(1)}, bf16[144,512]{1,0:T(8,128)(2,1)S(1)}, u32[]{:S(2)}, u32[]{:S(2)}) collective-permute-start(bf16[144,512]{1,0:T(8,128)(2,1)S(1)} %fusion.41), channel_id=1, source_target_pairs={{0,4},{2,6},{4,0},{6,2},{8,12},{10,14},{12,8},{14,10},{16,20},{18,... | collective-permute-start | bytes 442376 | tf_op jit(solution)/shard_map/ppermute | solution.py:45
  36.1 3.5 %collective-permute-done.4 = bf16[144,512]{1,0:T(8,128)(2,1)S(1)} collective-permute-done((bf16[144,512]{1,0:T(8,128)(2,1)S(1)}, bf16[144,512]{1,0:T(8,128)(2,1)S(1)}, u32[]{:S(2)}, u32[]{:S(2)}) %collective-permute-start.4) | collective-permute-done | bytes 147488 | tf_op jit(solution)/shard_map/ppermute | solution.py:45
  40.0 3.8 %collective-permute-start.7 = (bf16[272,128]{1,0:T(8,128)(2,1)S(1)}, bf16[272,128]{1,0:T(8,128)(2,1)S(1)}, u32[]{:S(2)}, u32[]{:S(2)}) collective-permute-start(bf16[272,128]{1,0:T(8,128)(2,1)S(1)} %fusion.68), channel_id=1, source_target_pairs={{0,24},{2,26},{4,28},{6,30},{8,16},{10,18},{12,20},{14,22},{16,8},... | collective-permute-start | bytes 208904 | tf_op jit(solution)/shard_map/ppermute | solution.py:45
  44.0 0.7 collective-permute-start.5
  44.7 2.1 %collective-permute-done.7 = bf16[272,128]{1,0:T(8,128)(2,1)S(1)} collective-permute-done((bf16[272,128]{1,0:T(8,128)(2,1)S(1)}, bf16[272,128]{1,0:T(8,128)(2,1)S(1)}, u32[]{:S(2)}, u32[]{:S(2)}) %collective-permute-start.7) | collective-permute-done | bytes 69664 | tf_op jit(solution)/shard_map/ppermute | solution.py:45
  46.8 2.4 %collective-permute-done.6 = bf16[272,128]{1,0:T(8,128)(2,1)S(1)} collective-permute-done((bf16[272,128]{1,0:T(8,128)(2,1)S(1)}, bf16[272,128]{1,0:T(8,128)(2,1)S(1)}, u32[]{:S(2)}, u32[]{:S(2)}) %collective-permute-start.6) | collective-permute-done | bytes 69664 | tf_op jit(solution)/shard_map/ppermute | solution.py:45
  49.6 0.8 subtract_maximum_fusion.1
  50.5 1.6 collective-permute-start.12
  52.1 0.8 collective-permute-start.13
  52.9 2.0 %collective-permute-start.14 = (bf16[272,128]{1,0:T(8,128)(2,1)S(1)}, bf16[272,128]{1,0:T(8,128)(2,1)S(1)}, u32[]{:S(2)}, u32[]{:S(2)}) collective-permute-start(bf16[272,128]{1,0:T(8,128)(2,1)S(1)} %pad_maximum_fusion.27), channel_id=1, source_target_pairs={{0,8},{2,10},{4,12},{6,14},{8,0},{10,2},{12,4},{14,6},{16,24},{18,... | collective-permute-start | bytes 208904 | tf_op jit(solution)/shard_map/ppermute | solution.py:45
  54.9 1.7 %collective-permute-done.12 = bf16[272,128]{1,0:T(8,128)(2,1)S(1)} collective-permute-done((bf16[272,128]{1,0:T(8,128)(2,1)S(1)}, bf16[272,128]{1,0:T(8,128)(2,1)S(1)}, u32[]{:S(2)}, u32[]{:S(2)}) %collective-permute-start.12) | collective-permute-done | bytes 69664 | tf_op jit(solution)/shard_map/ppermute | solution.py:45
  56.7 0.8 collective-permute-done.13
  58.3 2.1 %collective-permute-start.15 = (bf16[144,512]{1,0:T(8,128)(2,1)S(1)}, bf16[144,512]{1,0:T(8,128)(2,1)S(1)}, u32[]{:S(2)}, u32[]{:S(2)}) collective-permute-start(bf16[144,512]{1,0:T(8,128)(2,1)S(1)} %slice.850), channel_id=1, source_target_pairs={{0,4},{2,6},{4,0},{6,2},{8,12},{10,14},{12,8},{14,10},{16,20},{18,... | collective-permute-start | bytes 442376 | tf_op jit(solution)/shard_map/ppermute | solution.py:45
  60.4 3.5 %fusion.1 = (f32[2048]{0:T(1024)S(1)}, f32[2048]{0:T(1024)S(1)}) fusion(bf16[1080,4096]{1,0:T(8,128)(2,1)} %param.5, s32[]{:T(128)S(6)} %select_n.1141), kind=kLoop, calls=%fused_computation.5 | loop fusion | flops 8843264 | bytes 4440068 | tf_op jit(solution)/shard_map/reduce_sum | solution.py:225
  64.2 1.7 collective-permute-start.20
  66.3 3.8 %fusion.251 = (bf16[1080,128]{1,0:T(8,128)(2,1)S(1)}, f32[1080,128]{1,0:T(8,128)S(1)}) fusion(f32[128]{0:T(128)S(1)} %convolution_reduce_fusion.3, bf16[144,1024]{1,0:T(8,128)(2,1)S(1)} %get-tuple-element.117, bf16[144,1024]{1,0:T(8,128)(2,1)S(1)} %get-tuple-element.118, bf16[1080,4096]{1,0:T(8,128)(2,1)} %param.5, s32[]{:T(128)S(6)} %select_n.1136), kind=kOutput, calls=%fused_computation.674 | convolution fusion | flops 567556096 | bytes 5843460 | tf_op jit(solution)/shard_map/dot_general | solution.py:312
  70.5 1.6 collective-permute-start.17
  72.4 7.0 %collective-permute-done.17 = bf16[1080,128]{1,0:T(8,128)(2,1)S(1)} collective-permute-done((bf16[1080,128]{1,0:T(8,128)(2,1)S(1)}, bf16[1080,128]{1,0:T(8,128)(2,1)S(1)}, u32[]{:S(2)}, u32[]{:S(2)}) %collective-permute-start.17) | collective-permute-done | bytes 276512 | tf_op jit(solution)/shard_map/ppermute | solution.py:185
  79.7 1.4 fusion.16
  81.2 0.7 fusion.34
  81.9 4.6 %fusion.250 = (bf16[1080,128]{1,0:T(8,128)(2,1)}, f32[1080,128]{1,0:T(8,128)}) fusion(f32[128]{0:T(128)S(1)} %convolution_reduce_fusion.2, bf16[128,1024]{1,0:T(8,128)(2,1)} %copy-done.5, bf16[128,1024]{1,0:T(8,128)(2,1)} %copy-done.4, bf16[1080,4096]{1,0:T(8,128)(2,1)} %param.5, s32[]{:T(128)S(6)} %select_n.1136), kind=kOutput, calls=%fused_computation.673 | convolution fusion | flops 567556096 | bytes 5777924 | tf_op jit(solution)/shard_map/dot_general | solution.py:312
  86.5 1.5 collective-permute-start.22
  89.4 6.4 %collective-permute-done.22 = bf16[1080,128]{1,0:T(8,128)(2,1)S(1)} collective-permute-done((bf16[1080,128]{1,0:T(8,128)(2,1)}, bf16[1080,128]{1,0:T(8,128)(2,1)S(1)}, u32[]{:S(2)}, u32[]{:S(2)}) %collective-permute-start.22) | collective-permute-done | bytes 276512 | tf_op jit(solution)/shard_map/ppermute | solution.py:185
  95.8 0.9 convert_element_type.727
  96.6 0.7 slice_convert_fusion.2
  97.4 0.7 slice_bitcast_fusion.3
  98.3 1.1 multiply_add_fusion.1
  99.6 1.7 collective-permute-start.19
  101.2 1.4 convert_reduce_fusion.2
  102.6 3.2 %fusion.19 = f32[128,2048]{1,0:T(8,128)S(1)} fusion(bf16[1080,4096]{1,0:T(8,128)(2,1)} %param.5, s32[]{:T(128)S(6)} %select_n.1141, f32[128]{0:T(128)S(1)} %get-tuple-element.52, f32[2048]{0:T(1024)S(1)} %get-tuple-element.172, f32[1080,128]{1,0:T(8,128)S(1)} %get-tuple-element.53), kind=kOutput, calls=%fused_computation.19 | convolution fusion | flops 566893568 | bytes 6033924 | tf_op jit(solution)/shard_map/dot_general | solution.py:239
  106.3 1.3 collective-permute-done.23
  108.5 5.4 %collective-permute-done.24 = bf16[144,512]{1,0:T(8,128)(2,1)S(1)} collective-permute-done((bf16[144,512]{1,0:T(8,128)(2,1)S(1)}, bf16[144,512]{1,0:T(8,128)(2,1)S(1)}, u32[]{:S(2)}, u32[]{:S(2)}) %collective-permute-start.24) | collective-permute-done | bytes 147488 | tf_op jit(solution)/shard_map/ppermute | solution.py:45
  114.4 2.8 %collective-permute-start.27 = (bf16[272,128]{1,0:T(8,128)(2,1)S(1)}, bf16[272,128]{1,0:T(8,128)(2,1)S(1)}, u32[]{:S(2)}, u32[]{:S(2)}) collective-permute-start(bf16[272,128]{1,0:T(8,128)(2,1)S(1)} %fusion.71), channel_id=1, source_target_pairs={{0,24},{2,26},{4,28},{6,30},{8,16},{10,18},{12,20},{14,22},{16,8},... | collective-permute-start | bytes 208904 | tf_op jit(solution)/shard_map/ppermute | solution.py:45
  117.4 1.7 collective-permute-start.25
  119.1 1.5 collective-permute-done.27
  120.6 2.8 %collective-permute-done.26 = bf16[272,128]{1,0:T(8,128)(2,1)S(1)} collective-permute-done((bf16[272,128]{1,0:T(8,128)(2,1)S(1)}, bf16[272,128]{1,0:T(8,128)(2,1)S(1)}, u32[]{:S(2)}, u32[]{:S(2)}) %collective-permute-start.26) | collective-permute-done | bytes 69664 | tf_op jit(solution)/shard_map/ppermute | solution.py:45
  123.8 0.8 subtract_maximum_fusion
  124.7 2.1 %collective-permute-start.28 = (bf16[272,128]{1,0:T(8,128)(2,1)S(1)}, bf16[272,128]{1,0:T(8,128)(2,1)S(1)}, u32[]{:S(2)}, u32[]{:S(2)}) collective-permute-start(bf16[272,128]{1,0:T(8,128)(2,1)S(1)} %pad_maximum_fusion.28), channel_id=1, source_target_pairs={{0,24},{2,26},{4,28},{6,30},{8,16},{10,18},{12,20},{14,22},{16,8},... | collective-permute-start | bytes 208904 | tf_op jit(solution)/shard_map/ppermute | solution.py:45
  126.8 2.3 %collective-permute-start.30 = (bf16[272,128]{1,0:T(8,128)(2,1)S(1)}, bf16[272,128]{1,0:T(8,128)(2,1)S(1)}, u32[]{:S(2)}, u32[]{:S(2)}) collective-permute-start(bf16[272,128]{1,0:T(8,128)(2,1)S(1)} %pad_maximum_fusion.28), channel_id=1, source_target_pairs={{0,8},{2,10},{4,12},{6,14},{8,0},{10,2},{12,4},{14,6},{16,24},{18,... | collective-permute-start | bytes 208904 | tf_op jit(solution)/shard_map/ppermute | solution.py:45
  129.1 1.9 %collective-permute-done.28 = bf16[272,128]{1,0:T(8,128)(2,1)S(1)} collective-permute-done((bf16[272,128]{1,0:T(8,128)(2,1)S(1)}, bf16[272,128]{1,0:T(8,128)(2,1)S(1)}, u32[]{:S(2)}, u32[]{:S(2)}) %collective-permute-start.28) | collective-permute-done | bytes 69664 | tf_op jit(solution)/shard_map/ppermute | solution.py:45
  131.0 2.2 %collective-permute-done.29 = bf16[272,128]{1,0:T(8,128)(2,1)S(1)} collective-permute-done((bf16[272,128]{1,0:T(8,128)(2,1)S(1)}, bf16[272,128]{1,0:T(8,128)(2,1)S(1)}, u32[]{:S(2)}, u32[]{:S(2)}) %collective-permute-start.29) | collective-permute-done | bytes 69664 | tf_op jit(solution)/shard_map/ppermute | solution.py:45
  133.8 5.3 %collective-permute-done.32 = bf16[144,512]{1,0:T(8,128)(2,1)S(1)} collective-permute-done((bf16[144,512]{1,0:T(8,128)(2,1)S(1)}, bf16[144,512]{1,0:T(8,128)(2,1)S(1)}, u32[]{:S(2)}, u32[]{:S(2)}) %collective-permute-start.32) | collective-permute-done | bytes 147488 | tf_op jit(solution)/shard_map/ppermute | solution.py:45
  139.9 1.0 collective-permute-done.33
  141.3 3.8 %fusion.253 = (bf16[1080,128]{1,0:T(8,128)(2,1)S(1)}, f32[1080,128]{1,0:T(8,128)S(1)}) fusion(f32[128]{0:T(128)S(1)} %convolution_reduce_fusion.1, bf16[144,1024]{1,0:T(8,128)(2,1)S(1)} %get-tuple-element.115, bf16[144,1024]{1,0:T(8,128)(2,1)S(1)} %get-tuple-element.116, bf16[1080,4096]{1,0:T(8,128)(2,1)} %param.5, s32[]{:T(128)S(6)} %select_n.1141), kind=kOutput, calls=%fused_computation.676 | convolution fusion | flops 567556096 | bytes 5843460 | tf_op jit(solution)/shard_map/dot_general | solution.py:312
  145.5 1.5 collective-permute-done.34
  147.4 1.3 fusion.252
  148.8 2.6 %collective-permute-start.35 = (f32[2,1,2,2,16,128]{5,4,3,2,1,0:T(8,128)S(1)}, f32[2,1,2,2,16,128]{5,4,3,2,1,0:T(8,128)S(1)}, u32[]{:S(2)}, u32[]{:S(2)}) collective-permute-start(f32[2,1,2,2,16,128]{5,4,3,2,1,0:T(8,128)S(1)} %get-tuple-element.151), channel_id=1, source_target_pairs={{0,24},{2,26},{4,28},{6,30},{8,16},{10,18},{12,20},{14,22},{16,8},... | collective-permute-start | bytes 196616 | tf_op jit(solution)/shard_map/ppermute | solution.py:45
  151.4 1.9 %collective-permute-start.37 = (f32[2,1,2,2,16,128]{5,4,3,2,1,0:T(8,128)S(1)}, f32[2,1,2,2,16,128]{5,4,3,2,1,0:T(8,128)S(1)}, u32[]{:S(2)}, u32[]{:S(2)}) collective-permute-start(f32[2,1,2,2,16,128]{5,4,3,2,1,0:T(8,128)S(1)} %get-tuple-element.150), channel_id=1, source_target_pairs={{0,8},{2,10},{4,12},{6,14},{8,0},{10,2},{12,4},{14,6},{16,24},{18,... | collective-permute-start | bytes 196616 | tf_op jit(solution)/shard_map/ppermute | solution.py:45
  155.9 1.6 collective-permute-start.40
  158.6 6.8 %collective-permute-done.40 = bf16[1080,128]{1,0:T(8,128)(2,1)S(1)} collective-permute-done((bf16[1080,128]{1,0:T(8,128)(2,1)S(1)}, bf16[1080,128]{1,0:T(8,128)(2,1)S(1)}, u32[]{:S(2)}, u32[]{:S(2)}) %collective-permute-start.40) | collective-permute-done | bytes 276512 | tf_op jit(solution)/shard_map/ppermute | solution.py:185
  165.7 4.0 %collective-permute-done.41 = bf16[1080,128]{1,0:T(8,128)(2,1)S(1)} collective-permute-done((bf16[1080,128]{1,0:T(8,128)(2,1)S(1)}, bf16[1080,128]{1,0:T(8,128)(2,1)S(1)}, u32[]{:S(2)}, u32[]{:S(2)}) %collective-permute-start.41) | collective-permute-done | bytes 276512 | tf_op jit(solution)/shard_map/ppermute | solution.py:185
  169.8 1.1 pad_maximum_fusion
  170.9 0.7 pad_maximum_fusion.16
  (328 shorter events, 13.2 us)
Async XLA Ops:
  4.4 8.8 %collective-permute-start = (f32[2,16,1024]{2,1,0:T(8,128)S(1)}, f32[2,16,1024]{2,1,0:T(8,128)S(1)}, u32[]{:S(2)}, u32[]{:S(2)}) collective-permute-start(f32[2,16,1024]{2,1,0:T(8,128)S(1)} %broadcast_select_fusion.23), channel_id=1, source_target_pairs={{0,2},{2,0},{4,6},{6,4},{8,10},{10,8},{12,14},{14,12},{16,18},{18,... | collective-permute-start | bytes 393224 | tf_op jit(solution)/shard_map/ppermute | solution.py:45
  13.3 6.7 %collective-permute-start.8 = (f32[2,32,512]{2,1,0:T(8,128)S(1)}, f32[2,32,512]{2,1,0:T(8,128)S(1)}, u32[]{:S(2)}, u32[]{:S(2)}) collective-permute-start(f32[2,32,512]{2,1,0:T(8,128)S(1)} %broadcast_select_fusion.19), channel_id=1, source_target_pairs={{0,4},{2,6},{4,0},{6,2},{8,12},{10,14},{12,8},{14,10},{16,20},{18,... | collective-permute-start | bytes 393224 | tf_op jit(solution)/shard_map/ppermute | solution.py:45
  16.0 8.6 %collective-permute-start.1 = (bf16[144,1024]{1,0:T(8,128)(2,1)S(1)}, bf16[144,1024]{1,0:T(8,128)(2,1)S(1)}, u32[]{:S(2)}, u32[]{:S(2)}) collective-permute-start(bf16[144,1024]{1,0:T(8,128)(2,1)S(1)} %fusion.32), channel_id=1, source_target_pairs={{0,2},{2,0},{4,6},{6,4},{8,10},{10,8},{12,14},{14,12},{16,18},{18,... | collective-permute-start | bytes 884744 | tf_op jit(solution)/shard_map/ppermute | solution.py:45
  20.1 10.4 %collective-permute-start.9 = (f32[2,64,128]{2,1,0:T(8,128)S(1)}, f32[2,64,128]{2,1,0:T(8,128)S(1)}, u32[]{:S(2)}, u32[]{:S(2)}) collective-permute-start(f32[2,64,128]{2,1,0:T(8,128)S(1)} %get-tuple-element.160), channel_id=1, source_target_pairs={{0,24},{2,26},{4,28},{6,30},{8,16},{10,18},{12,20},{14,22},{16,8},... | collective-permute-start | bytes 196616 | tf_op jit(solution)/shard_map/ppermute | solution.py:45
  24.0 6.5 %collective-permute-start.10 = (f32[2,64,128]{2,1,0:T(8,128)S(1)}, f32[2,64,128]{2,1,0:T(8,128)S(1)}, u32[]{:S(2)}, u32[]{:S(2)}) collective-permute-start(f32[2,64,128]{2,1,0:T(8,128)S(1)} %get-tuple-element.159), channel_id=1, source_target_pairs={{0,16},{2,18},{4,20},{6,22},{8,24},{10,26},{12,28},{14,30},{16,0},... | collective-permute-start | bytes 196616 | tf_op jit(solution)/shard_map/ppermute | solution.py:45
  24.0 6.5 %collective-permute-start.11 = (f32[2,64,128]{2,1,0:T(8,128)S(1)}, f32[2,64,128]{2,1,0:T(8,128)S(1)}, u32[]{:S(2)}, u32[]{:S(2)}) collective-permute-start(f32[2,64,128]{2,1,0:T(8,128)S(1)} %get-tuple-element.108), channel_id=1, source_target_pairs={{0,8},{2,10},{4,12},{6,14},{8,0},{10,2},{12,4},{14,6},{16,24},{18,... | collective-permute-start | bytes 196616 | tf_op jit(solution)/shard_map/ppermute | solution.py:45
  28.6 5.2 %collective-permute-start.2 = (bf16[144,512]{1,0:T(8,128)(2,1)S(1)}, bf16[144,512]{1,0:T(8,128)(2,1)S(1)}, u32[]{:S(2)}, u32[]{:S(2)}) collective-permute-start(bf16[144,512]{1,0:T(8,128)(2,1)S(1)} %fusion.40), channel_id=1, source_target_pairs={{0,4},{2,6},{4,0},{6,2},{8,12},{10,14},{12,8},{14,10},{16,20},{18,... | collective-permute-start | bytes 442376 | tf_op jit(solution)/shard_map/ppermute | solution.py:45
  30.4 3.6 %collective-permute-start.3 = (bf16[144,1024]{1,0:T(8,128)(2,1)S(1)}, bf16[144,1024]{1,0:T(8,128)(2,1)S(1)}, u32[]{:S(2)}, u32[]{:S(2)}) collective-permute-start(bf16[144,1024]{1,0:T(8,128)(2,1)S(1)} %fusion.33), channel_id=1, source_target_pairs={{0,2},{2,0},{4,6},{6,4},{8,10},{10,8},{12,14},{14,12},{16,18},{18,... | collective-permute-start | bytes 884744 | tf_op jit(solution)/shard_map/ppermute | solution.py:45
  34.4 5.2 %collective-permute-start.4 = (bf16[144,512]{1,0:T(8,128)(2,1)S(1)}, bf16[144,512]{1,0:T(8,128)(2,1)S(1)}, u32[]{:S(2)}, u32[]{:S(2)}) collective-permute-start(bf16[144,512]{1,0:T(8,128)(2,1)S(1)} %fusion.41), channel_id=1, source_target_pairs={{0,4},{2,6},{4,0},{6,2},{8,12},{10,14},{12,8},{14,10},{16,20},{18,... | collective-permute-start | bytes 442376 | tf_op jit(solution)/shard_map/ppermute | solution.py:45
  40.0 6.8 %collective-permute-start.7 = (bf16[272,128]{1,0:T(8,128)(2,1)S(1)}, bf16[272,128]{1,0:T(8,128)(2,1)S(1)}, u32[]{:S(2)}, u32[]{:S(2)}) collective-permute-start(bf16[272,128]{1,0:T(8,128)(2,1)S(1)} %fusion.68), channel_id=1, source_target_pairs={{0,24},{2,26},{4,28},{6,30},{8,16},{10,18},{12,20},{14,22},{16,8},... | collective-permute-start | bytes 208904 | tf_op jit(solution)/shard_map/ppermute | solution.py:45
  43.9 5.3 %collective-permute-start.6 = (bf16[272,128]{1,0:T(8,128)(2,1)S(1)}, bf16[272,128]{1,0:T(8,128)(2,1)S(1)}, u32[]{:S(2)}, u32[]{:S(2)}) collective-permute-start(bf16[272,128]{1,0:T(8,128)(2,1)S(1)} %fusion.67), channel_id=1, source_target_pairs={{0,16},{2,18},{4,20},{6,22},{8,24},{10,26},{12,28},{14,30},{16,0},... | collective-permute-start | bytes 208904 | tf_op jit(solution)/shard_map/ppermute | solution.py:45
  44.0 5.1 %collective-permute-start.5 = (bf16[272,128]{1,0:T(8,128)(2,1)S(1)}, bf16[272,128]{1,0:T(8,128)(2,1)S(1)}, u32[]{:S(2)}, u32[]{:S(2)}) collective-permute-start(bf16[272,128]{1,0:T(8,128)(2,1)S(1)} %fusion.66), channel_id=1, source_target_pairs={{0,8},{2,10},{4,12},{6,14},{8,0},{10,2},{12,4},{14,6},{16,24},{18,... | collective-permute-start | bytes 208904 | tf_op jit(solution)/shard_map/ppermute | solution.py:45
  49.6 8.7 %copy-start.1 = (f32[256,128]{1,0:T(8,128)}, f32[256,128]{1,0:T(8,128)S(1)}, u32[]{:S(2)}) copy-start(f32[256,128]{1,0:T(8,128)S(1)} %get-tuple-element.70) | copy-start | bytes 393220
  50.5 6.2 %collective-permute-start.12 = (bf16[272,128]{1,0:T(8,128)(2,1)S(1)}, bf16[272,128]{1,0:T(8,128)(2,1)S(1)}, u32[]{:S(2)}, u32[]{:S(2)}) collective-permute-start(bf16[272,128]{1,0:T(8,128)(2,1)S(1)} %pad_maximum_fusion.27), channel_id=1, source_target_pairs={{0,24},{2,26},{4,28},{6,30},{8,16},{10,18},{12,20},{14,22},{16,8},... | collective-permute-start | bytes 208904 | tf_op jit(solution)/shard_map/ppermute | solution.py:45
  52.1 5.4 %collective-permute-start.13 = (bf16[272,128]{1,0:T(8,128)(2,1)S(1)}, bf16[272,128]{1,0:T(8,128)(2,1)S(1)}, u32[]{:S(2)}, u32[]{:S(2)}) collective-permute-start(bf16[272,128]{1,0:T(8,128)(2,1)S(1)} %pad_maximum_fusion.27), channel_id=1, source_target_pairs={{0,16},{2,18},{4,20},{6,22},{8,24},{10,26},{12,28},{14,30},{16,0},... | collective-permute-start | bytes 208904 | tf_op jit(solution)/shard_map/ppermute | solution.py:45
  52.9 5.2 %collective-permute-start.14 = (bf16[272,128]{1,0:T(8,128)(2,1)S(1)}, bf16[272,128]{1,0:T(8,128)(2,1)S(1)}, u32[]{:S(2)}, u32[]{:S(2)}) collective-permute-start(bf16[272,128]{1,0:T(8,128)(2,1)S(1)} %pad_maximum_fusion.27), channel_id=1, source_target_pairs={{0,8},{2,10},{4,12},{6,14},{8,0},{10,2},{12,4},{14,6},{16,24},{18,... | collective-permute-start | bytes 208904 | tf_op jit(solution)/shard_map/ppermute | solution.py:45
  58.3 5.6 %collective-permute-start.15 = (bf16[144,512]{1,0:T(8,128)(2,1)S(1)}, bf16[144,512]{1,0:T(8,128)(2,1)S(1)}, u32[]{:S(2)}, u32[]{:S(2)}) collective-permute-start(bf16[144,512]{1,0:T(8,128)(2,1)S(1)} %slice.850), channel_id=1, source_target_pairs={{0,4},{2,6},{4,0},{6,2},{8,12},{10,14},{12,8},{14,10},{16,20},{18,... | collective-permute-start | bytes 442376 | tf_op jit(solution)/shard_map/ppermute | solution.py:45
  60.4 19.2 %slice-start = ((s8[8847360]{0:T(1024)(128)(4,1)}), s8[458752]{0:T(1024)(128)(4,1)S(1)}, s32[]{:S(2)}) async-start(s8[8847360]{0:T(1024)(128)(4,1)} %bitcast.300), calls=%async_computation | async-start | bytes 917504
  64.1 1.8 %collective-permute-start.16 = (bf16[144,1024]{1,0:T(8,128)(2,1)S(1)}, bf16[144,1024]{1,0:T(8,128)(2,1)S(1)}, u32[]{:S(2)}, u32[]{:S(2)}) collective-permute-start(bf16[144,1024]{1,0:T(8,128)(2,1)S(1)} %pad_maximum_fusion.8), channel_id=1, source_target_pairs={{0,2},{2,0},{4,6},{6,4},{8,10},{10,8},{12,14},{14,12},{16,18},{18,... | collective-permute-start | bytes 884744 | tf_op jit(solution)/shard_map/ppermute | solution.py:45
  64.2 5.9 %collective-permute-start.20 = (bf16[128,512]{1,0:T(8,128)(2,1)S(1)}, bf16[128,512]{1,0:T(8,128)(2,1)S(1)}, u32[]{:S(2)}, u32[]{:S(2)}) collective-permute-start(bf16[128,512]{1,0:T(8,128)(2,1)S(1)} %pad_maximum_fusion.24), channel_id=1, source_target_pairs={{0,4},{2,6},{4,0},{6,2},{8,12},{10,14},{12,8},{14,10},{16,20},{18,... | collective-permute-start | bytes 393224 | tf_op jit(solution)/shard_map/ppermute | solution.py:45
  66.0 13.7 %slice-start.1 = ((s8[8847360]{0:T(1024)(128)(4,1)}), s8[4194304]{0:T(1024)(128)(4,1)S(1)}, s32[]{:S(2)}) async-start(s8[8847360]{0:T(1024)(128)(4,1)} %bitcast.300), calls=%async_computation.1 | async-start | bytes 8388608
  66.2 13.2 %copy-start = (f32[1080,256]{1,0:T(8,128)S(1)}, f32[1080,256]{1,0:T(8,128)}, u32[]{:S(2)}) copy-start(f32[1080,256]{1,0:T(8,128)} %param.6) | copy-start | bytes 3317764
  66.3 13.4 %slice-start.2 = ((s8[8847360]{0:T(1024)(128)(4,1)}), s8[4194304]{0:T(1024)(128)(4,1)S(1)}, s32[]{:S(2)}) async-start(s8[8847360]{0:T(1024)(128)(4,1)} %bitcast.300), calls=%async_computation.2 | async-start | bytes 8388608
  70.2 1.9 %collective-permute-start.21 = (bf16[128,1024]{1,0:T(8,128)(2,1)S(1)}, bf16[128,1024]{1,0:T(8,128)(2,1)S(1)}, u32[]{:S(2)}, u32[]{:S(2)}) collective-permute-start(bf16[128,1024]{1,0:T(8,128)(2,1)S(1)} %pad_maximum_fusion.12), channel_id=1, source_target_pairs={{0,2},{2,0},{4,6},{6,4},{8,10},{10,8},{12,14},{14,12},{16,18},{18,... | collective-permute-start | bytes 786440 | tf_op jit(solution)/shard_map/ppermute | solution.py:45
  70.5 8.9 %collective-permute-start.17 = (bf16[1080,128]{1,0:T(8,128)(2,1)S(1)}, bf16[1080,128]{1,0:T(8,128)(2,1)S(1)}, u32[]{:S(2)}, u32[]{:S(2)}) collective-permute-start(bf16[1080,128]{1,0:T(8,128)(2,1)S(1)} %get-tuple-element.254), channel_id=1, source_target_pairs={{0,1},{1,0},{2,3},{3,2},{4,5},{5,4},{6,7},{7,6},{8,9},{9,8},{10,11... | collective-permute-start | bytes 829448 | tf_op jit(solution)/shard_map/ppermute | solution.py:185
  72.2 8.9 %copy-start.4 = (bf16[128,1024]{1,0:T(8,128)(2,1)}, bf16[128,1024]{1,0:T(8,128)(2,1)S(1)}, u32[]{:S(2)}) copy-start(bf16[128,1024]{1,0:T(8,128)(2,1)S(1)} %get-tuple-element.125) | copy-start | bytes 786436
  72.2 8.9 %copy-start.5 = (bf16[128,1024]{1,0:T(8,128)(2,1)}, bf16[128,1024]{1,0:T(8,128)(2,1)S(1)}, u32[]{:S(2)}) copy-start(bf16[128,1024]{1,0:T(8,128)(2,1)S(1)} %get-tuple-element.126) | copy-start | bytes 786436
  81.9 14.7 %collective-permute-start.18 = (bf16[144,1024]{1,0:T(8,128)(2,1)}, bf16[144,1024]{1,0:T(8,128)(2,1)}, u32[]{:S(2)}, u32[]{:S(2)}) collective-permute-start(bf16[144,1024]{1,0:T(8,128)(2,1)} %fusion.34), channel_id=1, source_target_pairs={{0,2},{2,0},{4,6},{6,4},{8,10},{10,8},{12,14},{14,12},{16,18},{18,... | collective-permute-start | bytes 884744 | tf_op jit(solution)/shard_map/ppermute | solution.py:45
  86.5 9.2 %collective-permute-start.22 = (bf16[1080,128]{1,0:T(8,128)(2,1)}, bf16[1080,128]{1,0:T(8,128)(2,1)S(1)}, u32[]{:S(2)}, u32[]{:S(2)}) collective-permute-start(bf16[1080,128]{1,0:T(8,128)(2,1)} %get-tuple-element.252), channel_id=1, source_target_pairs={{0,1},{1,0},{2,3},{3,2},{4,5},{5,4},{6,7},{7,6},{8,9},{9,8},{10,11... | collective-permute-start | bytes 829448 | tf_op jit(solution)/shard_map/ppermute | solution.py:185
  99.6 6.5 %collective-permute-start.19 = (bf16[144,512]{1,0:T(8,128)(2,1)S(1)}, bf16[144,512]{1,0:T(8,128)(2,1)S(1)}, u32[]{:S(2)}, u32[]{:S(2)}) collective-permute-start(bf16[144,512]{1,0:T(8,128)(2,1)S(1)} %fusion.42), channel_id=1, source_target_pairs={{0,4},{2,6},{4,0},{6,2},{8,12},{10,14},{12,8},{14,10},{16,20},{18,... | collective-permute-start | bytes 442376 | tf_op jit(solution)/shard_map/ppermute | solution.py:45
  105.9 17.7 %copy-start.2 = (f32[256,128]{1,0:T(8,128)S(1)}, f32[256,128]{1,0:T(8,128)}, u32[]{:S(2)}) copy-start(f32[256,128]{1,0:T(8,128)} %copy-done.1) | copy-start | bytes 393220
  106.0 1.6 collective-permute-start.23
  108.0 6.0 %collective-permute-start.24 = (bf16[144,512]{1,0:T(8,128)(2,1)S(1)}, bf16[144,512]{1,0:T(8,128)(2,1)S(1)}, u32[]{:S(2)}, u32[]{:S(2)}) collective-permute-start(bf16[144,512]{1,0:T(8,128)(2,1)S(1)} %fusion.43), channel_id=1, source_target_pairs={{0,4},{2,6},{4,0},{6,2},{8,12},{10,14},{12,8},{14,10},{16,20},{18,... | collective-permute-start | bytes 442376 | tf_op jit(solution)/shard_map/ppermute | solution.py:45
  114.2 33.1 %slice-start.3 = ((s8[8847360]{0:T(1024)(128)(4,1)}), s8[458752]{0:T(1024)(128)(4,1)S(1)}, s32[]{:S(2)}) async-start(s8[8847360]{0:T(1024)(128)(4,1)} %bitcast.302), calls=%async_computation.3 | async-start | bytes 917504
  114.4 6.2 %collective-permute-start.27 = (bf16[272,128]{1,0:T(8,128)(2,1)S(1)}, bf16[272,128]{1,0:T(8,128)(2,1)S(1)}, u32[]{:S(2)}, u32[]{:S(2)}) collective-permute-start(bf16[272,128]{1,0:T(8,128)(2,1)S(1)} %fusion.71), channel_id=1, source_target_pairs={{0,24},{2,26},{4,28},{6,30},{8,16},{10,18},{12,20},{14,22},{16,8},... | collective-permute-start | bytes 208904 | tf_op jit(solution)/shard_map/ppermute | solution.py:45
  117.3 6.1 %collective-permute-start.26 = (bf16[272,128]{1,0:T(8,128)(2,1)S(1)}, bf16[272,128]{1,0:T(8,128)(2,1)S(1)}, u32[]{:S(2)}, u32[]{:S(2)}) collective-permute-start(bf16[272,128]{1,0:T(8,128)(2,1)S(1)} %fusion.70), channel_id=1, source_target_pairs={{0,16},{2,18},{4,20},{6,22},{8,24},{10,26},{12,28},{14,30},{16,0},... | collective-permute-start | bytes 208904 | tf_op jit(solution)/shard_map/ppermute | solution.py:45
  117.4 5.9 %collective-permute-start.25 = (bf16[272,128]{1,0:T(8,128)(2,1)S(1)}, bf16[272,128]{1,0:T(8,128)(2,1)S(1)}, u32[]{:S(2)}, u32[]{:S(2)}) collective-permute-start(bf16[272,128]{1,0:T(8,128)(2,1)S(1)} %fusion.69), channel_id=1, source_target_pairs={{0,8},{2,10},{4,12},{6,14},{8,0},{10,2},{12,4},{14,6},{16,24},{18,... | collective-permute-start | bytes 208904 | tf_op jit(solution)/shard_map/ppermute | solution.py:45
  124.7 6.4 %collective-permute-start.28 = (bf16[272,128]{1,0:T(8,128)(2,1)S(1)}, bf16[272,128]{1,0:T(8,128)(2,1)S(1)}, u32[]{:S(2)}, u32[]{:S(2)}) collective-permute-start(bf16[272,128]{1,0:T(8,128)(2,1)S(1)} %pad_maximum_fusion.28), channel_id=1, source_target_pairs={{0,24},{2,26},{4,28},{6,30},{8,16},{10,18},{12,20},{14,22},{16,8},... | collective-permute-start | bytes 208904 | tf_op jit(solution)/shard_map/ppermute | solution.py:45
  126.8 6.4 %collective-permute-start.29 = (bf16[272,128]{1,0:T(8,128)(2,1)S(1)}, bf16[272,128]{1,0:T(8,128)(2,1)S(1)}, u32[]{:S(2)}, u32[]{:S(2)}) collective-permute-start(bf16[272,128]{1,0:T(8,128)(2,1)S(1)} %pad_maximum_fusion.28), channel_id=1, source_target_pairs={{0,16},{2,18},{4,20},{6,22},{8,24},{10,26},{12,28},{14,30},{16,0},... | collective-permute-start | bytes 208904 | tf_op jit(solution)/shard_map/ppermute | solution.py:45
  126.8 6.4 %collective-permute-start.30 = (bf16[272,128]{1,0:T(8,128)(2,1)S(1)}, bf16[272,128]{1,0:T(8,128)(2,1)S(1)}, u32[]{:S(2)}, u32[]{:S(2)}) collective-permute-start(bf16[272,128]{1,0:T(8,128)(2,1)S(1)} %pad_maximum_fusion.28), channel_id=1, source_target_pairs={{0,8},{2,10},{4,12},{6,14},{8,0},{10,2},{12,4},{14,6},{16,24},{18,... | collective-permute-start | bytes 208904 | tf_op jit(solution)/shard_map/ppermute | solution.py:45
  133.3 5.8 %collective-permute-start.32 = (bf16[144,512]{1,0:T(8,128)(2,1)S(1)}, bf16[144,512]{1,0:T(8,128)(2,1)S(1)}, u32[]{:S(2)}, u32[]{:S(2)}) collective-permute-start(bf16[144,512]{1,0:T(8,128)(2,1)S(1)} %pad_maximum_fusion.17), channel_id=1, source_target_pairs={{0,4},{2,6},{4,0},{6,2},{8,12},{10,14},{12,8},{14,10},{16,20},{18,... | collective-permute-start | bytes 442376 | tf_op jit(solution)/shard_map/ppermute | solution.py:45
  139.2 1.6 collective-permute-start.33
  139.3 8.0 %slice-start.4 = ((s8[8847360]{0:T(1024)(128)(4,1)}), s8[4194304]{0:T(1024)(128)(4,1)S(1)}, s32[]{:S(2)}) async-start(s8[8847360]{0:T(1024)(128)(4,1)} %bitcast.302), calls=%async_computation.4 | async-start | bytes 8388608
  139.3 6.0 %collective-permute-start.31 = (bf16[128,512]{1,0:T(8,128)(2,1)S(1)}, bf16[128,512]{1,0:T(8,128)(2,1)S(1)}, u32[]{:S(2)}, u32[]{:S(2)}) collective-permute-start(bf16[128,512]{1,0:T(8,128)(2,1)S(1)} %pad_maximum_fusion.22), channel_id=1, source_target_pairs={{0,4},{2,6},{4,0},{6,2},{8,12},{10,14},{12,8},{14,10},{16,20},{18,... | collective-permute-start | bytes 393224 | tf_op jit(solution)/shard_map/ppermute | solution.py:45
  141.3 6.1 %slice-start.5 = ((s8[8847360]{0:T(1024)(128)(4,1)}), s8[4194304]{0:T(1024)(128)(4,1)S(1)}, s32[]{:S(2)}) async-start(s8[8847360]{0:T(1024)(128)(4,1)} %bitcast.302), calls=%async_computation.5 | async-start | bytes 8388608
  145.4 1.6 collective-permute-start.34
  148.8 9.2 %collective-permute-start.35 = (f32[2,1,2,2,16,128]{5,4,3,2,1,0:T(8,128)S(1)}, f32[2,1,2,2,16,128]{5,4,3,2,1,0:T(8,128)S(1)}, u32[]{:S(2)}, u32[]{:S(2)}) collective-permute-start(f32[2,1,2,2,16,128]{5,4,3,2,1,0:T(8,128)S(1)} %get-tuple-element.151), channel_id=1, source_target_pairs={{0,24},{2,26},{4,28},{6,30},{8,16},{10,18},{12,20},{14,22},{16,8},... | collective-permute-start | bytes 196616 | tf_op jit(solution)/shard_map/ppermute | solution.py:45
  151.4 6.6 %collective-permute-start.36 = (f32[2,1,2,2,16,128]{5,4,3,2,1,0:T(8,128)S(1)}, f32[2,1,2,2,16,128]{5,4,3,2,1,0:T(8,128)S(1)}, u32[]{:S(2)}, u32[]{:S(2)}) collective-permute-start(f32[2,1,2,2,16,128]{5,4,3,2,1,0:T(8,128)S(1)} %select_select_fusion.16), channel_id=1, source_target_pairs={{0,16},{2,18},{4,20},{6,22},{8,24},{10,26},{12,28},{14,30},{16,0},... | collective-permute-start | bytes 196616 | tf_op jit(solution)/shard_map/ppermute | solution.py:45
  151.4 6.6 %collective-permute-start.37 = (f32[2,1,2,2,16,128]{5,4,3,2,1,0:T(8,128)S(1)}, f32[2,1,2,2,16,128]{5,4,3,2,1,0:T(8,128)S(1)}, u32[]{:S(2)}, u32[]{:S(2)}) collective-permute-start(f32[2,1,2,2,16,128]{5,4,3,2,1,0:T(8,128)S(1)} %get-tuple-element.150), channel_id=1, source_target_pairs={{0,8},{2,10},{4,12},{6,14},{8,0},{10,2},{12,4},{14,6},{16,24},{18,... | collective-permute-start | bytes 196616 | tf_op jit(solution)/shard_map/ppermute | solution.py:45
  155.9 9.6 %collective-permute-start.40 = (bf16[1080,128]{1,0:T(8,128)(2,1)S(1)}, bf16[1080,128]{1,0:T(8,128)(2,1)S(1)}, u32[]{:S(2)}, u32[]{:S(2)}) collective-permute-start(bf16[1080,128]{1,0:T(8,128)(2,1)S(1)} %get-tuple-element.258), channel_id=1, source_target_pairs={{0,1},{1,0},{2,3},{3,2},{4,5},{5,4},{6,7},{7,6},{8,9},{9,8},{10,11... | collective-permute-start | bytes 829448 | tf_op jit(solution)/shard_map/ppermute | solution.py:185
  157.5 12.2 %collective-permute-start.41 = (bf16[1080,128]{1,0:T(8,128)(2,1)S(1)}, bf16[1080,128]{1,0:T(8,128)(2,1)S(1)}, u32[]{:S(2)}, u32[]{:S(2)}) collective-permute-start(bf16[1080,128]{1,0:T(8,128)(2,1)S(1)} %get-tuple-element.256), channel_id=1, source_target_pairs={{0,1},{1,0},{2,3},{3,2},{4,5},{5,4},{6,7},{7,6},{8,9},{9,8},{10,11... | collective-permute-start | bytes 829448 | tf_op jit(solution)/shard_map/ppermute | solution.py:185
  158.1 12.8 %copy-start.3 = (f32[16,4096]{1,0:T(8,128)S(1)}, f32[16,4096]{1,0:T(8,128)}, u32[]{:S(2)}) copy-start(f32[16,4096]{1,0:T(8,128)} %param.7) | copy-start | bytes 786436
  158.1 7.4 %collective-permute-start.38 = (f32[2,1,1,2,16,512]{5,4,3,2,1,0:T(8,128)S(1)}, f32[2,1,1,2,16,512]{5,4,3,2,1,0:T(8,128)S(1)}, u32[]{:S(2)}, u32[]{:S(2)}) collective-permute-start(f32[2,1,1,2,16,512]{5,4,3,2,1,0:T(8,128)S(1)} %slice_select_fusion.1), channel_id=1, source_target_pairs={{0,4},{2,6},{4,0},{6,2},{8,12},{10,14},{12,8},{14,10},{16,20},{18,... | collective-permute-start | bytes 393224 | tf_op jit(solution)/shard_map/ppermute | solution.py:45
  165.6 5.2 %collective-permute-start.39 = (f32[2,1,1,1,16,1024]{5,4,3,2,1,0:T(8,128)S(1)}, f32[2,1,1,1,16,1024]{5,4,3,2,1,0:T(8,128)S(1)}, u32[]{:S(2)}, u32[]{:S(2)}) collective-permute-start(f32[2,1,1,1,16,1024]{5,4,3,2,1,0:T(8,128)S(1)} %broadcast_select_fusion.28), channel_id=1, source_target_pairs={{0,2},{2,0},{4,6},{6,4},{8,10},{10,8},{12,14},{14,12},{16,18},{18,... | collective-permute-start | bytes 393224 | tf_op jit(solution)/shard_map/ppermute | solution.py:45
where the time goes:
time: 172 us
  waiting for transfers between devices  65.4 us (38%)
  starting transfers between devices  47.1 us (27%)
  matrix products  25.6 us (15%)
  other arithmetic  20.7 us (12%)
  between operations  7.66 us (4%)
  local copies, waits for them, and re-layouts  5.25 us (3%)
    ppermute x38, starting transfers between devices, send(): return lax.ppermute(value, 'samp', self.pairs(step))  42 us
    ppermute x38, waiting for transfers between devices, send(): return lax.ppermute(value, 'samp', self.pairs(step))  41.2 us
    ppermute x4, waiting for transfers between devices, over_var(): lax.ppermute(value.astype(BF16), 'var', [(i, i ^ step) for i in range(siz...  24.1 us
    dot_general x4, matrix products, descent(): lax.dot_general(values, piece, (((1,), (1,)), ((), ())), preferred_elemen...  13.5 us
    dot_general x4, matrix products, descent(): lax.dot_general(rounded, values, (((0,), (0,)), ((), ())), preferred_elem...  11.1 us
    reduce_sum x2, other arithmetic, descent(): twos = 0.5 * (jnp.sum(wide * wide, axis=0) - counts)  6.99 us
    ppermute x4, starting transfers between devices, over_var(): lax.ppermute(value.astype(BF16), 'var', [(i, i ^ step) for i in range(siz...  5.18 us
  transfers between devices with their start and end apart: 42, of which 23 were waited for; matrix products, arithmetic and copies ran while one was open for 22% of the time, Pallas kernels for 0%

commit v1 on v0

v1 whole, which is shorter than its diff:
```python
import jax
import jax.numpy as jnp
from jax import lax
from jax.experimental import pallas as pl
from jax.experimental.pallas import tpu as pltpu
from jax.sharding import PartitionSpec as P

BS = 2048
ROUNDS = 2
F32 = jnp.float32
BF16 = jnp.bfloat16


def stage_radices(size):
    radices = []
    while len(radices) < 2 and size % 2 == 0:
        radices.append(2)
        size //= 2
    if size > 1:
        radices.append(size)
    return radices


class Stage:
    def __init__(self, size, radix, stride):
        self.size, self.radix, self.stride = size, radix, stride
        self.digit = (lax.axis_index("samp") // stride) % radix

    def partner(self, digit, step):
        if self.radix & (self.radix - 1) == 0:
            return digit ^ step
        return (digit + step) % self.radix

    def source(self, digit, step):
        if self.radix & (self.radix - 1) == 0:
            return digit ^ step
        return (digit - step) % self.radix

    def pairs(self, step):
        out = []
        for i in range(self.size):
            d = (i // self.stride) % self.radix
            out.append((i, i + (self.partner(d, step) - d) * self.stride))
        return out

    def send(self, value, step):
        return lax.ppermute(value, "samp", self.pairs(step))


def stages(size):
    out, stride = [], 1
    for radix in stage_radices(size):
        out.append(Stage(size, radix, stride))
        stride *= radix
    return out


def pick(parts, index):
    value = parts[0]
    for i in range(1, len(parts)):
        value = jnp.where(index == i, parts[i], value)
    return value


def split_cols(value, radix):
    width = value.shape[-1] // radix
    return [value[..., i * width : (i + 1) * width] for i in range(radix)]


def ordered(stage, own, received):
    by_step = [own] + received
    out = []
    for digit in range(stage.radix):
        value = by_step[0]
        for step in range(1, stage.radix):
            value = jnp.where(stage.source(stage.digit, step) == digit, by_step[step], value)
        out.append(value)
    return out


def rounded_to_bf16(value):
    return lax.reduce_precision(value, 8, 7)


def split_bf16(value, terms):
    out = []
    for _ in range(terms):
        top = rounded_to_bf16(value)
        out.append(top.astype(BF16))
        value = value - top
    return out


def after(value, *others):
    return lax.optimization_barrier((value, *others))[0]


def scatter_stage(value, stage, gate=()):
    parts = split_cols(value, stage.radix)
    own = pick(parts, stage.digit)
    received = [
        stage.send(pick(parts, stage.partner(stage.digit, step)), step) for step in range(1, stage.radix)
    ]
    received = [after(value, *gate) for value in received]
    return jnp.concatenate(ordered(stage, own, received), axis=-2)


def home_stage(value, stage, axis, gate=()):
    parts = [lax.index_in_dim(value, i, axis, keepdims=False) for i in range(stage.radix)]
    own = pick(parts, stage.digit)
    received = [
        stage.send(pick(parts, stage.partner(stage.digit, step)), step) for step in range(1, stage.radix)
    ]
    received = [after(value, *gate) for value in received]
    return jnp.stack(ordered(stage, own, received))


def gather_stage(value, stage):
    received = [stage.send(value, step) for step in range(1, stage.radix)]
    return jnp.concatenate(ordered(stage, value, received), axis=-1)


def pad_rows(rows):
    return jnp.pad(rows, ((0, -rows.shape[0] % 16), (0, 0)))


def sum_rows(resid_sum, width):
    size = resid_sum.shape[0]
    fit = min(width, size)
    rows = [
        jnp.pad(row.reshape(-1, fit), ((0, 0), (0, width - fit))) for row in split_bf16(resid_sum, 3)
    ]
    return jnp.concatenate(rows, axis=0)


def read_sums(rows, width, size):
    fit = min(width, size)
    return jnp.sum(rows.astype(F32).reshape(3, size // fit, width)[:, :, :fit], axis=0).reshape(size)


def merge_stage(stage, partial, resid_sum, stats, samples, known=None, gate=()):
    size, width = partial.shape[0], partial.shape[1] // stage.radix
    n_stats = stats.shape[0]
    parts = split_cols(partial, stage.radix)
    stat_parts = split_cols(stats, stage.radix)
    sums = sum_rows(resid_sum, width)
    n_sum = sums.shape[0]
    partials = [pick(parts, stage.digit)]
    resid_sums = [resid_sum]
    members = [pick(stat_parts, stage.digit)] if known is None else known
    sent = []
    for step in range(1, stage.radix):
        to = stage.partner(stage.digit, step)
        extra = sums
        if known is None:
            extra = jnp.concatenate([sums] + split_bf16(pick(stat_parts, to), 2), axis=0)
        message = jnp.concatenate([pick(parts, to).astype(BF16), pad_rows(extra)], axis=0)
        sent.append(message)
        message = after(stage.send(message, step), *gate)
        partials.append(message[:size].astype(F32))
        tail = message[size:]
        resid_sums.append(read_sums(tail[:n_sum], width, size))
        if known is None:
            terms = tail[n_sum : n_sum + 2 * n_stats].astype(F32)
            members.append(terms[:n_stats] + terms[n_stats:])
    count_mean = sum(m[0] for m in members) / stage.radix
    sum_mean = sum(resid_sums) / stage.radix
    total = sum(partials)
    for s, m in zip(resid_sums, members):
        total = total + (s - sum_mean)[:, None] * ((m[0] - count_mean) / samples)[None, :]
    return total, sum(resid_sums), members, sent


def sum_stage(stage, partial):
    parts = split_cols(partial, stage.radix)
    total = pick(parts, stage.digit)
    sent = []
    for step in range(1, stage.radix):
        sent.append(pick(parts, stage.partner(stage.digit, step)).astype(BF16))
        total = total + stage.send(sent[-1], step).astype(F32)
    return total, sent


TILES = 4


def head_kernel(columns, genotypes, residual, partial, stats, resid_sum, blocks, sems):
    samples, phenotypes = residual.shape
    width = BS // TILES

    def copy(r, t):
        at = pl.multiple_of(columns[r] * BS + t * width, width)
        return pltpu.make_async_copy(
            genotypes.at[:, pl.ds(at, width)], blocks.at[r, :, pl.ds(t * width, width)], sems.at[r, t]
        )

    for r in range(ROUNDS):
        for t in range(TILES):
            copy(r, t).start()
    rounded = residual[...].astype(BF16)
    sums = jnp.sum(rounded.astype(F32), axis=0, keepdims=True)
    resid_sum[...] = sums
    column = jnp.broadcast_to(jnp.transpose(jnp.broadcast_to(sums, (8, phenotypes)))[:, :1], (phenotypes, width))
    for r in range(ROUNDS):
        for t in range(TILES):
            copy(r, t).wait()
            here = pl.ds(t * width, width)
            values = blocks[r, :, here]
            wide = values.astype(F32)
            counts = jnp.sum(wide, axis=0, keepdims=True)
            squares = jnp.sum(wide * wide, axis=0, keepdims=True)
            stats[2 * r : 2 * r + 1, here] = counts
            stats[2 * r + 1 : 2 * r + 2, here] = 0.5 * (squares - counts)
            if r == 0:
                product = lax.dot_general(
                    rounded, values, (((0,), (0,)), ((), ())), preferred_element_type=F32
                )
                partial[:, here] = product - column * (counts * (1.0 / samples))


def head(columns, genotypes, residual):
    samples, phenotypes = residual.shape
    whole = pl.BlockSpec(memory_space=pltpu.VMEM)
    return pl.pallas_call(
        head_kernel,
        out_shape=[
            jax.ShapeDtypeStruct((phenotypes, BS), F32),
            jax.ShapeDtypeStruct((2 * ROUNDS, BS), F32),
            jax.ShapeDtypeStruct((1, phenotypes), F32),
        ],
        in_specs=[pl.BlockSpec(memory_space=pltpu.SMEM), pl.BlockSpec(memory_space=pltpu.HBM), whole],
        out_specs=[whole] * 3,
        scratch_shapes=[pltpu.VMEM((ROUNDS, samples, BS), BF16), pltpu.SemaphoreType.DMA((ROUNDS, TILES))],
        cost_estimate=pl.CostEstimate(
            flops=4 * samples * phenotypes * BS, bytes_accessed=4 * samples * BS, transcendentals=0
        ),
        compiler_params=pltpu.CompilerParams(vmem_limit_bytes=50 * 1024 * 1024),
        name="head",
    )(columns, genotypes, residual)


def over_var(value):
    size = lax.axis_size("var")
    if size & (size - 1):
        total = lax.psum(value, "var")
        return total, jnp.zeros_like(total)
    step, other = 1, jnp.zeros_like(value)
    while step < size:
        value = value + other
        other = lax.ppermute(value.astype(BF16), "var", [(i, i ^ step) for i in range(size)]).astype(F32)
        value = rounded_to_bf16(value)
        step *= 2
    return value, other


def chosen_block(genotypes, block, gate):
    genotypes = after(genotypes, gate)
    return lax.optimization_barrier(lax.dynamic_slice_in_dim(genotypes, block * BS, BS, 1))


def descent(genotypes, residual, coefficients, penalty, colors):
    samp = lax.axis_size("samp")
    rows_own = coefficients.shape[0]
    phenotypes = rows_own * samp
    local_samples, total_samples = genotypes.shape[0], genotypes.shape[0] * samp
    width = BS // samp
    all_stages = stages(samp)
    early, last = all_stages[:-1], all_stages[-1]
    top = len(early) - 1
    chunks = 2 if phenotypes % 256 == 0 else 1
    size = phenotypes // chunks
    chosen = colors[:, 0]

    olds = [lax.dynamic_slice_in_dim(coefficients, chosen[r] * BS, BS, 1) for r in range(ROUNDS)]
    old_columns = jnp.stack(olds)
    partial, stats, resid_sum = head(chosen, genotypes, residual)
    values = []
    partial_chunks = [partial[c * size : (c + 1) * size] for c in range(chunks)]
    sum_chunks = [resid_sum[0, c * size : (c + 1) * size] for c in range(chunks)]

    first = jnp.int32(0)
    for stage in all_stages:
        first = first * stage.radix + stage.digit
    first = first * width

    for i in range(top):
        old_columns = scatter_stage(old_columns, early[i])
    learned, moments, samples = [], stats, local_samples
    ahead = ()
    for c in range(chunks):
        gate = ahead
        here, moments, samples = (partial_chunks[c], sum_chunks[c]), stats, local_samples
        for i, stage in enumerate(early):
            *here, members, ahead = merge_stage(
                stage, *here, moments, samples, learned[i] if c else None, () if i else gate
            )
            if not c:
                learned.append(members)
            moments, samples = sum(learned[i]), samples * stage.radix
        partial_chunks[c], sum_chunks[c] = here
    old_columns = scatter_stage(old_columns, early[top], ahead)
    old = scatter_stage(old_columns[0], last)
    gradient, _, members, _ = merge_stage(
        last, jnp.concatenate(partial_chunks, axis=0), jnp.concatenate(sum_chunks), moments, samples
    )
    moments = sum(members)

    residuals = [residual[:, c * size : (c + 1) * size] for c in range(chunks)]
    news = []
    for r in range(ROUNDS):
        counts, twos = moments[2 * r], moments[2 * r + 1]
        mean = counts / total_samples
        scale = (counts + 2.0 * twos) - counts * mean
        if r:
            ahead = ()
            for c in range(chunks):
                own, other = pending[c]
                if c:
                    other = after(other, *ahead)
                residuals[c] = residuals[c] - (own + other)
                rounded = residuals[c].astype(BF16)
                resid_sum = jnp.sum(rounded.astype(F32), axis=0)
                partial = lax.dot_general(rounded, values[r], (((0,), (0,)), ((), ())), preferred_element_type=F32)
                partial = partial - resid_sum[:, None] * means[r][None, :]
                for stage in early:
                    partial, ahead = sum_stage(stage, partial)
                partial_chunks[c] = partial
            old = scatter_stage(after(old_columns[r], *ahead), last)
            gradient, _ = sum_stage(last, jnp.concatenate(partial_chunks, axis=0))
            for before in range(r):
                old = jnp.where(chosen[before] == chosen[r], news[before], old)
        weight = lax.dynamic_slice_in_dim(penalty, chosen[r] * BS + first, width, 0)
        shifted = old + gradient / scale[None, :]
        norm = jnp.sqrt(jnp.sum(shifted * shifted, axis=0) + 1e-06)
        shrink = jnp.maximum(0.0, 1.0 - weight * jnp.sqrt(phenotypes / scale) / norm)
        new = shrink[None, :] * shifted
        news.append(new)
        change = (new - old).astype(BF16)
        means_sent = [mean] if r else [moments[2 * i] / total_samples for i in range(ROUNDS)]
        rows = [row[None, :] for sent in means_sent for row in split_bf16(sent, 3)]
        rows = pad_rows(jnp.concatenate(rows, axis=0))
        lead = rows.shape[0]
        message = jnp.concatenate([rows, change], axis=0)
        if r == 0:
            values.append(chosen_block(genotypes, chosen[0], message))
        gathered = gather_stage(message, last)
        cuts = [0] + [lead + size * (c + 1) for c in range(chunks)]
        pieces = [gathered[cuts[c] : cuts[c + 1]] for c in range(chunks)]
        received = []
        for c in range(chunks):
            received.append([early[top].send(pieces[c], step) for step in range(1, early[top].radix)])
        pending = []
        for c in range(chunks):
            if c:
                received[c] = [after(value, product) for value in received[c]]
            piece = jnp.concatenate(ordered(early[top], pieces[c], received[c]), axis=-1)
            for i in reversed(range(top)):
                piece = gather_stage(piece, early[i])
            if c == 0:
                rows, piece = piece[:lead], piece[lead:]
                if r == 0:
                    means = [jnp.sum(rows[3 * i : 3 * i + 3].astype(F32), axis=0) for i in range(ROUNDS)]
            shift = lax.dot_general(
                rows[:3], piece, (((1,), (1,)), ((), ())), preferred_element_type=F32
            )
            shift = jnp.sum(shift, axis=0)
            product = lax.dot_general(
                values[r], piece, (((1,), (1,)), ((), ())), preferred_element_type=F32
            )
            product = product - shift[None, :]
            pending.append(over_var(product))
        if r + 1 < ROUNDS:
            values.append(chosen_block(genotypes, chosen[r + 1], product))

    for c in range(chunks):
        own, other = pending[c]
        residuals[c] = residuals[c] - (own + other)

    home = jnp.stack(news).reshape(
        [ROUNDS] + [stage.radix for stage in reversed(all_stages)] + [rows_own, width]
    )
    axes = list(reversed(range(len(all_stages))))
    found = []
    for i in [top, top + 1] + list(reversed(range(top))):
        axis = len(found) + 1 + axes.index(i)
        home = home_stage(home, all_stages[i], axis, [product] if i == top else ())
        axes.remove(i)
        found.insert(0, i)
    home = jnp.transpose(home, [found.index(i) for i in range(len(found))] + [len(found) + j for j in range(3)])
    home = home.reshape(samp, ROUNDS, rows_own, width)
    new_rows = [jnp.concatenate([home[s, r] for s in range(samp)], axis=-1) for r in range(ROUNDS)]
    out = []
    for block in range(genotypes.shape[1] // BS):
        piece = coefficients[:, block * BS : (block + 1) * BS]
        for r in range(ROUNDS):
            piece = jnp.where(chosen[r] == block, new_rows[r], piece)
        out.append(piece)
    return (jnp.concatenate(out, axis=1), jnp.concatenate(residuals, axis=1))


def solution(mesh):
    placed = (P("samp", "var"), P("samp", None), P("samp", "var"), P("var"), P(None, "var"))
    return jax.shard_map(
        descent,
        mesh=mesh,
        in_specs=placed,
        out_specs=(P("samp", "var"), P("samp", None)),
        check_vma=False,
    )
```

time: 172 us -> 158 us (0.919)
  matrix products: 25.6 us -> 9.42 us
  other arithmetic: 20.7 us -> 10.8 us
  Pallas kernels: 0 us -> 5.05 us
  local copies, waits for them, and re-layouts: 5.25 us -> 9.67 us
  waiting for transfers between devices: 65.4 us -> 67.9 us
    dot_general x12 -> x10, matrix products: 25.6 us -> 9.42 us  [the longest x4 6.04 us: descent(): lax.dot_general(values[r], piece, (((1,), (1,)), ((), ())), preferred_ele...]
    reduce_sum x2 -> x1, other arithmetic: 6.99 us -> 0.03 us  [descent(): jnp.sum(rows[3 * i:3 * i + 3].astype(F32), axis=0)]
    ppermute x38 -> x41, waiting for transfers between devices: 41.2 us -> 46.6 us  [send(): return lax.ppermute(value, 'samp', self.pairs(step))]
    pallas_call x0 -> x1, Pallas kernels: none -> 5.05 us  [head(): pl.pallas_call(head_kernel, out_shape=[jax.ShapeDtypeStruct((phenotypes,...]
    dynamic_slice x0 -> x2, local copies, waits for them, and re-layouts: none -> 3.62 us  [chosen_block(): lax.dynamic_slice_in_dim(genotypes, block * BS, BS, 1)]
    ppermute x4, waiting for transfers between devices: 24.1 us -> 21.3 us  [over_var(): lax.ppermute(value.astype(BF16), 'var', [(i, i ^ step) for i in range(siz...]
    unnamed x24 -> x35, local copies, waits for them, and re-layouts: 0.08 us -> 2.01 us
    ppermute x38 -> x41, starting transfers between devices: 42 us -> 42 us  [send(): return lax.ppermute(value, 'samp', self.pairs(step))]
  transfers between devices with their start and end apart: 42 -> 45, of which waited for: 23 -> 28; matrix products, arithmetic and copies ran while one was open for 22% -> 12% of each run, Pallas kernels for 0% -> 3%
where the time goes in v1:
time: 158 us; the launch traced here: 157 us
  waiting for transfers between devices  67.9 us (43%)
  starting transfers between devices  47.3 us (30%)
  other arithmetic  10.8 us (7%)
  local copies, waits for them, and re-layouts  9.67 us (6%)
  matrix products  9.42 us (6%)
  between operations  7.04 us (4%)
  Pallas kernels  5.05 us (3%)
    ppermute x41, waiting for transfers between devices, send(): return lax.ppermute(value, 'samp', self.pairs(step))  46.6 us
    ppermute x41, starting transfers between devices, send(): return lax.ppermute(value, 'samp', self.pairs(step))  42 us
    ppermute x4, waiting for transfers between devices, over_var(): lax.ppermute(value.astype(BF16), 'var', [(i, i ^ step) for i in range(siz...  21.3 us
    dot_general x4, matrix products, descent(): lax.dot_general(values[r], piece, (((1,), (1,)), ((), ())), preferred_ele...  6.04 us
    ppermute x4, starting transfers between devices, over_var(): lax.ppermute(value.astype(BF16), 'var', [(i, i ^ step) for i in range(siz...  5.28 us
    pallas_call x1, Pallas kernels, head(): pl.pallas_call(head_kernel, out_shape=[jax.ShapeDtypeStruct((phenotypes,...  5.05 us
    dynamic_slice x2, local copies, waits for them, and re-layouts, chosen_block(): lax.dynamic_slice_in_dim(genotypes, block * BS, BS, 1)  3.62 us
  transfers between devices with their start and end apart: 45, of which 28 were waited for; matrix products, arithmetic and copies ran while one was open for 12% of the time, Pallas kernels for 3%

profile of v1, /device:TPU:0, one launch (start us, length us, event | category | flops | bytes accessed | tf_op | source)
XLA Modules:
  0.0 157.2 jit_solution(6594823084789348849)
XLA Ops:
  0.6 1.3 fusion.134
  3.3 1.0 dynamic-slice_bitcast_fusion.1
  4.8 1.2 copy-done
  6.7 5.0 %head.1 = (f32[256,2048]{1,0:T(8,128)S(1)}, f32[4,2048]{1,0:T(4,128)S(1)}, f32[1,256]{1,0:T(1,128)S(1)}) custom-call(s32[2]{0:T(128)S(1)} %bitcast.393, bf16[1080,4096]{1,0:T(8,128)(2,1)} %genotypes.1, f32[1080,256]{1,0:T(8,128)S(1)} %copy-done), custom_call_target="tpu_custom_call" | custom-call | flops 2264924160 | bytes 8847360 | tf_op jit(solution)/shard_map/head/pallas_call | solution.py:224
  13.1 2.8 %collective-permute-start.8 = (f32[2,32,512]{2,1,0:T(8,128)}, f32[2,32,512]{2,1,0:T(8,128)S(1)}, u32[]{:S(2)}, u32[]{:S(2)}) collective-permute-start(f32[2,32,512]{2,1,0:T(8,128)} %broadcast_select_fusion.23), channel_id=1, source_target_pairs={{0,4},{2,6},{4,0},{6,2},{8,12},{10,14},{12,8},{14,10},{16,20},{18,... | collective-permute-start | bytes 393224 | tf_op jit(solution)/shard_map/ppermute | solution.py:47
  15.9 0.8 slice_convert_fusion
  17.5 1.1 multiply_add_fusion.1
  19.8 4.8 %collective-permute-done.1 = bf16[144,512]{1,0:T(8,128)(2,1)S(1)} collective-permute-done((bf16[144,512]{1,0:T(8,128)(2,1)S(1)}, bf16[144,512]{1,0:T(8,128)(2,1)S(1)}, u32[]{:S(2)}, u32[]{:S(2)}) %collective-permute-start.1) | collective-permute-done | bytes 147488 | tf_op jit(solution)/shard_map/ppermute | solution.py:47
  25.0 1.2 collective-permute-start.3
  26.3 2.6 %collective-permute-start.10 = (f32[64,128]{1,0:T(8,128)S(1)}, f32[64,128]{1,0:T(8,128)S(1)}, u32[]{:S(2)}, u32[]{:S(2)}) collective-permute-start(f32[64,128]{1,0:T(8,128)S(1)} %select_select_fusion.25), channel_id=1, source_target_pairs={{0,16},{2,18},{4,20},{6,22},{8,24},{10,26},{12,28},{14,30},{16,0},... | collective-permute-start | bytes 98312 | tf_op jit(solution)/shard_map/ppermute | solution.py:47
  29.0 1.4 collective-permute-start.9
  31.2 3.5 %collective-permute-done.9 = f32[64,128]{1,0:T(8,128)S(1)} collective-permute-done((f32[64,128]{1,0:T(8,128)S(1)}, f32[64,128]{1,0:T(8,128)S(1)}, u32[]{:S(2)}, u32[]{:S(2)}) %collective-permute-start.9) | collective-permute-done | bytes 32800 | tf_op jit(solution)/shard_map/ppermute | solution.py:47
  35.3 2.1 %collective-permute-start.6 = (bf16[272,128]{1,0:T(8,128)(2,1)S(1)}, bf16[272,128]{1,0:T(8,128)(2,1)S(1)}, u32[]{:S(2)}, u32[]{:S(2)}) collective-permute-start(bf16[272,128]{1,0:T(8,128)(2,1)S(1)} %fusion.37), channel_id=1, source_target_pairs={{0,24},{2,26},{4,28},{6,30},{8,16},{10,18},{12,20},{14,22},{16,8},... | collective-permute-start | bytes 208904 | tf_op jit(solution)/shard_map/ppermute | solution.py:47
  37.9 2.4 %collective-permute-start.4 = (bf16[272,128]{1,0:T(8,128)(2,1)S(1)}, bf16[272,128]{1,0:T(8,128)(2,1)S(1)}, u32[]{:S(2)}, u32[]{:S(2)}) collective-permute-start(bf16[272,128]{1,0:T(8,128)(2,1)S(1)} %fusion.35), channel_id=1, source_target_pairs={{0,8},{2,10},{4,12},{6,14},{8,0},{10,2},{12,4},{14,6},{16,24},{18,... | collective-permute-start | bytes 208904 | tf_op jit(solution)/shard_map/ppermute | solution.py:47
  40.3 1.1 collective-permute-done.6
  41.5 1.6 %collective-permute-done.5 = bf16[272,128]{1,0:T(8,128)(2,1)S(1)} collective-permute-done((bf16[272,128]{1,0:T(8,128)(2,1)S(1)}, bf16[272,128]{1,0:T(8,128)(2,1)S(1)}, u32[]{:S(2)}, u32[]{:S(2)}) %collective-permute-start.5) | collective-permute-done | bytes 69664 | tf_op jit(solution)/shard_map/ppermute | solution.py:47
  43.8 0.8 subtract_maximum_fusion.1
  44.6 2.1 %collective-permute-start.12 = (bf16[272,128]{1,0:T(8,128)(2,1)S(1)}, bf16[272,128]{1,0:T(8,128)(2,1)S(1)}, u32[]{:S(2)}, u32[]{:S(2)}) collective-permute-start(bf16[272,128]{1,0:T(8,128)(2,1)S(1)} %fusion.34), channel_id=1, source_target_pairs={{0,24},{2,26},{4,28},{6,30},{8,16},{10,18},{12,20},{14,22},{16,8},... | collective-permute-start | bytes 208904 | tf_op jit(solution)/shard_map/ppermute | solution.py:47
  47.4 1.7 %collective-permute-start.14 = (bf16[272,128]{1,0:T(8,128)(2,1)S(1)}, bf16[272,128]{1,0:T(8,128)(2,1)S(1)}, u32[]{:S(2)}, u32[]{:S(2)}) collective-permute-start(bf16[272,128]{1,0:T(8,128)(2,1)S(1)} %fusion.34), channel_id=1, source_target_pairs={{0,8},{2,10},{4,12},{6,14},{8,0},{10,2},{12,4},{14,6},{16,24},{18,... | collective-permute-start | bytes 208904 | tf_op jit(solution)/shard_map/ppermute | solution.py:47
  49.1 1.7 %collective-permute-done.12 = bf16[272,128]{1,0:T(8,128)(2,1)S(1)} collective-permute-done((bf16[272,128]{1,0:T(8,128)(2,1)S(1)}, bf16[272,128]{1,0:T(8,128)(2,1)S(1)}, u32[]{:S(2)}, u32[]{:S(2)}) %collective-permute-start.12) | collective-permute-done | bytes 69664 | tf_op jit(solution)/shard_map/ppermute | solution.py:47
  50.8 1.7 %collective-permute-done.13 = bf16[272,128]{1,0:T(8,128)(2,1)S(1)} collective-permute-done((bf16[272,128]{1,0:T(8,128)(2,1)S(1)}, bf16[272,128]{1,0:T(8,128)(2,1)S(1)}, u32[]{:S(2)}, u32[]{:S(2)}) %collective-permute-start.13) | collective-permute-done | bytes 69664 | tf_op jit(solution)/shard_map/ppermute | solution.py:47
  52.6 0.9 collective-permute-start.16
  53.6 4.3 %collective-permute-done.16 = bf16[144,512]{1,0:T(8,128)(2,1)S(1)} collective-permute-done((bf16[144,512]{1,0:T(8,128)(2,1)S(1)}, bf16[144,512]{1,0:T(8,128)(2,1)S(1)}, u32[]{:S(2)}, u32[]{:S(2)}) %collective-permute-start.16) | collective-permute-done | bytes 147488 | tf_op jit(solution)/shard_map/ppermute | solution.py:47
  58.0 3.0 %constant_dynamic-slice_fusion.1 = bf16[1080,2048]{1,0:T(8,128)(2,1)S(1)} fusion(bf16[1080,4096]{1,0:T(8,128)(2,1)} %genotypes.1, s32[]{:T(128)S(6)} %select_n.1158), kind=kLoop, calls=%fused_computation.405 | loop fusion | bytes 8847364 | tf_op jit(solution)/shard_map/dynamic_slice | solution.py:258
  61.0 0.9 collective-permute-start.15
  62.4 1.5 fusion.136
  63.8 3.1 %collective-permute-done.15 = bf16[128,512]{1,0:T(8,128)(2,1)S(1)} collective-permute-done((bf16[128,512]{1,0:T(8,128)(2,1)S(1)}, bf16[128,512]{1,0:T(8,128)(2,1)S(1)}, u32[]{:S(2)}, u32[]{:S(2)}) %collective-permute-start.15) | collective-permute-done | bytes 131104 | tf_op jit(solution)/shard_map/ppermute | solution.py:47
  67.1 1.6 %collective-permute-start.20 = (bf16[1080,128]{1,0:T(8,128)(2,1)S(1)}, bf16[1080,128]{1,0:T(8,128)(2,1)S(1)}, u32[]{:S(2)}, u32[]{:S(2)}) collective-permute-start(bf16[1080,128]{1,0:T(8,128)(2,1)S(1)} %get-tuple-element.224), channel_id=1, source_target_pairs={{0,1},{1,0},{2,3},{3,2},{4,5},{5,4},{6,7},{7,6},{8,9},{9,8},{10,11... | collective-permute-start | bytes 829448 | tf_op jit(solution)/shard_map/ppermute | solution.py:250
  69.1 1.5 fusion.135
  71.3 4.8 %collective-permute-done.20 = bf16[1080,128]{1,0:T(8,128)(2,1)S(1)} collective-permute-done((bf16[1080,128]{1,0:T(8,128)(2,1)S(1)}, bf16[1080,128]{1,0:T(8,128)(2,1)S(1)}, u32[]{:S(2)}, u32[]{:S(2)}) %collective-permute-start.20) | collective-permute-done | bytes 276512 | tf_op jit(solution)/shard_map/ppermute | solution.py:250
  76.3 1.2 convolution_subtract_fusion.5
  77.7 1.6 %collective-permute-start.19 = (bf16[1080,128]{1,0:T(8,128)(2,1)S(1)}, bf16[1080,128]{1,0:T(8,128)(2,1)S(1)}, u32[]{:S(2)}, u32[]{:S(2)}) collective-permute-start(bf16[1080,128]{1,0:T(8,128)(2,1)S(1)} %get-tuple-element.222), channel_id=1, source_target_pairs={{0,1},{1,0},{2,3},{3,2},{4,5},{5,4},{6,7},{7,6},{8,9},{9,8},{10,11... | collective-permute-start | bytes 829448 | tf_op jit(solution)/shard_map/ppermute | solution.py:250
  80.0 6.6 %collective-permute-done.19 = bf16[1080,128]{1,0:T(8,128)(2,1)S(1)} collective-permute-done((bf16[1080,128]{1,0:T(8,128)(2,1)S(1)}, bf16[1080,128]{1,0:T(8,128)(2,1)S(1)}, u32[]{:S(2)}, u32[]{:S(2)}) %collective-permute-start.19) | collective-permute-done | bytes 276512 | tf_op jit(solution)/shard_map/ppermute | solution.py:250
  86.9 1.2 convolution_subtract_fusion.4
  89.6 0.9 collective-permute-start.26
  90.7 1.5 collective-permute-start.24
  92.2 1.9 %collective-permute-start.23 = (f32[64,128]{1,0:T(8,128)S(1)}, f32[64,128]{1,0:T(8,128)S(1)}, u32[]{:S(2)}, u32[]{:S(2)}) collective-permute-start(f32[64,128]{1,0:T(8,128)S(1)} %get-tuple-element.167), channel_id=1, source_target_pairs={{0,24},{2,26},{4,28},{6,30},{8,16},{10,18},{12,20},{14,22},{16,8},... | collective-permute-start | bytes 98312 | tf_op jit(solution)/shard_map/ppermute | solution.py:47
  94.3 1.4 collective-permute-done.26
  95.8 0.9 collective-permute-start.27
  96.8 1.3 collective-permute-done.23
  98.4 2.6 %collective-permute-done.27 = bf16[128,512]{1,0:T(8,128)(2,1)S(1)} collective-permute-done((bf16[128,512]{1,0:T(8,128)(2,1)S(1)}, bf16[128,512]{1,0:T(8,128)(2,1)S(1)}, u32[]{:S(2)}, u32[]{:S(2)}) %collective-permute-start.27) | collective-permute-done | bytes 131104 | tf_op jit(solution)/shard_map/ppermute | solution.py:47
  101.1 1.5 collective-permute-start.29
  102.6 1.8 %collective-permute-start.30 = (bf16[256,128]{1,0:T(8,128)(2,1)S(1)}, bf16[256,128]{1,0:T(8,128)(2,1)S(1)}, u32[]{:S(2)}, u32[]{:S(2)}) collective-permute-start(bf16[256,128]{1,0:T(8,128)(2,1)S(1)} %get-tuple-element.95), channel_id=1, source_target_pairs={{0,24},{2,26},{4,28},{6,30},{8,16},{10,18},{12,20},{14,22},{16,8},... | collective-permute-start | bytes 196616 | tf_op jit(solution)/shard_map/ppermute | solution.py:47
  104.6 3.0 %collective-permute-done.29 = bf16[256,128]{1,0:T(8,128)(2,1)S(1)} collective-permute-done((bf16[256,128]{1,0:T(8,128)(2,1)S(1)}, bf16[256,128]{1,0:T(8,128)(2,1)S(1)}, u32[]{:S(2)}, u32[]{:S(2)}) %collective-permute-start.29) | collective-permute-done | bytes 65568 | tf_op jit(solution)/shard_map/ppermute | solution.py:47
  107.6 1.1 collective-permute-done.30
  109.5 0.8 subtract_maximum_fusion
  110.3 1.9 %collective-permute-start.32 = (bf16[272,128]{1,0:T(8,128)(2,1)S(1)}, bf16[272,128]{1,0:T(8,128)(2,1)S(1)}, u32[]{:S(2)}, u32[]{:S(2)}) collective-permute-start(bf16[272,128]{1,0:T(8,128)(2,1)S(1)} %pad_maximum_fusion.28), channel_id=1, source_target_pairs={{0,24},{2,26},{4,28},{6,30},{8,16},{10,18},{12,20},{14,22},{16,8},... | collective-permute-start | bytes 208904 | tf_op jit(solution)/shard_map/ppermute | solution.py:47
  112.2 2.6 %collective-permute-start.34 = (bf16[272,128]{1,0:T(8,128)(2,1)S(1)}, bf16[272,128]{1,0:T(8,128)(2,1)S(1)}, u32[]{:S(2)}, u32[]{:S(2)}) collective-permute-start(bf16[272,128]{1,0:T(8,128)(2,1)S(1)} %pad_maximum_fusion.28), channel_id=1, source_target_pairs={{0,8},{2,10},{4,12},{6,14},{8,0},{10,2},{12,4},{14,6},{16,24},{18,... | collective-permute-start | bytes 208904 | tf_op jit(solution)/shard_map/ppermute | solution.py:47
  114.8 1.7 %collective-permute-done.32 = bf16[272,128]{1,0:T(8,128)(2,1)S(1)} collective-permute-done((bf16[272,128]{1,0:T(8,128)(2,1)S(1)}, bf16[272,128]{1,0:T(8,128)(2,1)S(1)}, u32[]{:S(2)}, u32[]{:S(2)}) %collective-permute-start.32) | collective-permute-done | bytes 69664 | tf_op jit(solution)/shard_map/ppermute | solution.py:47
  116.5 1.5 collective-permute-done.33
  118.1 0.9 collective-permute-start.36
  119.1 4.3 %collective-permute-done.36 = bf16[144,512]{1,0:T(8,128)(2,1)S(1)} collective-permute-done((bf16[144,512]{1,0:T(8,128)(2,1)S(1)}, bf16[144,512]{1,0:T(8,128)(2,1)S(1)}, u32[]{:S(2)}, u32[]{:S(2)}) %collective-permute-start.36) | collective-permute-done | bytes 147488 | tf_op jit(solution)/shard_map/ppermute | solution.py:47
  123.5 0.9 collective-permute-start.35
  125.5 1.4 fusion.138
  126.9 2.5 %collective-permute-done.35 = bf16[128,512]{1,0:T(8,128)(2,1)S(1)} collective-permute-done((bf16[128,512]{1,0:T(8,128)(2,1)S(1)}, bf16[128,512]{1,0:T(8,128)(2,1)S(1)}, u32[]{:S(2)}, u32[]{:S(2)}) %collective-permute-start.35) | collective-permute-done | bytes 131104 | tf_op jit(solution)/shard_map/ppermute | solution.py:47
  129.6 0.9 collective-permute-start.31
  131.5 1.7 %fusion.137 = (bf16[1080,128]{1,0:T(8,128)(2,1)S(1)}, f32[1080,128]{1,0:T(8,128)S(1)}) fusion(f32[128]{0:T(128)S(1)} %convolution_reduce_fusion, bf16[1080,2048]{1,0:T(8,128)(2,1)S(1)} %bitcast.395, bf16[128,1024]{1,0:T(8,128)(2,1)S(1)} %get-tuple-element.93, bf16[128,1024]{1,0:T(8,128)(2,1)S(1)} %get-tuple-element.92), kind=kOutput, calls=%fused_computation.483 | convolution fusion | flops 567556096 | bytes 5777920 | tf_op jit(solution)/shard_map/dot_general | solution.py:367
  133.2 2.4 %collective-permute-done.31 = f32[2,4,2,16,128]{4,3,2,1,0:T(8,128)S(1)} collective-permute-done((f32[2,4,2,16,128]{4,3,2,1,0:T(8,128)S(1)}, f32[2,4,2,16,128]{4,3,2,1,0:T(8,128)S(1)}, u32[]{:S(2)}, u32[]{:S(2)}) %collective-permute-start.31) | collective-permute-done | bytes 131104 | tf_op jit(solution)/shard_map/ppermute | solution.py:47
  135.7 1.9 %collective-permute-start.39 = (f32[2,2,2,16,128]{4,3,2,1,0:T(8,128)S(1)}, f32[2,2,2,16,128]{4,3,2,1,0:T(8,128)S(1)}, u32[]{:S(2)}, u32[]{:S(2)}) collective-permute-start(f32[2,2,2,16,128]{4,3,2,1,0:T(8,128)S(1)} %get-tuple-element.154), channel_id=1, source_target_pairs={{0,24},{2,26},{4,28},{6,30},{8,16},{10,18},{12,20},{14,22},{16,8},... | collective-permute-start | bytes 196616 | tf_op jit(solution)/shard_map/ppermute | solution.py:47
  138.3 1.8 %collective-permute-start.41 = (f32[2,2,2,16,128]{4,3,2,1,0:T(8,128)S(1)}, f32[2,2,2,16,128]{4,3,2,1,0:T(8,128)S(1)}, u32[]{:S(2)}, u32[]{:S(2)}) collective-permute-start(f32[2,2,2,16,128]{4,3,2,1,0:T(8,128)S(1)} %get-tuple-element.28), channel_id=1, source_target_pairs={{0,8},{2,10},{4,12},{6,14},{8,0},{10,2},{12,4},{14,6},{16,24},{18,... | collective-permute-start | bytes 196616 | tf_op jit(solution)/shard_map/ppermute | solution.py:47
  142.7 1.6 %collective-permute-start.43 = (bf16[1080,128]{1,0:T(8,128)(2,1)S(1)}, bf16[1080,128]{1,0:T(8,128)(2,1)S(1)}, u32[]{:S(2)}, u32[]{:S(2)}) collective-permute-start(bf16[1080,128]{1,0:T(8,128)(2,1)S(1)} %get-tuple-element.228), channel_id=1, source_target_pairs={{0,1},{1,0},{2,3},{3,2},{4,5},{5,4},{6,7},{7,6},{8,9},{9,8},{10,11... | collective-permute-start | bytes 829448 | tf_op jit(solution)/shard_map/ppermute | solution.py:250
  145.0 7.2 %collective-permute-done.43 = bf16[1080,128]{1,0:T(8,128)(2,1)S(1)} collective-permute-done((bf16[1080,128]{1,0:T(8,128)(2,1)S(1)}, bf16[1080,128]{1,0:T(8,128)(2,1)S(1)}, u32[]{:S(2)}, u32[]{:S(2)}) %collective-permute-start.43) | collective-permute-done | bytes 276512 | tf_op jit(solution)/shard_map/ppermute | solution.py:250
  153.4 2.6 %collective-permute-done.44 = bf16[1080,128]{1,0:T(8,128)(2,1)S(1)} collective-permute-done((bf16[1080,128]{1,0:T(8,128)(2,1)S(1)}, bf16[1080,128]{1,0:T(8,128)(2,1)S(1)}, u32[]{:S(2)}, u32[]{:S(2)}) %collective-permute-start.44) | collective-permute-done | bytes 276512 | tf_op jit(solution)/shard_map/ppermute | solution.py:250
  156.1 1.1 pad_maximum_fusion
  (228 shorter events, 18.2 us)
Async XLA Ops:
  4.3 8.1 %collective-permute-start.7 = (f32[2,16,1024]{2,1,0:T(8,128)S(1)}, f32[2,16,1024]{2,1,0:T(8,128)S(1)}, u32[]{:S(2)}, u32[]{:S(2)}) collective-permute-start(f32[2,16,1024]{2,1,0:T(8,128)S(1)} %broadcast_select_fusion.20), channel_id=1, source_target_pairs={{0,2},{2,0},{4,6},{6,4},{8,10},{10,8},{12,14},{14,12},{16,18},{18,... | collective-permute-start | bytes 393224 | tf_op jit(solution)/shard_map/ppermute | solution.py:47
  4.8 1.2 copy-start
  6.1 0.7 copy-start.2
  12.2 3.8 %collective-permute-start = (bf16[144,1024]{1,0:T(8,128)(2,1)S(1)}, bf16[144,1024]{1,0:T(8,128)(2,1)}, u32[]{:S(2)}, u32[]{:S(2)}) collective-permute-start(bf16[144,1024]{1,0:T(8,128)(2,1)S(1)} %fusion.4), channel_id=1, source_target_pairs={{0,2},{2,0},{4,6},{6,4},{8,10},{10,8},{12,14},{14,12},{16,18},{18,... | collective-permute-start | bytes 884744 | tf_op jit(solution)/shard_map/ppermute | solution.py:47
  13.1 13.2 %collective-permute-start.8 = (f32[2,32,512]{2,1,0:T(8,128)}, f32[2,32,512]{2,1,0:T(8,128)S(1)}, u32[]{:S(2)}, u32[]{:S(2)}) collective-permute-start(f32[2,32,512]{2,1,0:T(8,128)} %broadcast_select_fusion.23), channel_id=1, source_target_pairs={{0,4},{2,6},{4,0},{6,2},{8,12},{10,14},{12,8},{14,10},{16,20},{18,... | collective-permute-start | bytes 393224 | tf_op jit(solution)/shard_map/ppermute | solution.py:47
  18.9 5.7 %collective-permute-start.1 = (bf16[144,512]{1,0:T(8,128)(2,1)S(1)}, bf16[144,512]{1,0:T(8,128)(2,1)S(1)}, u32[]{:S(2)}, u32[]{:S(2)}) collective-permute-start(bf16[144,512]{1,0:T(8,128)(2,1)S(1)} %fusion.8), channel_id=1, source_target_pairs={{0,4},{2,6},{4,0},{6,2},{8,12},{10,14},{12,8},{14,10},{16,20},{18,... | collective-permute-start | bytes 442376 | tf_op jit(solution)/shard_map/ppermute | solution.py:47
  19.6 5.1 %collective-permute-start.2 = (bf16[144,1024]{1,0:T(8,128)(2,1)S(1)}, bf16[144,1024]{1,0:T(8,128)(2,1)S(1)}, u32[]{:S(2)}, u32[]{:S(2)}) collective-permute-start(bf16[144,1024]{1,0:T(8,128)(2,1)S(1)} %fusion.5), channel_id=1, source_target_pairs={{0,2},{2,0},{4,6},{6,4},{8,10},{10,8},{12,14},{14,12},{16,18},{18,... | collective-permute-start | bytes 884744 | tf_op jit(solution)/shard_map/ppermute | solution.py:47
  25.0 9.7 %collective-permute-start.3 = (bf16[144,512]{1,0:T(8,128)(2,1)S(1)}, bf16[144,512]{1,0:T(8,128)(2,1)S(1)}, u32[]{:S(2)}, u32[]{:S(2)}) collective-permute-start(bf16[144,512]{1,0:T(8,128)(2,1)S(1)} %fusion.9), channel_id=1, source_target_pairs={{0,4},{2,6},{4,0},{6,2},{8,12},{10,14},{12,8},{14,10},{16,20},{18,... | collective-permute-start | bytes 442376 | tf_op jit(solution)/shard_map/ppermute | solution.py:47
  26.3 4.9 %collective-permute-start.10 = (f32[64,128]{1,0:T(8,128)S(1)}, f32[64,128]{1,0:T(8,128)S(1)}, u32[]{:S(2)}, u32[]{:S(2)}) collective-permute-start(f32[64,128]{1,0:T(8,128)S(1)} %select_select_fusion.25), channel_id=1, source_target_pairs={{0,16},{2,18},{4,20},{6,22},{8,24},{10,26},{12,28},{14,30},{16,0},... | collective-permute-start | bytes 98312 | tf_op jit(solution)/shard_map/ppermute | solution.py:47
  29.0 5.7 %collective-permute-start.9 = (f32[64,128]{1,0:T(8,128)S(1)}, f32[64,128]{1,0:T(8,128)S(1)}, u32[]{:S(2)}, u32[]{:S(2)}) collective-permute-start(f32[64,128]{1,0:T(8,128)S(1)} %get-tuple-element.172), channel_id=1, source_target_pairs={{0,24},{2,26},{4,28},{6,30},{8,16},{10,18},{12,20},{14,22},{16,8},... | collective-permute-start | bytes 98312 | tf_op jit(solution)/shard_map/ppermute | solution.py:47
  30.3 4.4 %collective-permute-start.11 = (f32[64,128]{1,0:T(8,128)S(1)}, f32[64,128]{1,0:T(8,128)S(1)}, u32[]{:S(2)}, u32[]{:S(2)}) collective-permute-start(f32[64,128]{1,0:T(8,128)S(1)} %get-tuple-element.171), channel_id=1, source_target_pairs={{0,8},{2,10},{4,12},{6,14},{8,0},{10,2},{12,4},{14,6},{16,24},{18,... | collective-permute-start | bytes 98312 | tf_op jit(solution)/shard_map/ppermute | solution.py:47
  35.3 6.2 %collective-permute-start.6 = (bf16[272,128]{1,0:T(8,128)(2,1)S(1)}, bf16[272,128]{1,0:T(8,128)(2,1)S(1)}, u32[]{:S(2)}, u32[]{:S(2)}) collective-permute-start(bf16[272,128]{1,0:T(8,128)(2,1)S(1)} %fusion.37), channel_id=1, source_target_pairs={{0,24},{2,26},{4,28},{6,30},{8,16},{10,18},{12,20},{14,22},{16,8},... | collective-permute-start | bytes 208904 | tf_op jit(solution)/shard_map/ppermute | solution.py:47
  37.5 5.5 %collective-permute-start.5 = (bf16[272,128]{1,0:T(8,128)(2,1)S(1)}, bf16[272,128]{1,0:T(8,128)(2,1)S(1)}, u32[]{:S(2)}, u32[]{:S(2)}) collective-permute-start(bf16[272,128]{1,0:T(8,128)(2,1)S(1)} %fusion.36), channel_id=1, source_target_pairs={{0,16},{2,18},{4,20},{6,22},{8,24},{10,26},{12,28},{14,30},{16,0},... | collective-permute-start | bytes 208904 | tf_op jit(solution)/shard_map/ppermute | solution.py:47
  37.9 5.4 %collective-permute-start.4 = (bf16[272,128]{1,0:T(8,128)(2,1)S(1)}, bf16[272,128]{1,0:T(8,128)(2,1)S(1)}, u32[]{:S(2)}, u32[]{:S(2)}) collective-permute-start(bf16[272,128]{1,0:T(8,128)(2,1)S(1)} %fusion.35), channel_id=1, source_target_pairs={{0,8},{2,10},{4,12},{6,14},{8,0},{10,2},{12,4},{14,6},{16,24},{18,... | collective-permute-start | bytes 208904 | tf_op jit(solution)/shard_map/ppermute | solution.py:47
  44.6 6.2 %collective-permute-start.12 = (bf16[272,128]{1,0:T(8,128)(2,1)S(1)}, bf16[272,128]{1,0:T(8,128)(2,1)S(1)}, u32[]{:S(2)}, u32[]{:S(2)}) collective-permute-start(bf16[272,128]{1,0:T(8,128)(2,1)S(1)} %fusion.34), channel_id=1, source_target_pairs={{0,24},{2,26},{4,28},{6,30},{8,16},{10,18},{12,20},{14,22},{16,8},... | collective-permute-start | bytes 208904 | tf_op jit(solution)/shard_map/ppermute | solution.py:47
  46.7 5.8 %collective-permute-start.13 = (bf16[272,128]{1,0:T(8,128)(2,1)S(1)}, bf16[272,128]{1,0:T(8,128)(2,1)S(1)}, u32[]{:S(2)}, u32[]{:S(2)}) collective-permute-start(bf16[272,128]{1,0:T(8,128)(2,1)S(1)} %fusion.34), channel_id=1, source_target_pairs={{0,16},{2,18},{4,20},{6,22},{8,24},{10,26},{12,28},{14,30},{16,0},... | collective-permute-start | bytes 208904 | tf_op jit(solution)/shard_map/ppermute | solution.py:47
  47.4 5.1 %collective-permute-start.14 = (bf16[272,128]{1,0:T(8,128)(2,1)S(1)}, bf16[272,128]{1,0:T(8,128)(2,1)S(1)}, u32[]{:S(2)}, u32[]{:S(2)}) collective-permute-start(bf16[272,128]{1,0:T(8,128)(2,1)S(1)} %fusion.34), channel_id=1, source_target_pairs={{0,8},{2,10},{4,12},{6,14},{8,0},{10,2},{12,4},{14,6},{16,24},{18,... | collective-permute-start | bytes 208904 | tf_op jit(solution)/shard_map/ppermute | solution.py:47
  52.6 5.2 %collective-permute-start.16 = (bf16[144,512]{1,0:T(8,128)(2,1)S(1)}, bf16[144,512]{1,0:T(8,128)(2,1)S(1)}, u32[]{:S(2)}, u32[]{:S(2)}) collective-permute-start(bf16[144,512]{1,0:T(8,128)(2,1)S(1)} %pad_maximum_fusion.16), channel_id=1, source_target_pairs={{0,4},{2,6},{4,0},{6,2},{8,12},{10,14},{12,8},{14,10},{16,20},{18,... | collective-permute-start | bytes 442376 | tf_op jit(solution)/shard_map/ppermute | solution.py:47
  57.9 4.1 %collective-permute-start.17 = (bf16[144,1024]{1,0:T(8,128)(2,1)S(1)}, bf16[144,1024]{1,0:T(8,128)(2,1)S(1)}, u32[]{:S(2)}, u32[]{:S(2)}) collective-permute-start(bf16[144,1024]{1,0:T(8,128)(2,1)S(1)} %pad_maximum_fusion.7), channel_id=1, source_target_pairs={{0,2},{2,0},{4,6},{6,4},{8,10},{10,8},{12,14},{14,12},{16,18},{18,... | collective-permute-start | bytes 884744 | tf_op jit(solution)/shard_map/ppermute | solution.py:47
  58.0 12.6 %slice-start.2 = ((s8[8847360]{0:T(1024)(128)(4,1)}), s8[4194304]{0:T(1024)(128)(4,1)S(1)}, s32[]{:S(2)}) async-start(s8[8847360]{0:T(1024)(128)(4,1)} %bitcast.396), calls=%async_computation.2 | async-start | bytes 8388608
  61.0 9.6 %slice-start.3 = ((s8[8847360]{0:T(1024)(128)(4,1)}), s8[4194304]{0:T(1024)(128)(4,1)S(1)}, s32[]{:S(2)}) async-start(s8[8847360]{0:T(1024)(128)(4,1)} %bitcast.396), calls=%async_computation.3 | async-start | bytes 8388608
  61.0 5.9 %collective-permute-start.15 = (bf16[128,512]{1,0:T(8,128)(2,1)S(1)}, bf16[128,512]{1,0:T(8,128)(2,1)S(1)}, u32[]{:S(2)}, u32[]{:S(2)}) collective-permute-start(bf16[128,512]{1,0:T(8,128)(2,1)S(1)} %pad_maximum_fusion.22), channel_id=1, source_target_pairs={{0,4},{2,6},{4,0},{6,2},{8,12},{10,14},{12,8},{14,10},{16,20},{18,... | collective-permute-start | bytes 393224 | tf_op jit(solution)/shard_map/ppermute | solution.py:47
  67.0 3.6 %slice-start.4 = ((s8[8847360]{0:T(1024)(128)(4,1)}), s8[458752]{0:T(1024)(128)(4,1)S(1)}, s32[]{:S(2)}) async-start(s8[8847360]{0:T(1024)(128)(4,1)} %bitcast.396), calls=%async_computation.4 | async-start | bytes 917504
  67.0 1.7 %collective-permute-start.18 = (bf16[128,1024]{1,0:T(8,128)(2,1)S(1)}, bf16[128,1024]{1,0:T(8,128)(2,1)S(1)}, u32[]{:S(2)}, u32[]{:S(2)}) collective-permute-start(bf16[128,1024]{1,0:T(8,128)(2,1)S(1)} %pad_maximum_fusion.9), channel_id=1, source_target_pairs={{0,2},{2,0},{4,6},{6,4},{8,10},{10,8},{12,14},{14,12},{16,18},{18,... | collective-permute-start | bytes 786440 | tf_op jit(solution)/shard_map/ppermute | solution.py:47
  67.1 9.0 %collective-permute-start.20 = (bf16[1080,128]{1,0:T(8,128)(2,1)S(1)}, bf16[1080,128]{1,0:T(8,128)(2,1)S(1)}, u32[]{:S(2)}, u32[]{:S(2)}) collective-permute-start(bf16[1080,128]{1,0:T(8,128)(2,1)S(1)} %get-tuple-element.224), channel_id=1, source_target_pairs={{0,1},{1,0},{2,3},{3,2},{4,5},{5,4},{6,7},{7,6},{8,9},{9,8},{10,11... | collective-permute-start | bytes 829448 | tf_op jit(solution)/shard_map/ppermute | solution.py:250
  70.6 5.5 %copy-start.1 = (f32[1080,256]{1,0:T(8,128)S(1)}, f32[1080,256]{1,0:T(8,128)}, u32[]{:S(2)}) copy-start(f32[1080,256]{1,0:T(8,128)} %residual.1) | copy-start | bytes 3317764
  71.3 15.6 %copy-start.3 = (bf16[1080,2048]{1,0:T(8,128)(2,1)}, bf16[1080,2048]{1,0:T(8,128)(2,1)S(1)}, u32[]{:S(2)}) copy-start(bf16[1080,2048]{1,0:T(8,128)(2,1)S(1)} %constant_dynamic-slice_fusion) | copy-start | bytes 13271044
  77.6 1.7 %collective-permute-start.21 = (bf16[128,1024]{1,0:T(8,128)(2,1)S(1)}, bf16[128,1024]{1,0:T(8,128)(2,1)S(1)}, u32[]{:S(2)}, u32[]{:S(2)}) collective-permute-start(bf16[128,1024]{1,0:T(8,128)(2,1)S(1)} %select_convert_fusion.1), channel_id=1, source_target_pairs={{0,2},{2,0},{4,6},{6,4},{8,10},{10,8},{12,14},{14,12},{16,18},{18,... | collective-permute-start | bytes 786440 | tf_op jit(solution)/shard_map/ppermute | solution.py:47
  77.7 9.0 %collective-permute-start.19 = (bf16[1080,128]{1,0:T(8,128)(2,1)S(1)}, bf16[1080,128]{1,0:T(8,128)(2,1)S(1)}, u32[]{:S(2)}, u32[]{:S(2)}) collective-permute-start(bf16[1080,128]{1,0:T(8,128)(2,1)S(1)} %get-tuple-element.222), channel_id=1, source_target_pairs={{0,1},{1,0},{2,3},{3,2},{4,5},{5,4},{6,7},{7,6},{8,9},{9,8},{10,11... | collective-permute-start | bytes 829448 | tf_op jit(solution)/shard_map/ppermute | solution.py:250
  88.2 2.3 %collective-permute-start.22 = (bf16[128,1024]{1,0:T(8,128)(2,1)S(1)}, bf16[128,1024]{1,0:T(8,128)(2,1)S(1)}, u32[]{:S(2)}, u32[]{:S(2)}) collective-permute-start(bf16[128,1024]{1,0:T(8,128)(2,1)S(1)} %select_convert_fusion), channel_id=1, source_target_pairs={{0,2},{2,0},{4,6},{6,4},{8,10},{10,8},{12,14},{14,12},{16,18},{18,... | collective-permute-start | bytes 786440 | tf_op jit(solution)/shard_map/ppermute | solution.py:47
  89.6 6.2 %collective-permute-start.26 = (bf16[128,512]{1,0:T(8,128)(2,1)}, bf16[128,512]{1,0:T(8,128)(2,1)S(1)}, u32[]{:S(2)}, u32[]{:S(2)}) collective-permute-start(bf16[128,512]{1,0:T(8,128)(2,1)} %select_convert_fusion.5), channel_id=1, source_target_pairs={{0,4},{2,6},{4,0},{6,2},{8,12},{10,14},{12,8},{14,10},{16,20},{18,... | collective-permute-start | bytes 393224 | tf_op jit(solution)/shard_map/ppermute | solution.py:47
  90.5 35.0 %slice-start = ((s8[4423680]{0:T(1024)(128)(4,1)}), s8[4194304]{0:T(1024)(128)(4,1)S(1)}, s32[]{:S(2)}) async-start(s8[4423680]{0:T(1024)(128)(4,1)} %bitcast.394), calls=%async_computation | async-start | bytes 8388608
  90.7 6.1 %collective-permute-start.24 = (f32[64,128]{1,0:T(8,128)S(1)}, f32[64,128]{1,0:T(8,128)S(1)}, u32[]{:S(2)}, u32[]{:S(2)}) collective-permute-start(f32[64,128]{1,0:T(8,128)S(1)} %select_select_fusion.17), channel_id=1, source_target_pairs={{0,16},{2,18},{4,20},{6,22},{8,24},{10,26},{12,28},{14,30},{16,0},... | collective-permute-start | bytes 98312 | tf_op jit(solution)/shard_map/ppermute | solution.py:47
  92.2 5.8 %collective-permute-start.23 = (f32[64,128]{1,0:T(8,128)S(1)}, f32[64,128]{1,0:T(8,128)S(1)}, u32[]{:S(2)}, u32[]{:S(2)}) collective-permute-start(f32[64,128]{1,0:T(8,128)S(1)} %get-tuple-element.167), channel_id=1, source_target_pairs={{0,24},{2,26},{4,28},{6,30},{8,16},{10,18},{12,20},{14,22},{16,8},... | collective-permute-start | bytes 98312 | tf_op jit(solution)/shard_map/ppermute | solution.py:47
  94.1 4.3 %collective-permute-start.25 = (f32[64,128]{1,0:T(8,128)S(1)}, f32[64,128]{1,0:T(8,128)S(1)}, u32[]{:S(2)}, u32[]{:S(2)}) collective-permute-start(f32[64,128]{1,0:T(8,128)S(1)} %get-tuple-element.166), channel_id=1, source_target_pairs={{0,8},{2,10},{4,12},{6,14},{8,0},{10,2},{12,4},{14,6},{16,24},{18,... | collective-permute-start | bytes 98312 | tf_op jit(solution)/shard_map/ppermute | solution.py:47
  95.8 5.1 %collective-permute-start.27 = (bf16[128,512]{1,0:T(8,128)(2,1)S(1)}, bf16[128,512]{1,0:T(8,128)(2,1)S(1)}, u32[]{:S(2)}, u32[]{:S(2)}) collective-permute-start(bf16[128,512]{1,0:T(8,128)(2,1)S(1)} %select_convert_fusion.4), channel_id=1, source_target_pairs={{0,4},{2,6},{4,0},{6,2},{8,12},{10,14},{12,8},{14,10},{16,20},{18,... | collective-permute-start | bytes 393224 | tf_op jit(solution)/shard_map/ppermute | solution.py:47
  101.1 6.6 %collective-permute-start.29 = (bf16[256,128]{1,0:T(8,128)(2,1)S(1)}, bf16[256,128]{1,0:T(8,128)(2,1)S(1)}, u32[]{:S(2)}, u32[]{:S(2)}) collective-permute-start(bf16[256,128]{1,0:T(8,128)(2,1)S(1)} %get-tuple-element.94), channel_id=1, source_target_pairs={{0,16},{2,18},{4,20},{6,22},{8,24},{10,26},{12,28},{14,30},{16,0},... | collective-permute-start | bytes 196616 | tf_op jit(solution)/shard_map/ppermute | solution.py:47
  102.6 6.2 %collective-permute-start.30 = (bf16[256,128]{1,0:T(8,128)(2,1)S(1)}, bf16[256,128]{1,0:T(8,128)(2,1)S(1)}, u32[]{:S(2)}, u32[]{:S(2)}) collective-permute-start(bf16[256,128]{1,0:T(8,128)(2,1)S(1)} %get-tuple-element.95), channel_id=1, source_target_pairs={{0,24},{2,26},{4,28},{6,30},{8,16},{10,18},{12,20},{14,22},{16,8},... | collective-permute-start | bytes 196616 | tf_op jit(solution)/shard_map/ppermute | solution.py:47
  104.4 5.0 %collective-permute-start.28 = (bf16[256,128]{1,0:T(8,128)(2,1)S(1)}, bf16[256,128]{1,0:T(8,128)(2,1)S(1)}, u32[]{:S(2)}, u32[]{:S(2)}) collective-permute-start(bf16[256,128]{1,0:T(8,128)(2,1)S(1)} %get-tuple-element.39), channel_id=1, source_target_pairs={{0,8},{2,10},{4,12},{6,14},{8,0},{10,2},{12,4},{14,6},{16,24},{18,... | collective-permute-start | bytes 196616 | tf_op jit(solution)/shard_map/ppermute | solution.py:47
  109.4 16.1 %slice-start.1 = ((s8[4423680]{0:T(1024)(128)(4,1)}), s8[229376]{0:T(1024)(128)(4,1)S(1)}, s32[]{:S(2)}) async-start(s8[4423680]{0:T(1024)(128)(4,1)} %bitcast.394), calls=%async_computation.1 | async-start | bytes 458752
  110.3 6.2 %collective-permute-start.32 = (bf16[272,128]{1,0:T(8,128)(2,1)S(1)}, bf16[272,128]{1,0:T(8,128)(2,1)S(1)}, u32[]{:S(2)}, u32[]{:S(2)}) collective-permute-start(bf16[272,128]{1,0:T(8,128)(2,1)S(1)} %pad_maximum_fusion.28), channel_id=1, source_target_pairs={{0,24},{2,26},{4,28},{6,30},{8,16},{10,18},{12,20},{14,22},{16,8},... | collective-permute-start | bytes 208904 | tf_op jit(solution)/shard_map/ppermute | solution.py:47
  112.2 5.8 %collective-permute-start.33 = (bf16[272,128]{1,0:T(8,128)(2,1)S(1)}, bf16[272,128]{1,0:T(8,128)(2,1)S(1)}, u32[]{:S(2)}, u32[]{:S(2)}) collective-permute-start(bf16[272,128]{1,0:T(8,128)(2,1)S(1)} %pad_maximum_fusion.28), channel_id=1, source_target_pairs={{0,16},{2,18},{4,20},{6,22},{8,24},{10,26},{12,28},{14,30},{16,0},... | collective-permute-start | bytes 208904 | tf_op jit(solution)/shard_map/ppermute | solution.py:47
  112.2 5.8 %collective-permute-start.34 = (bf16[272,128]{1,0:T(8,128)(2,1)S(1)}, bf16[272,128]{1,0:T(8,128)(2,1)S(1)}, u32[]{:S(2)}, u32[]{:S(2)}) collective-permute-start(bf16[272,128]{1,0:T(8,128)(2,1)S(1)} %pad_maximum_fusion.28), channel_id=1, source_target_pairs={{0,8},{2,10},{4,12},{6,14},{8,0},{10,2},{12,4},{14,6},{16,24},{18,... | collective-permute-start | bytes 208904 | tf_op jit(solution)/shard_map/ppermute | solution.py:47
  118.1 5.2 %collective-permute-start.36 = (bf16[144,512]{1,0:T(8,128)(2,1)S(1)}, bf16[144,512]{1,0:T(8,128)(2,1)S(1)}, u32[]{:S(2)}, u32[]{:S(2)}) collective-permute-start(bf16[144,512]{1,0:T(8,128)(2,1)S(1)} %pad_maximum_fusion.13), channel_id=1, source_target_pairs={{0,4},{2,6},{4,0},{6,2},{8,12},{10,14},{12,8},{14,10},{16,20},{18,... | collective-permute-start | bytes 442376 | tf_op jit(solution)/shard_map/ppermute | solution.py:47
  123.4 1.6 %collective-permute-start.37 = (bf16[144,1024]{1,0:T(8,128)(2,1)S(1)}, bf16[144,1024]{1,0:T(8,128)(2,1)S(1)}, u32[]{:S(2)}, u32[]{:S(2)}) collective-permute-start(bf16[144,1024]{1,0:T(8,128)(2,1)S(1)} %pad_maximum_fusion.8), channel_id=1, source_target_pairs={{0,2},{2,0},{4,6},{6,4},{8,10},{10,8},{12,14},{14,12},{16,18},{18,... | collective-permute-start | bytes 884744 | tf_op jit(solution)/shard_map/ppermute | solution.py:47
  123.5 6.0 %collective-permute-start.35 = (bf16[128,512]{1,0:T(8,128)(2,1)S(1)}, bf16[128,512]{1,0:T(8,128)(2,1)S(1)}, u32[]{:S(2)}, u32[]{:S(2)}) collective-permute-start(bf16[128,512]{1,0:T(8,128)(2,1)S(1)} %pad_maximum_fusion.19), channel_id=1, source_target_pairs={{0,4},{2,6},{4,0},{6,2},{8,12},{10,14},{12,8},{14,10},{16,20},{18,... | collective-permute-start | bytes 393224 | tf_op jit(solution)/shard_map/ppermute | solution.py:47
  129.5 1.6 %collective-permute-start.38 = (bf16[128,1024]{1,0:T(8,128)(2,1)S(1)}, bf16[128,1024]{1,0:T(8,128)(2,1)S(1)}, u32[]{:S(2)}, u32[]{:S(2)}) collective-permute-start(bf16[128,1024]{1,0:T(8,128)(2,1)S(1)} %pad_maximum_fusion.10), channel_id=1, source_target_pairs={{0,2},{2,0},{4,6},{6,4},{8,10},{10,8},{12,14},{14,12},{16,18},{18,... | collective-permute-start | bytes 786440 | tf_op jit(solution)/shard_map/ppermute | solution.py:47
  129.6 6.0 %collective-permute-start.31 = (f32[2,4,2,16,128]{4,3,2,1,0:T(8,128)S(1)}, f32[2,4,2,16,128]{4,3,2,1,0:T(8,128)S(1)}, u32[]{:S(2)}, u32[]{:S(2)}) collective-permute-start(f32[2,4,2,16,128]{4,3,2,1,0:T(8,128)S(1)} %fusion.29), channel_id=1, source_target_pairs={{0,4},{2,6},{4,0},{6,2},{8,12},{10,14},{12,8},{14,10},{16,20},{18,... | collective-permute-start | bytes 393224 | tf_op jit(solution)/shard_map/ppermute | solution.py:47
  133.2 19.5 %copy-start.4 = (f32[16,4096]{1,0:T(8,128)S(1)}, f32[16,4096]{1,0:T(8,128)}, u32[]{:S(2)}) copy-start(f32[16,4096]{1,0:T(8,128)} %param.7) | copy-start | bytes 786436
  135.7 9.1 %collective-permute-start.39 = (f32[2,2,2,16,128]{4,3,2,1,0:T(8,128)S(1)}, f32[2,2,2,16,128]{4,3,2,1,0:T(8,128)S(1)}, u32[]{:S(2)}, u32[]{:S(2)}) collective-permute-start(f32[2,2,2,16,128]{4,3,2,1,0:T(8,128)S(1)} %get-tuple-element.154), channel_id=1, source_target_pairs={{0,24},{2,26},{4,28},{6,30},{8,16},{10,18},{12,20},{14,22},{16,8},... | collective-permute-start | bytes 196616 | tf_op jit(solution)/shard_map/ppermute | solution.py:47
  137.6 7.2 %collective-permute-start.40 = (f32[2,2,2,16,128]{4,3,2,1,0:T(8,128)S(1)}, f32[2,2,2,16,128]{4,3,2,1,0:T(8,128)S(1)}, u32[]{:S(2)}, u32[]{:S(2)}) collective-permute-start(f32[2,2,2,16,128]{4,3,2,1,0:T(8,128)S(1)} %get-tuple-element.153), channel_id=1, source_target_pairs={{0,16},{2,18},{4,20},{6,22},{8,24},{10,26},{12,28},{14,30},{16,0},... | collective-permute-start | bytes 196616 | tf_op jit(solution)/shard_map/ppermute | solution.py:47
  138.3 6.5 %collective-permute-start.41 = (f32[2,2,2,16,128]{4,3,2,1,0:T(8,128)S(1)}, f32[2,2,2,16,128]{4,3,2,1,0:T(8,128)S(1)}, u32[]{:S(2)}, u32[]{:S(2)}) collective-permute-start(f32[2,2,2,16,128]{4,3,2,1,0:T(8,128)S(1)} %get-tuple-element.28), channel_id=1, source_target_pairs={{0,8},{2,10},{4,12},{6,14},{8,0},{10,2},{12,4},{14,6},{16,24},{18,... | collective-permute-start | bytes 196616 | tf_op jit(solution)/shard_map/ppermute | solution.py:47
  142.7 9.5 %collective-permute-start.43 = (bf16[1080,128]{1,0:T(8,128)(2,1)S(1)}, bf16[1080,128]{1,0:T(8,128)(2,1)S(1)}, u32[]{:S(2)}, u32[]{:S(2)}) collective-permute-start(bf16[1080,128]{1,0:T(8,128)(2,1)S(1)} %get-tuple-element.228), channel_id=1, source_target_pairs={{0,1},{1,0},{2,3},{3,2},{4,5},{5,4},{6,7},{7,6},{8,9},{9,8},{10,11... | collective-permute-start | bytes 829448 | tf_op jit(solution)/shard_map/ppermute | solution.py:250
  144.3 11.7 %collective-permute-start.44 = (bf16[1080,128]{1,0:T(8,128)(2,1)S(1)}, bf16[1080,128]{1,0:T(8,128)(2,1)S(1)}, u32[]{:S(2)}, u32[]{:S(2)}) collective-permute-start(bf16[1080,128]{1,0:T(8,128)(2,1)S(1)} %get-tuple-element.226), channel_id=1, source_target_pairs={{0,1},{1,0},{2,3},{3,2},{4,5},{5,4},{6,7},{7,6},{8,9},{9,8},{10,11... | collective-permute-start | bytes 829448 | tf_op jit(solution)/shard_map/ppermute | solution.py:250
  144.9 7.4 %collective-permute-start.42 = (f32[4,2,2,16,128]{4,3,2,1,0:T(8,128)S(1)}, f32[4,2,2,16,128]{4,3,2,1,0:T(8,128)S(1)}, u32[]{:S(2)}, u32[]{:S(2)}) collective-permute-start(f32[4,2,2,16,128]{4,3,2,1,0:T(8,128)S(1)} %fusion.28), channel_id=1, source_target_pairs={{0,2},{2,0},{4,6},{6,4},{8,10},{10,8},{12,14},{14,12},{16,18},{18,... | collective-permute-start | bytes 393224 | tf_op jit(solution)/shard_map/ppermute | solution.py:47

commit v2 on v1

--- a/solution.py
+++ b/solution.py
@@ -95,28 +95,18 @@
     return lax.optimization_barrier((value, *others))[0]
 
 
-def scatter_stage(value, stage, gate=()):
-    parts = split_cols(value, stage.radix)
+def send_parts(stage, parts):
     own = pick(parts, stage.digit)
-    received = [
-        stage.send(pick(parts, stage.partner(stage.digit, step)), step) for step in range(1, stage.radix)
-    ]
-    received = [after(value, *gate) for value in received]
-    return jnp.concatenate(ordered(stage, own, received), axis=-2)
-
-
-def home_stage(value, stage, axis, gate=()):
-    parts = [lax.index_in_dim(value, i, axis, keepdims=False) for i in range(stage.radix)]
-    own = pick(parts, stage.digit)
-    received = [
-        stage.send(pick(parts, stage.partner(stage.digit, step)), step) for step in range(1, stage.radix)
-    ]
-    received = [after(value, *gate) for value in received]
-    return jnp.stack(ordered(stage, own, received))
-
-
-def gather_stage(value, stage):
-    received = [stage.send(value, step) for step in range(1, stage.radix)]
+    sent = [pick(parts, stage.partner(stage.digit, step)) for step in range(1, stage.radix)]
+    return own, [stage.send(sent[step - 1], step) for step in range(1, stage.radix)]
+
+
+def in_order(stage, own, received, gate=()):
+    return ordered(stage, own, [after(value, *gate) for value in received])
+
+
+def gather_stage(value, stage, gate=()):
+    received = [after(stage.send(value, step), *gate) for step in range(1, stage.radix)]
     return jnp.concatenate(ordered(stage, value, received), axis=-1)
 
 
@@ -138,66 +128,117 @@
     return jnp.sum(rows.astype(F32).reshape(3, size // fit, width)[:, :, :fit], axis=0).reshape(size)
 
 
-def merge_stage(stage, partial, resid_sum, stats, samples, known=None, gate=()):
+def merge_stage(stage, partial, resid_sum, riders, stats, samples):
     size, width = partial.shape[0], partial.shape[1] // stage.radix
-    n_stats = stats.shape[0]
     parts = split_cols(partial, stage.radix)
-    stat_parts = split_cols(stats, stage.radix)
     sums = sum_rows(resid_sum, width)
     n_sum = sums.shape[0]
-    partials = [pick(parts, stage.digit)]
-    resid_sums = [resid_sum]
-    members = [pick(stat_parts, stage.digit)] if known is None else known
-    sent = []
+    stat_parts = None if stats is None else split_cols(stats, stage.radix)
+    rider_parts = None if riders is None else split_cols(riders, stage.radix)
+    sent, arrived = [], []
     for step in range(1, stage.radix):
         to = stage.partner(stage.digit, step)
         extra = sums
-        if known is None:
+        if stats is not None:
             extra = jnp.concatenate([sums] + split_bf16(pick(stat_parts, to), 2), axis=0)
-        message = jnp.concatenate([pick(parts, to).astype(BF16), pad_rows(extra)], axis=0)
-        sent.append(message)
-        message = after(stage.send(message, step), *gate)
-        partials.append(message[:size].astype(F32))
-        tail = message[size:]
-        resid_sums.append(read_sums(tail[:n_sum], width, size))
-        if known is None:
-            terms = tail[n_sum : n_sum + 2 * n_stats].astype(F32)
-            members.append(terms[:n_stats] + terms[n_stats:])
-    count_mean = sum(m[0] for m in members) / stage.radix
-    sum_mean = sum(resid_sums) / stage.radix
-    total = sum(partials)
-    for s, m in zip(resid_sums, members):
-        total = total + (s - sum_mean)[:, None] * ((m[0] - count_mean) / samples)[None, :]
-    return total, sum(resid_sums), members, sent
+        message = [pick(parts, to).astype(BF16), pad_rows(extra)]
+        n_extra = message[1].shape[0]
+        if riders is not None:
+            message.append(pick(rider_parts, to))
+        sent.append(jnp.concatenate(message, axis=0))
+        arrived.append(stage.send(sent[-1], step))
+
+    def finish(gate=(), members=None):
+        partials, resid_sums, ridden = [pick(parts, stage.digit)], [resid_sum], []
+        if stats is not None:
+            n_stats = stats.shape[0]
+            members = [pick(stat_parts, stage.digit)]
+        for message in arrived:
+            message = after(message, *gate)
+            partials.append(message[:size].astype(F32))
+            tail = message[size:]
+            ridden.append(tail[n_extra:])
+            resid_sums.append(read_sums(tail[:n_sum], width, size))
+            if stats is not None:
+                terms = tail[n_sum : n_sum + 2 * n_stats].astype(F32)
+                members.append(terms[:n_stats] + terms[n_stats:])
+        count_mean = sum(m[0] for m in members) / stage.radix
+        sum_mean = sum(resid_sums) / stage.radix
+        total = sum(partials)
+        for s, m in zip(resid_sums, members):
+            total = total + (s - sum_mean)[:, None] * ((m[0] - count_mean) / samples)[None, :]
+        merged = None
+        if riders is not None:
+            merged = jnp.concatenate(ordered(stage, pick(rider_parts, stage.digit), ridden), axis=0)
+        return (total, sum(resid_sums), merged), members
+
+    return sent, finish
 
 
 def sum_stage(stage, partial):
     parts = split_cols(partial, stage.radix)
-    total = pick(parts, stage.digit)
-    sent = []
-    for step in range(1, stage.radix):
-        sent.append(pick(parts, stage.partner(stage.digit, step)).astype(BF16))
-        total = total + stage.send(sent[-1], step).astype(F32)
-    return total, sent
+    own = pick(parts, stage.digit)
+    sent = [
+        pick(parts, stage.partner(stage.digit, step)).astype(BF16) for step in range(1, stage.radix)
+    ]
+    arrived = [stage.send(sent[step - 1], step) for step in range(1, stage.radix)]
+
+    def finish(gate=()):
+        return sum((after(value, *gate).astype(F32) for value in arrived), start=own)
+
+    return sent, finish
 
 
 TILES = 4
-
-
-def head_kernel(columns, genotypes, residual, partial, stats, resid_sum, blocks, sems):
+GROUP = 64
+
+
+def column_moments(values):
+    rows, width = values.shape
+    whole = rows // 16 * 16
+    counts = jnp.zeros((1, width), F32)
+    twos = jnp.zeros((1, width), F32)
+    one, zero = jnp.bfloat16(1), jnp.bfloat16(0)
+    for begin in range(0, whole, 16 * GROUP):
+        count_sum = two_sum = None
+        for at in range(begin, min(begin + 16 * GROUP, whole), 16):
+            part = values[at : at + 16]
+            above = jnp.maximum(part - one, zero)
+            count_sum = part if count_sum is None else count_sum + part
+            two_sum = above if two_sum is None else two_sum + above
+        counts = counts + jnp.sum(count_sum.astype(F32), axis=0, keepdims=True)
+        twos = twos + jnp.sum(two_sum.astype(F32), axis=0, keepdims=True)
+    if whole < rows:
+        part = values[whole:].astype(F32)
+        counts = counts + jnp.sum(part, axis=0, keepdims=True)
+        twos = twos + jnp.sum(jnp.maximum(part - 1.0, 0.0), axis=0, keepdims=True)
+    return counts, twos
+
+
+def head_kernel(
+    colors, genotypes, residual, coefficients, partial, stats, resid_sum, olds, blocks, resid, sems, resid_sem, old_sems
+):
     samples, phenotypes = residual.shape
     width = BS // TILES
 
     def copy(r, t):
-        at = pl.multiple_of(columns[r] * BS + t * width, width)
+        at = pl.multiple_of(colors[r, 0] * BS + t * width, width)
         return pltpu.make_async_copy(
             genotypes.at[:, pl.ds(at, width)], blocks.at[r, :, pl.ds(t * width, width)], sems.at[r, t]
         )
 
+    def old_copy(r):
+        at = pl.multiple_of(colors[r, 0] * BS, BS)
+        return pltpu.make_async_copy(coefficients.at[:, pl.ds(at, BS)], olds.at[r], old_sems.at[r])
+
+    resid_copy = pltpu.make_async_copy(residual, resid, resid_sem)
+    resid_copy.start()
     for r in range(ROUNDS):
         for t in range(TILES):
             copy(r, t).start()
-    rounded = residual[...].astype(BF16)
+        old_copy(r).start()
+    resid_copy.wait()
+    rounded = resid[...].astype(BF16)
     sums = jnp.sum(rounded.astype(F32), axis=0, keepdims=True)
     resid_sum[...] = sums
     column = jnp.broadcast_to(jnp.transpose(jnp.broadcast_to(sums, (8, phenotypes)))[:, :1], (phenotypes, width))
@@ -206,37 +247,45 @@
             copy(r, t).wait()
             here = pl.ds(t * width, width)
             values = blocks[r, :, here]
-            wide = values.astype(F32)
-            counts = jnp.sum(wide, axis=0, keepdims=True)
-            squares = jnp.sum(wide * wide, axis=0, keepdims=True)
+            counts, twos = column_moments(values)
             stats[2 * r : 2 * r + 1, here] = counts
-            stats[2 * r + 1 : 2 * r + 2, here] = 0.5 * (squares - counts)
+            stats[2 * r + 1 : 2 * r + 2, here] = twos
             if r == 0:
                 product = lax.dot_general(
                     rounded, values, (((0,), (0,)), ((), ())), preferred_element_type=F32
                 )
                 partial[:, here] = product - column * (counts * (1.0 / samples))
-
-
-def head(columns, genotypes, residual):
+        old_copy(r).wait()
+
+
+def head(colors, genotypes, residual, coefficients):
     samples, phenotypes = residual.shape
+    rows_own = coefficients.shape[0]
     whole = pl.BlockSpec(memory_space=pltpu.VMEM)
+    far = pl.BlockSpec(memory_space=pltpu.HBM)
     return pl.pallas_call(
         head_kernel,
         out_shape=[
             jax.ShapeDtypeStruct((phenotypes, BS), F32),
             jax.ShapeDtypeStruct((2 * ROUNDS, BS), F32),
             jax.ShapeDtypeStruct((1, phenotypes), F32),
+            jax.ShapeDtypeStruct((ROUNDS, rows_own, BS), F32),
         ],
-        in_specs=[pl.BlockSpec(memory_space=pltpu.SMEM), pl.BlockSpec(memory_space=pltpu.HBM), whole],
-        out_specs=[whole] * 3,
-        scratch_shapes=[pltpu.VMEM((ROUNDS, samples, BS), BF16), pltpu.SemaphoreType.DMA((ROUNDS, TILES))],
+        in_specs=[pl.BlockSpec(memory_space=pltpu.SMEM), far, far, far],
+        out_specs=[whole] * 4,
+        scratch_shapes=[
+            pltpu.VMEM((ROUNDS, samples, BS), BF16),
+            pltpu.VMEM((samples, phenotypes), F32),
+            pltpu.SemaphoreType.DMA((ROUNDS, TILES)),
+            pltpu.SemaphoreType.DMA,
+            pltpu.SemaphoreType.DMA((ROUNDS,)),
+        ],
         cost_estimate=pl.CostEstimate(
             flops=4 * samples * phenotypes * BS, bytes_accessed=4 * samples * BS, transcendentals=0
         ),
         compiler_params=pltpu.CompilerParams(vmem_limit_bytes=50 * 1024 * 1024),
         name="head",
-    )(columns, genotypes, residual)
+    )(colors, genotypes, residual, coefficients)
 
 
 def over_var(value):
@@ -271,39 +320,56 @@
     size = phenotypes // chunks
     chosen = colors[:, 0]
 
-    olds = [lax.dynamic_slice_in_dim(coefficients, chosen[r] * BS, BS, 1) for r in range(ROUNDS)]
-    old_columns = jnp.stack(olds)
-    partial, stats, resid_sum = head(chosen, genotypes, residual)
-    values = []
+    partial, stats, resid_sum, olds = head(colors, genotypes, residual, coefficients)
     partial_chunks = [partial[c * size : (c + 1) * size] for c in range(chunks)]
     sum_chunks = [resid_sum[0, c * size : (c + 1) * size] for c in range(chunks)]
+    values = []
 
     first = jnp.int32(0)
     for stage in all_stages:
         first = first * stage.radix + stage.digit
     first = first * width
 
+    def weights(r, gate):
+        part = lax.dynamic_slice_in_dim(after(penalty, gate), chosen[r] * BS + first, width, 0)
+        return lax.optimization_barrier(part)
+
+    riders = [None] * (chunks - 1) + [jnp.concatenate(split_bf16(olds[0], 2), axis=0)]
+    states = list(zip(partial_chunks, sum_chunks, riders))
+    moments, samples = stats, local_samples
+    sent_top, end_top, ends, members, gate = [], [], [], [None] * len(all_stages), ()
+    for c in range(chunks):
+        samples = local_samples
+        for i in range(top + 1):
+            sent, finish = merge_stage(early[i], *states[c], None if c else moments, samples)
+            if i < top:
+                states[c], members[i] = finish(gate, members[i])
+                moments, samples = sum(members[i]), samples * early[i].radix
+        sent_top.append(sent)
+        end_top.append(finish)
+        gate = sent
+    gate = sent_top[-1]
+    for c in range(chunks):
+        states[c], members[top] = end_top[c](gate, members[top])
+        if not c:
+            moments, samples = sum(members[top]), samples * early[top].radix
+        sent, finish = merge_stage(last, *states[c], None if c else moments, samples)
+        ends.append(finish)
+        gate = sent
+    partial_chunks, members = [], None
+    for finish in ends:
+        (partial, _, riders), members = finish(gate, members)
+        partial_chunks.append(partial)
+    gradient = jnp.concatenate(partial_chunks, axis=0)
+    moments = sum(members)
+    old = jnp.sum(riders.astype(F32).reshape(samp, 2, rows_own, width), axis=1).reshape(phenotypes, width)
+    ahead = sent_top[-1]
+    weight = weights(0, ahead[0])
+    values = [None] + [chosen_block(genotypes, chosen[r], ahead[0]) for r in range(1, ROUNDS)]
+    old_later = jnp.stack([after(olds[r], *ahead) for r in range(1, ROUNDS)])
     for i in range(top):
-        old_columns = scatter_stage(old_columns, early[i])
-    learned, moments, samples = [], stats, local_samples
-    ahead = ()
-    for c in range(chunks):
-        gate = ahead
-        here, moments, samples = (partial_chunks[c], sum_chunks[c]), stats, local_samples
-        for i, stage in enumerate(early):
-            *here, members, ahead = merge_stage(
-                stage, *here, moments, samples, learned[i] if c else None, () if i else gate
-            )
-            if not c:
-                learned.append(members)
-            moments, samples = sum(learned[i]), samples * stage.radix
-        partial_chunks[c], sum_chunks[c] = here
-    old_columns = scatter_stage(old_columns, early[top], ahead)
-    old = scatter_stage(old_columns[0], last)
-    gradient, _, members, _ = merge_stage(
-        last, jnp.concatenate(partial_chunks, axis=0), jnp.concatenate(sum_chunks), moments, samples
-    )
-    moments = sum(members)
+        parts = send_parts(early[i], split_cols(old_later, early[i].radix))
+        old_later = jnp.concatenate(in_order(early[i], *parts, sent), axis=-2)
 
     residuals = [residual[:, c * size : (c + 1) * size] for c in range(chunks)]
     news = []
@@ -312,24 +378,33 @@
         mean = counts / total_samples
         scale = (counts + 2.0 * twos) - counts * mean
         if r:
-            ahead = ()
+            sent_top, end_top, ends = [], [], []
             for c in range(chunks):
                 own, other = pending[c]
                 if c:
-                    other = after(other, *ahead)
+                    other = after(other, *sent_top[-1])
                 residuals[c] = residuals[c] - (own + other)
                 rounded = residuals[c].astype(BF16)
                 resid_sum = jnp.sum(rounded.astype(F32), axis=0)
                 partial = lax.dot_general(rounded, values[r], (((0,), (0,)), ((), ())), preferred_element_type=F32)
                 partial = partial - resid_sum[:, None] * means[r][None, :]
-                for stage in early:
-                    partial, ahead = sum_stage(stage, partial)
-                partial_chunks[c] = partial
-            old = scatter_stage(after(old_columns[r], *ahead), last)
-            gradient, _ = sum_stage(last, jnp.concatenate(partial_chunks, axis=0))
+                for i in range(top + 1):
+                    sent, finish = sum_stage(early[i], partial)
+                    if i < top:
+                        partial = finish()
+                sent_top.append(sent)
+                end_top.append(finish)
+            gate = ahead = sent_top[-1]
+            weight = weights(r, ahead[0])
+            for c in range(chunks):
+                partial = end_top[c](gate)
+                gate, finish = sum_stage(last, partial)
+                ends.append(finish)
+            partial_chunks = [finish(gate) for finish in ends]
+            old = jnp.concatenate(in_order(last, *old_parts, ahead), axis=-2)[r - 1]
+            gradient = jnp.concatenate(partial_chunks, axis=0)
             for before in range(r):
                 old = jnp.where(chosen[before] == chosen[r], news[before], old)
-        weight = lax.dynamic_slice_in_dim(penalty, chosen[r] * BS + first, width, 0)
         shifted = old + gradient / scale[None, :]
         norm = jnp.sqrt(jnp.sum(shifted * shifted, axis=0) + 1e-06)
         shrink = jnp.maximum(0.0, 1.0 - weight * jnp.sqrt(phenotypes / scale) / norm)
@@ -342,7 +417,8 @@
         lead = rows.shape[0]
         message = jnp.concatenate([rows, change], axis=0)
         if r == 0:
-            values.append(chosen_block(genotypes, chosen[0], message))
+            values[0] = chosen_block(genotypes, chosen[0], message)
+            old_parts = send_parts(early[top], split_cols(old_later, early[top].radix))
         gathered = gather_stage(message, last)
         cuts = [0] + [lead + size * (c + 1) for c in range(chunks)]
         pieces = [gathered[cuts[c] : cuts[c + 1]] for c in range(chunks)]
@@ -369,23 +445,24 @@
             )
             product = product - shift[None, :]
             pending.append(over_var(product))
-        if r + 1 < ROUNDS:
-            values.append(chosen_block(genotypes, chosen[r + 1], product))
+        if r == 0:
+            old_later = jnp.concatenate(in_order(early[top], *old_parts, [product]), axis=-2)
+            old_parts = send_parts(last, split_cols(old_later, last.radix))
 
     for c in range(chunks):
         own, other = pending[c]
         residuals[c] = residuals[c] - (own + other)
 
-    home = jnp.stack(news).reshape(
-        [ROUNDS] + [stage.radix for stage in reversed(all_stages)] + [rows_own, width]
-    )
-    axes = list(reversed(range(len(all_stages))))
-    found = []
-    for i in [top, top + 1] + list(reversed(range(top))):
-        axis = len(found) + 1 + axes.index(i)
-        home = home_stage(home, all_stages[i], axis, [product] if i == top else ())
-        axes.remove(i)
-        found.insert(0, i)
+    home = [new.reshape([stage.radix for stage in reversed(all_stages)] + [rows_own, width]) for new in news]
+    home = jnp.stack(home, axis=len(all_stages))
+    steps = [(top, 1, []), (top + 1, 1, [])] + [
+        (i, len(all_stages) - 1 - i, []) for i in reversed(range(top))
+    ]
+    for i, axis, gate in steps:
+        stage = all_stages[i]
+        parts = [lax.index_in_dim(home, d, axis, keepdims=False) for d in range(stage.radix)]
+        home = jnp.stack(in_order(stage, *send_parts(stage, parts), gate))
+    found = list(range(top)) + [top + 1, top]
     home = jnp.transpose(home, [found.index(i) for i in range(len(found))] + [len(found) + j for j in range(3)])
     home = home.reshape(samp, ROUNDS, rows_own, width)
     new_rows = [jnp.concatenate([home[s, r] for s in range(samp)], axis=-1) for r in range(ROUNDS)]

time: 158 us -> 156 us (0.987)
  waiting for transfers between devices: 67.9 us -> 53 us
  starting transfers between devices: 47.3 us -> 55.2 us
  local copies, waits for them, and re-layouts: 9.67 us -> 13.8 us
    ppermute x41 -> x44, waiting for transfers between devices: 46.6 us -> 28.7 us  [send(): return lax.ppermute(value, 'samp', self.pairs(step))]
    ppermute x41 -> x44, starting transfers between devices: 42 us -> 50 us  [send(): return lax.ppermute(value, 'samp', self.pairs(step))]
    ppermute x4, waiting for transfers between devices: 21.3 us -> 24.3 us  [over_var(): lax.ppermute(value.astype(BF16), 'var', [(i, i ^ step) for i in range(siz...]
    dynamic_slice x2, local copies, waits for them, and re-layouts: 3.62 us -> 5.64 us  [chosen_block(): lax.dynamic_slice_in_dim(genotypes, block * BS, BS, 1)]
  transfers between devices with their start and end apart: 45 -> 48, of which waited for: 28 -> 21; matrix products, arithmetic and copies ran while one was open for 12% -> 16% of each run, Pallas kernels for 3% -> 0%
where the time goes in v2:
time: 156 us; the launch traced here: 155 us
  starting transfers between devices  55.2 us (35%)
  waiting for transfers between devices  53 us (34%)
  local copies, waits for them, and re-layouts  13.8 us (9%)
  other arithmetic  11 us (7%)
  matrix products  9.14 us (6%)
  between operations  7.41 us (5%)
  Pallas kernels  5.52 us (4%)
    ppermute x44, starting transfers between devices, send(): return lax.ppermute(value, 'samp', self.pairs(step))  50 us
    ppermute x44, waiting for transfers between devices, send(): return lax.ppermute(value, 'samp', self.pairs(step))  28.7 us
    ppermute x4, waiting for transfers between devices, over_var(): lax.ppermute(value.astype(BF16), 'var', [(i, i ^ step) for i in range(siz...  24.3 us
    dot_general x4, matrix products, descent(): lax.dot_general(values[r], piece, (((1,), (1,)), ((), ())), preferred_ele...  5.74 us
    dynamic_slice x2, local copies, waits for them, and re-layouts, chosen_block(): lax.dynamic_slice_in_dim(genotypes, block * BS, BS, 1)  5.64 us
    pallas_call x1, Pallas kernels, head(): pl.pallas_call(head_kernel, out_shape=[jax.ShapeDtypeStruct((phenotypes,...  5.52 us
    ppermute x4, starting transfers between devices, over_var(): lax.ppermute(value.astype(BF16), 'var', [(i, i ^ step) for i in range(siz...  5.24 us
  transfers between devices with their start and end apart: 48, of which 21 were waited for; matrix products, arithmetic and copies ran while one was open for 16% of the time, Pallas kernels for 0%

profile of v2, /device:TPU:0, one launch (start us, length us, event | category | flops | bytes accessed | tf_op | source)
XLA Modules:
  0.0 155.1 jit_solution(3566989264675241968)
XLA Ops:
  1.4 1.2 copy-done
  2.6 0.9 copy-done.2
  3.6 5.5 %head.1 = (f32[256,2048]{1,0:T(8,128)S(1)}, f32[4,2048]{1,0:T(4,128)S(1)}, f32[1,256]{1,0:T(1,128)S(1)}, f32[2,16,2048]{2,1,0:T(8,128)S(1)}) custom-call(s32[2,1]{1,0:T(2,128)S(1)} %copy.7.colors, bf16[1080,4096]{1,0:T(8,128)(2,1)} %genotypes.1, f32[1080,256]{1,0:T(8,128)S(1)} %copy-done, f32[16,4096]{1,0:T(8,128)S(1)} %copy-done.2), custom_call_target="tpu_custom_call" | custom-call | flops 2264924160 | bytes 8847360 | tf_op jit(solution)/shard_map/head/pallas_call | solution.py:266
  17.3 0.8 slice_convert_fusion
  18.1 0.8 fusion.8
  19.1 1.1 multiply_add_fusion.1
  20.5 2.9 %collective-permute-start.2 = (bf16[144,512]{1,0:T(8,128)(2,1)S(1)}, bf16[144,512]{1,0:T(8,128)(2,1)S(1)}, u32[]{:S(2)}, u32[]{:S(2)}) collective-permute-start(bf16[144,512]{1,0:T(8,128)(2,1)S(1)} %fusion.13), channel_id=1, source_target_pairs={{0,4},{2,6},{4,0},{6,2},{8,12},{10,14},{12,8},{14,10},{16,20},{18,... | collective-permute-start | bytes 442376 | tf_op jit(solution)/shard_map/ppermute | solution.py:47
  24.2 1.1 multiply_add_fusion
  25.3 0.9 broadcast_select_fusion.20
  26.3 1.2 collective-permute-done.2
  27.8 1.8 %collective-permute-start.4 = (bf16[208,512]{1,0:T(8,128)(2,1)S(1)}, bf16[208,512]{1,0:T(8,128)(2,1)S(1)}, u32[]{:S(2)}, u32[]{:S(2)}) collective-permute-start(bf16[208,512]{1,0:T(8,128)(2,1)S(1)} %fusion.12), channel_id=1, source_target_pairs={{0,4},{2,6},{4,0},{6,2},{8,12},{10,14},{12,8},{14,10},{16,20},{18,... | collective-permute-start | bytes 638984 | tf_op jit(solution)/shard_map/ppermute | solution.py:47
  29.8 3.7 %collective-permute-start.6 = (bf16[144,128]{1,0:T(8,128)(2,1)S(1)}, bf16[144,128]{1,0:T(8,128)(2,1)S(1)}, u32[]{:S(2)}, u32[]{:S(2)}) collective-permute-start(bf16[144,128]{1,0:T(8,128)(2,1)S(1)} %fusion.63), channel_id=1, source_target_pairs={{0,24},{2,26},{4,28},{6,30},{8,16},{10,18},{12,20},{14,22},{16,8},... | collective-permute-start | bytes 110600 | tf_op jit(solution)/shard_map/ppermute | solution.py:47
  34.0 0.8 collective-permute-start.3
  34.8 0.8 dynamic_slice.12
  36.0 2.2 %collective-permute-start.8 = (bf16[272,128]{1,0:T(8,128)(2,1)S(1)}, bf16[272,128]{1,0:T(8,128)(2,1)S(1)}, u32[]{:S(2)}, u32[]{:S(2)}) collective-permute-start(bf16[272,128]{1,0:T(8,128)(2,1)S(1)} %get-tuple-element.239), channel_id=1, source_target_pairs={{0,16},{2,18},{4,20},{6,22},{8,24},{10,26},{12,28},{14,30},{16,0},... | collective-permute-start | bytes 208904 | tf_op jit(solution)/shard_map/ppermute | solution.py:47
  38.2 1.5 collective-permute-start.7
  40.6 2.5 %collective-permute-done.8 = bf16[272,128]{1,0:T(8,128)(2,1)S(1)} collective-permute-done((bf16[272,128]{1,0:T(8,128)(2,1)S(1)}, bf16[272,128]{1,0:T(8,128)(2,1)S(1)}, u32[]{:S(2)}, u32[]{:S(2)}) %collective-permute-start.8) | collective-permute-done | bytes 69664 | tf_op jit(solution)/shard_map/ppermute | solution.py:47
  43.1 1.3 collective-permute-done.7
  45.2 2.3 %collective-permute-start.10 = (bf16[272,128]{1,0:T(8,128)(2,1)S(1)}, bf16[272,128]{1,0:T(8,128)(2,1)S(1)}, u32[]{:S(2)}, u32[]{:S(2)}) collective-permute-start(bf16[272,128]{1,0:T(8,128)(2,1)S(1)} %fusion.33), channel_id=1, source_target_pairs={{0,24},{2,26},{4,28},{6,30},{8,16},{10,18},{12,20},{14,22},{16,8},... | collective-permute-start | bytes 208904 | tf_op jit(solution)/shard_map/ppermute | solution.py:47
  47.5 2.2 %collective-permute-start.12 = (bf16[272,128]{1,0:T(8,128)(2,1)S(1)}, bf16[272,128]{1,0:T(8,128)(2,1)S(1)}, u32[]{:S(2)}, u32[]{:S(2)}) collective-permute-start(bf16[272,128]{1,0:T(8,128)(2,1)S(1)} %fusion.33), channel_id=1, source_target_pairs={{0,8},{2,10},{4,12},{6,14},{8,0},{10,2},{12,4},{14,6},{16,24},{18,... | collective-permute-start | bytes 208904 | tf_op jit(solution)/shard_map/ppermute | solution.py:47
  49.8 1.6 %collective-permute-done.10 = bf16[272,128]{1,0:T(8,128)(2,1)S(1)} collective-permute-done((bf16[272,128]{1,0:T(8,128)(2,1)S(1)}, bf16[272,128]{1,0:T(8,128)(2,1)S(1)}, u32[]{:S(2)}, u32[]{:S(2)}) %collective-permute-start.10) | collective-permute-done | bytes 69664 | tf_op jit(solution)/shard_map/ppermute | solution.py:47
  51.4 1.5 collective-permute-done.11
  53.1 0.8 collective-permute-start.14
  53.9 2.8 %constant_dynamic-slice_fusion = bf16[1080,2048]{1,0:T(8,128)(2,1)S(1)} fusion(bf16[1080,4096]{1,0:T(8,128)(2,1)} %genotypes.1, s32[]{:T(128)S(6)} %select_n.1411), kind=kLoop, calls=%fused_computation.509 | loop fusion | bytes 8847364 | tf_op jit(solution)/shard_map/dynamic_slice | solution.py:307
  56.7 1.6 %collective-permute-done.14 = bf16[144,512]{1,0:T(8,128)(2,1)S(1)} collective-permute-done((bf16[144,512]{1,0:T(8,128)(2,1)S(1)}, bf16[144,512]{1,0:T(8,128)(2,1)S(1)}, u32[]{:S(2)}, u32[]{:S(2)}) %collective-permute-start.14) | collective-permute-done | bytes 147488 | tf_op jit(solution)/shard_map/ppermute | solution.py:47
  58.4 2.8 %constant_dynamic-slice_fusion.1 = bf16[1080,2048]{1,0:T(8,128)(2,1)S(1)} fusion(bf16[1080,4096]{1,0:T(8,128)(2,1)} %genotypes.1, s32[]{:T(128)S(6)} %select_n.1372), kind=kLoop, calls=%fused_computation.510 | loop fusion | bytes 8847364 | tf_op jit(solution)/shard_map/dynamic_slice | solution.py:307
  61.3 0.8 collective-permute-start.13
  62.5 1.4 fusion.152
  63.9 3.3 %collective-permute-done.13 = bf16[128,512]{1,0:T(8,128)(2,1)S(1)} collective-permute-done((bf16[128,512]{1,0:T(8,128)(2,1)S(1)}, bf16[128,512]{1,0:T(8,128)(2,1)S(1)}, u32[]{:S(2)}, u32[]{:S(2)}) %collective-permute-start.13) | collective-permute-done | bytes 131104 | tf_op jit(solution)/shard_map/ppermute | solution.py:47
  67.4 1.6 %collective-permute-start.18 = (bf16[1080,128]{1,0:T(8,128)(2,1)S(1)}, bf16[1080,128]{1,0:T(8,128)(2,1)S(1)}, u32[]{:S(2)}, u32[]{:S(2)}) collective-permute-start(bf16[1080,128]{1,0:T(8,128)(2,1)S(1)} %get-tuple-element.282), channel_id=1, source_target_pairs={{0,1},{1,0},{2,3},{3,2},{4,5},{5,4},{6,7},{7,6},{8,9},{9,8},{10,11... | collective-permute-start | bytes 829448 | tf_op jit(solution)/shard_map/ppermute | solution.py:299
  69.0 0.8 collective-permute-start.22
  70.2 6.3 %collective-permute-done.18 = bf16[1080,128]{1,0:T(8,128)(2,1)S(1)} collective-permute-done((bf16[1080,128]{1,0:T(8,128)(2,1)S(1)}, bf16[1080,128]{1,0:T(8,128)(2,1)S(1)}, u32[]{:S(2)}, u32[]{:S(2)}) %collective-permute-start.18) | collective-permute-done | bytes 276512 | tf_op jit(solution)/shard_map/ppermute | solution.py:299
  76.7 1.2 convolution_subtract_fusion.5
  78.0 1.4 fusion.151
  79.5 1.6 %collective-permute-start.17 = (bf16[1080,128]{1,0:T(8,128)(2,1)S(1)}, bf16[1080,128]{1,0:T(8,128)(2,1)S(1)}, u32[]{:S(2)}, u32[]{:S(2)}) collective-permute-start(bf16[1080,128]{1,0:T(8,128)(2,1)S(1)} %get-tuple-element.280), channel_id=1, source_target_pairs={{0,1},{1,0},{2,3},{3,2},{4,5},{5,4},{6,7},{7,6},{8,9},{9,8},{10,11... | collective-permute-start | bytes 829448 | tf_op jit(solution)/shard_map/ppermute | solution.py:299
  81.2 7.4 %collective-permute-done.17 = bf16[1080,128]{1,0:T(8,128)(2,1)S(1)} collective-permute-done((bf16[1080,128]{1,0:T(8,128)(2,1)S(1)}, bf16[1080,128]{1,0:T(8,128)(2,1)S(1)}, u32[]{:S(2)}, u32[]{:S(2)}) %collective-permute-start.17) | collective-permute-done | bytes 276512 | tf_op jit(solution)/shard_map/ppermute | solution.py:299
  88.8 1.2 convolution_subtract_fusion.4
  90.1 1.2 collective-permute-start.25
  91.3 1.7 %collective-permute-start.24 = (f32[1,64,128]{2,1,0:T(8,128)S(1)}, f32[1,64,128]{2,1,0:T(8,128)S(1)}, u32[]{:S(2)}, u32[]{:S(2)}) collective-permute-start(f32[1,64,128]{2,1,0:T(8,128)S(1)} %get-tuple-element.224), channel_id=1, source_target_pairs={{0,16},{2,18},{4,20},{6,22},{8,24},{10,26},{12,28},{14,30},{16,0},... | collective-permute-start | bytes 98312 | tf_op jit(solution)/shard_map/ppermute | solution.py:47
  93.1 1.6 %collective-permute-start.23 = (f32[1,64,128]{2,1,0:T(8,128)S(1)}, f32[1,64,128]{2,1,0:T(8,128)S(1)}, u32[]{:S(2)}, u32[]{:S(2)}) collective-permute-start(f32[1,64,128]{2,1,0:T(8,128)S(1)} %get-tuple-element.225), channel_id=1, source_target_pairs={{0,24},{2,26},{4,28},{6,30},{8,16},{10,18},{12,20},{14,22},{16,8},... | collective-permute-start | bytes 98312 | tf_op jit(solution)/shard_map/ppermute | solution.py:47
  95.5 1.4 collective-permute-start.28
  96.9 1.8 %collective-permute-done.23 = f32[1,64,128]{2,1,0:T(8,128)S(1)} collective-permute-done((f32[1,64,128]{2,1,0:T(8,128)S(1)}, f32[1,64,128]{2,1,0:T(8,128)S(1)}, u32[]{:S(2)}, u32[]{:S(2)}) %collective-permute-start.23) | collective-permute-done | bytes 32800 | tf_op jit(solution)/shard_map/ppermute | solution.py:47
  98.8 2.2 %collective-permute-done.26 = bf16[128,512]{1,0:T(8,128)(2,1)S(1)} collective-permute-done((bf16[128,512]{1,0:T(8,128)(2,1)S(1)}, bf16[128,512]{1,0:T(8,128)(2,1)S(1)}, u32[]{:S(2)}, u32[]{:S(2)}) %collective-permute-start.26) | collective-permute-done | bytes 131104 | tf_op jit(solution)/shard_map/ppermute | solution.py:47
  101.4 2.6 %collective-permute-start.29 = (bf16[128,128]{1,0:T(8,128)(2,1)S(1)}, bf16[128,128]{1,0:T(8,128)(2,1)S(1)}, u32[]{:S(2)}, u32[]{:S(2)}) collective-permute-start(bf16[128,128]{1,0:T(8,128)(2,1)S(1)} %select_convert_fusion.12), channel_id=1, source_target_pairs={{0,16},{2,18},{4,20},{6,22},{8,24},{10,26},{12,28},{14,30},{16,0},... | collective-permute-start | bytes 98312 | tf_op jit(solution)/shard_map/ppermute | solution.py:47
  104.0 1.6 %collective-permute-start.30 = (bf16[128,128]{1,0:T(8,128)(2,1)S(1)}, bf16[128,128]{1,0:T(8,128)(2,1)S(1)}, u32[]{:S(2)}, u32[]{:S(2)}) collective-permute-start(bf16[128,128]{1,0:T(8,128)(2,1)S(1)} %get-tuple-element.201), channel_id=1, source_target_pairs={{0,24},{2,26},{4,28},{6,30},{8,16},{10,18},{12,20},{14,22},{16,8},... | collective-permute-start | bytes 98312 | tf_op jit(solution)/shard_map/ppermute | solution.py:47
  105.6 0.8 dynamic_slice.15
  106.6 2.8 %collective-permute-start.32 = (bf16[128,128]{1,0:T(8,128)(2,1)S(1)}, bf16[128,128]{1,0:T(8,128)(2,1)S(1)}, u32[]{:S(2)}, u32[]{:S(2)}) collective-permute-start(bf16[128,128]{1,0:T(8,128)(2,1)S(1)} %get-tuple-element.199), channel_id=1, source_target_pairs={{0,16},{2,18},{4,20},{6,22},{8,24},{10,26},{12,28},{14,30},{16,0},... | collective-permute-start | bytes 98312 | tf_op jit(solution)/shard_map/ppermute | solution.py:47
  109.3 1.6 %collective-permute-start.33 = (bf16[128,128]{1,0:T(8,128)(2,1)S(1)}, bf16[128,128]{1,0:T(8,128)(2,1)S(1)}, u32[]{:S(2)}, u32[]{:S(2)}) collective-permute-start(bf16[128,128]{1,0:T(8,128)(2,1)S(1)} %select_convert_fusion.8), channel_id=1, source_target_pairs={{0,24},{2,26},{4,28},{6,30},{8,16},{10,18},{12,20},{14,22},{16,8},... | collective-permute-start | bytes 98312 | tf_op jit(solution)/shard_map/ppermute | solution.py:47
  111.7 3.8 %collective-permute-done.33 = bf16[128,128]{1,0:T(8,128)(2,1)S(1)} collective-permute-done((bf16[128,128]{1,0:T(8,128)(2,1)S(1)}, bf16[128,128]{1,0:T(8,128)(2,1)S(1)}, u32[]{:S(2)}, u32[]{:S(2)}) %collective-permute-start.33) | collective-permute-done | bytes 32800 | tf_op jit(solution)/shard_map/ppermute | solution.py:47
  115.7 1.6 %collective-permute-start.39 = (bf16[272,128]{1,0:T(8,128)(2,1)S(1)}, bf16[272,128]{1,0:T(8,128)(2,1)S(1)}, u32[]{:S(2)}, u32[]{:S(2)}) collective-permute-start(bf16[272,128]{1,0:T(8,128)(2,1)S(1)} %pad_maximum_fusion.27), channel_id=1, source_target_pairs={{0,24},{2,26},{4,28},{6,30},{8,16},{10,18},{12,20},{14,22},{16,8},... | collective-permute-start | bytes 208904 | tf_op jit(solution)/shard_map/ppermute | solution.py:47
  117.3 2.8 %collective-permute-start.41 = (bf16[272,128]{1,0:T(8,128)(2,1)S(1)}, bf16[272,128]{1,0:T(8,128)(2,1)S(1)}, u32[]{:S(2)}, u32[]{:S(2)}) collective-permute-start(bf16[272,128]{1,0:T(8,128)(2,1)S(1)} %pad_maximum_fusion.27), channel_id=1, source_target_pairs={{0,8},{2,10},{4,12},{6,14},{8,0},{10,2},{12,4},{14,6},{16,24},{18,... | collective-permute-start | bytes 208904 | tf_op jit(solution)/shard_map/ppermute | solution.py:47
  120.2 1.0 collective-permute-start.34
  121.2 0.8 collective-permute-done.39
  122.0 3.6 %collective-permute-done.40 = bf16[272,128]{1,0:T(8,128)(2,1)S(1)} collective-permute-done((bf16[272,128]{1,0:T(8,128)(2,1)S(1)}, bf16[272,128]{1,0:T(8,128)(2,1)S(1)}, u32[]{:S(2)}, u32[]{:S(2)}) %collective-permute-start.40) | collective-permute-done | bytes 69664 | tf_op jit(solution)/shard_map/ppermute | solution.py:47
  126.6 1.7 %collective-permute-start.35 = (f32[2,2,2,16,128]{4,3,1,2,0:T(8,128)S(1)}, f32[2,2,2,16,128]{4,3,1,2,0:T(8,128)S(1)}, u32[]{:S(2)}, u32[]{:S(2)}) collective-permute-start(f32[2,2,2,16,128]{4,3,1,2,0:T(8,128)S(1)} %get-tuple-element.198), channel_id=1, source_target_pairs={{0,24},{2,26},{4,28},{6,30},{8,16},{10,18},{12,20},{14,22},{16,8},... | collective-permute-start | bytes 196616 | tf_op jit(solution)/shard_map/ppermute | solution.py:47
  128.3 2.7 %collective-permute-start.37 = (f32[2,2,2,16,128]{4,3,1,2,0:T(8,128)S(1)}, f32[2,2,2,16,128]{4,3,1,2,0:T(8,128)S(1)}, u32[]{:S(2)}, u32[]{:S(2)}) collective-permute-start(f32[2,2,2,16,128]{4,3,1,2,0:T(8,128)S(1)} %get-tuple-element.72), channel_id=1, source_target_pairs={{0,8},{2,10},{4,12},{6,14},{8,0},{10,2},{12,4},{14,6},{16,24},{18,... | collective-permute-start | bytes 196616 | tf_op jit(solution)/shard_map/ppermute | solution.py:47
  131.1 1.4 collective-permute-start.45
  132.7 1.4 collective-permute-done.36
  136.6 1.4 fusion.154
  139.3 1.5 collective-permute-start.44
  141.1 1.4 fusion.153
  143.2 5.6 %collective-permute-done.44 = bf16[1080,128]{1,0:T(8,128)(2,1)S(1)} collective-permute-done((bf16[1080,128]{1,0:T(8,128)(2,1)S(1)}, bf16[1080,128]{1,0:T(8,128)(2,1)S(1)}, u32[]{:S(2)}, u32[]{:S(2)}) %collective-permute-start.44) | collective-permute-done | bytes 276512 | tf_op jit(solution)/shard_map/ppermute | solution.py:299
  148.9 5.0 %collective-permute-done.47 = bf16[1080,128]{1,0:T(8,128)(2,1)S(1)} collective-permute-done((bf16[1080,128]{1,0:T(8,128)(2,1)S(1)}, bf16[1080,128]{1,0:T(8,128)(2,1)S(1)}, u32[]{:S(2)}, u32[]{:S(2)}) %collective-permute-start.47) | collective-permute-done | bytes 276512 | tf_op jit(solution)/shard_map/ppermute | solution.py:299
  154.0 1.1 pad_maximum_fusion
  (252 shorter events, 17.7 us)
Async XLA Ops:
  1.4 1.2 copy-start
  2.6 0.9 copy-start.2
  3.6 6.5 %copy-start.6 = (s32[2,1]{0,1:T(1,128)S(1)}, s32[2,1]{0,1:T(1,128)}, u32[]{:S(2)}) copy-start(s32[2,1]{0,1:T(1,128)} %param.9) | copy-start | bytes 28
  9.5 7.1 %collective-permute-start.1 = (bf16[144,1024]{1,0:T(8,128)(2,1)S(1)}, bf16[144,1024]{1,0:T(8,128)(2,1)}, u32[]{:S(2)}, u32[]{:S(2)}) collective-permute-start(bf16[144,1024]{1,0:T(8,128)(2,1)S(1)} %fusion.9), channel_id=1, source_target_pairs={{0,2},{2,0},{4,6},{6,4},{8,10},{10,8},{12,14},{14,12},{16,18},{18,... | collective-permute-start | bytes 884744 | tf_op jit(solution)/shard_map/ppermute | solution.py:47
  15.9 8.3 %copy-start.5 = (bf16[16,2048]{1,0:T(8,128)(2,1)}, bf16[16,2048]{1,0:T(8,128)(2,1)S(1)}, u32[]{:S(2)}) copy-start(bf16[16,2048]{1,0:T(8,128)(2,1)S(1)} %get-tuple-element.210) | copy-start | bytes 196612
  18.9 4.5 %collective-permute-start = (bf16[176,1024]{1,0:T(8,128)(2,1)}, bf16[176,1024]{1,0:T(8,128)(2,1)}, u32[]{:S(2)}, u32[]{:S(2)}) collective-permute-start(bf16[176,1024]{1,0:T(8,128)(2,1)} %fusion.8), channel_id=1, source_target_pairs={{0,2},{2,0},{4,6},{6,4},{8,10},{10,8},{12,14},{14,12},{16,18},{18,... | collective-permute-start | bytes 1081352 | tf_op jit(solution)/shard_map/ppermute | solution.py:47
  20.5 7.1 %collective-permute-start.2 = (bf16[144,512]{1,0:T(8,128)(2,1)S(1)}, bf16[144,512]{1,0:T(8,128)(2,1)S(1)}, u32[]{:S(2)}, u32[]{:S(2)}) collective-permute-start(bf16[144,512]{1,0:T(8,128)(2,1)S(1)} %fusion.13), channel_id=1, source_target_pairs={{0,4},{2,6},{4,0},{6,2},{8,12},{10,14},{12,8},{14,10},{16,20},{18,... | collective-permute-start | bytes 442376 | tf_op jit(solution)/shard_map/ppermute | solution.py:47
  25.3 24.4 %copy-start.4 = (f32[16,2048]{1,0:T(8,128)S(1)}, f32[16,2048]{1,0:T(8,128)}, u32[]{:S(2)}) copy-start(f32[16,2048]{1,0:T(8,128)} %slice_bitcast_fusion) | copy-start | bytes 393220
  27.8 7.8 %collective-permute-start.4 = (bf16[208,512]{1,0:T(8,128)(2,1)S(1)}, bf16[208,512]{1,0:T(8,128)(2,1)S(1)}, u32[]{:S(2)}, u32[]{:S(2)}) collective-permute-start(bf16[208,512]{1,0:T(8,128)(2,1)S(1)} %fusion.12), channel_id=1, source_target_pairs={{0,4},{2,6},{4,0},{6,2},{8,12},{10,14},{12,8},{14,10},{16,20},{18,... | collective-permute-start | bytes 638984 | tf_op jit(solution)/shard_map/ppermute | solution.py:47
  29.8 9.9 %collective-permute-start.6 = (bf16[144,128]{1,0:T(8,128)(2,1)S(1)}, bf16[144,128]{1,0:T(8,128)(2,1)S(1)}, u32[]{:S(2)}, u32[]{:S(2)}) collective-permute-start(bf16[144,128]{1,0:T(8,128)(2,1)S(1)} %fusion.63), channel_id=1, source_target_pairs={{0,24},{2,26},{4,28},{6,30},{8,16},{10,18},{12,20},{14,22},{16,8},... | collective-permute-start | bytes 110600 | tf_op jit(solution)/shard_map/ppermute | solution.py:47
  33.6 6.6 %collective-permute-start.5 = (bf16[144,128]{1,0:T(8,128)(2,1)S(1)}, bf16[144,128]{1,0:T(8,128)(2,1)S(1)}, u32[]{:S(2)}, u32[]{:S(2)}) collective-permute-start(bf16[144,128]{1,0:T(8,128)(2,1)S(1)} %fusion.62), channel_id=1, source_target_pairs={{0,16},{2,18},{4,20},{6,22},{8,24},{10,26},{12,28},{14,30},{16,0},... | collective-permute-start | bytes 110600 | tf_op jit(solution)/shard_map/ppermute | solution.py:47
  34.0 6.3 %collective-permute-start.3 = (bf16[144,128]{1,0:T(8,128)(2,1)S(1)}, bf16[144,128]{1,0:T(8,128)(2,1)S(1)}, u32[]{:S(2)}, u32[]{:S(2)}) collective-permute-start(bf16[144,128]{1,0:T(8,128)(2,1)S(1)} %fusion.61), channel_id=1, source_target_pairs={{0,8},{2,10},{4,12},{6,14},{8,0},{10,2},{12,4},{14,6},{16,24},{18,... | collective-permute-start | bytes 110600 | tf_op jit(solution)/shard_map/ppermute | solution.py:47
  36.0 7.1 %collective-permute-start.8 = (bf16[272,128]{1,0:T(8,128)(2,1)S(1)}, bf16[272,128]{1,0:T(8,128)(2,1)S(1)}, u32[]{:S(2)}, u32[]{:S(2)}) collective-permute-start(bf16[272,128]{1,0:T(8,128)(2,1)S(1)} %get-tuple-element.239), channel_id=1, source_target_pairs={{0,16},{2,18},{4,20},{6,22},{8,24},{10,26},{12,28},{14,30},{16,0},... | collective-permute-start | bytes 208904 | tf_op jit(solution)/shard_map/ppermute | solution.py:47
  38.2 6.2 %collective-permute-start.7 = (bf16[272,128]{1,0:T(8,128)(2,1)S(1)}, bf16[272,128]{1,0:T(8,128)(2,1)S(1)}, u32[]{:S(2)}, u32[]{:S(2)}) collective-permute-start(bf16[272,128]{1,0:T(8,128)(2,1)S(1)} %get-tuple-element.238), channel_id=1, source_target_pairs={{0,24},{2,26},{4,28},{6,30},{8,16},{10,18},{12,20},{14,22},{16,8},... | collective-permute-start | bytes 208904 | tf_op jit(solution)/shard_map/ppermute | solution.py:47
  39.7 5.1 %collective-permute-start.9 = (bf16[272,128]{1,0:T(8,128)(2,1)S(1)}, bf16[272,128]{1,0:T(8,128)(2,1)S(1)}, u32[]{:S(2)}, u32[]{:S(2)}) collective-permute-start(bf16[272,128]{1,0:T(8,128)(2,1)S(1)} %get-tuple-element.240), channel_id=1, source_target_pairs={{0,8},{2,10},{4,12},{6,14},{8,0},{10,2},{12,4},{14,6},{16,24},{18,... | collective-permute-start | bytes 208904 | tf_op jit(solution)/shard_map/ppermute | solution.py:47
  45.2 6.2 %collective-permute-start.10 = (bf16[272,128]{1,0:T(8,128)(2,1)S(1)}, bf16[272,128]{1,0:T(8,128)(2,1)S(1)}, u32[]{:S(2)}, u32[]{:S(2)}) collective-permute-start(bf16[272,128]{1,0:T(8,128)(2,1)S(1)} %fusion.33), channel_id=1, source_target_pairs={{0,24},{2,26},{4,28},{6,30},{8,16},{10,18},{12,20},{14,22},{16,8},... | collective-permute-start | bytes 208904 | tf_op jit(solution)/shard_map/ppermute | solution.py:47
  47.5 5.4 %collective-permute-start.11 = (bf16[272,128]{1,0:T(8,128)(2,1)S(1)}, bf16[272,128]{1,0:T(8,128)(2,1)S(1)}, u32[]{:S(2)}, u32[]{:S(2)}) collective-permute-start(bf16[272,128]{1,0:T(8,128)(2,1)S(1)} %fusion.33), channel_id=1, source_target_pairs={{0,16},{2,18},{4,20},{6,22},{8,24},{10,26},{12,28},{14,30},{16,0},... | collective-permute-start | bytes 208904 | tf_op jit(solution)/shard_map/ppermute | solution.py:47
  47.5 5.4 %collective-permute-start.12 = (bf16[272,128]{1,0:T(8,128)(2,1)S(1)}, bf16[272,128]{1,0:T(8,128)(2,1)S(1)}, u32[]{:S(2)}, u32[]{:S(2)}) collective-permute-start(bf16[272,128]{1,0:T(8,128)(2,1)S(1)} %fusion.33), channel_id=1, source_target_pairs={{0,8},{2,10},{4,12},{6,14},{8,0},{10,2},{12,4},{14,6},{16,24},{18,... | collective-permute-start | bytes 208904 | tf_op jit(solution)/shard_map/ppermute | solution.py:47
  49.7 7.0 %collective-permute-start.21 = (f32[1,16,1024]{2,1,0:T(8,128)S(1)}, f32[1,16,1024]{2,1,0:T(8,128)S(1)}, u32[]{:S(2)}, u32[]{:S(2)}) collective-permute-start(f32[1,16,1024]{2,1,0:T(8,128)S(1)} %slice_select_fusion.2), channel_id=1, source_target_pairs={{0,2},{2,0},{4,6},{6,4},{8,10},{10,8},{12,14},{14,12},{16,18},{18,... | collective-permute-start | bytes 196616 | tf_op jit(solution)/shard_map/ppermute | solution.py:47
  53.1 5.2 %collective-permute-start.14 = (bf16[144,512]{1,0:T(8,128)(2,1)S(1)}, bf16[144,512]{1,0:T(8,128)(2,1)S(1)}, u32[]{:S(2)}, u32[]{:S(2)}) collective-permute-start(bf16[144,512]{1,0:T(8,128)(2,1)S(1)} %pad_maximum_fusion.14), channel_id=1, source_target_pairs={{0,4},{2,6},{4,0},{6,2},{8,12},{10,14},{12,8},{14,10},{16,20},{18,... | collective-permute-start | bytes 442376 | tf_op jit(solution)/shard_map/ppermute | solution.py:47
  58.3 3.7 %collective-permute-start.15 = (bf16[144,1024]{1,0:T(8,128)(2,1)S(1)}, bf16[144,1024]{1,0:T(8,128)(2,1)S(1)}, u32[]{:S(2)}, u32[]{:S(2)}) collective-permute-start(bf16[144,1024]{1,0:T(8,128)(2,1)S(1)} %pad_maximum_fusion.7), channel_id=1, source_target_pairs={{0,2},{2,0},{4,6},{6,4},{8,10},{10,8},{12,14},{14,12},{16,18},{18,... | collective-permute-start | bytes 884744 | tf_op jit(solution)/shard_map/ppermute | solution.py:47
  61.3 6.0 %collective-permute-start.13 = (bf16[128,512]{1,0:T(8,128)(2,1)S(1)}, bf16[128,512]{1,0:T(8,128)(2,1)S(1)}, u32[]{:S(2)}, u32[]{:S(2)}) collective-permute-start(bf16[128,512]{1,0:T(8,128)(2,1)S(1)} %pad_maximum_fusion.19), channel_id=1, source_target_pairs={{0,4},{2,6},{4,0},{6,2},{8,12},{10,14},{12,8},{14,10},{16,20},{18,... | collective-permute-start | bytes 393224 | tf_op jit(solution)/shard_map/ppermute | solution.py:47
  62.4 14.0 %copy-start.1 = (f32[1080,256]{1,0:T(8,128)S(1)}, f32[1080,256]{1,0:T(8,128)}, u32[]{:S(2)}) copy-start(f32[1080,256]{1,0:T(8,128)} %residual.1) | copy-start | bytes 3317764
  67.3 2.6 %collective-permute-start.16 = (bf16[128,1024]{1,0:T(8,128)(2,1)S(1)}, bf16[128,1024]{1,0:T(8,128)(2,1)S(1)}, u32[]{:S(2)}, u32[]{:S(2)}) collective-permute-start(bf16[128,1024]{1,0:T(8,128)(2,1)S(1)} %pad_maximum_fusion.10), channel_id=1, source_target_pairs={{0,2},{2,0},{4,6},{6,4},{8,10},{10,8},{12,14},{14,12},{16,18},{18,... | collective-permute-start | bytes 786440 | tf_op jit(solution)/shard_map/ppermute | solution.py:47
  67.4 9.1 %collective-permute-start.18 = (bf16[1080,128]{1,0:T(8,128)(2,1)S(1)}, bf16[1080,128]{1,0:T(8,128)(2,1)S(1)}, u32[]{:S(2)}, u32[]{:S(2)}) collective-permute-start(bf16[1080,128]{1,0:T(8,128)(2,1)S(1)} %get-tuple-element.282), channel_id=1, source_target_pairs={{0,1},{1,0},{2,3},{3,2},{4,5},{5,4},{6,7},{7,6},{8,9},{9,8},{10,11... | collective-permute-start | bytes 829448 | tf_op jit(solution)/shard_map/ppermute | solution.py:299
  69.0 10.5 %collective-permute-start.22 = (f32[1,32,512]{2,1,0:T(8,128)S(1)}, f32[1,32,512]{2,1,0:T(8,128)S(1)}, u32[]{:S(2)}, u32[]{:S(2)}) collective-permute-start(f32[1,32,512]{2,1,0:T(8,128)S(1)} %broadcast_select_fusion.29), channel_id=1, source_target_pairs={{0,4},{2,6},{4,0},{6,2},{8,12},{10,14},{12,8},{14,10},{16,20},{18,... | collective-permute-start | bytes 196616 | tf_op jit(solution)/shard_map/ppermute | solution.py:47
  77.9 3.1 %collective-permute-start.19 = (bf16[128,1024]{1,0:T(8,128)(2,1)S(1)}, bf16[128,1024]{1,0:T(8,128)(2,1)S(1)}, u32[]{:S(2)}, u32[]{:S(2)}) collective-permute-start(bf16[128,1024]{1,0:T(8,128)(2,1)S(1)} %select_convert_fusion.1), channel_id=1, source_target_pairs={{0,2},{2,0},{4,6},{6,4},{8,10},{10,8},{12,14},{14,12},{16,18},{18,... | collective-permute-start | bytes 786440 | tf_op jit(solution)/shard_map/ppermute | solution.py:47
  79.5 9.1 %collective-permute-start.17 = (bf16[1080,128]{1,0:T(8,128)(2,1)S(1)}, bf16[1080,128]{1,0:T(8,128)(2,1)S(1)}, u32[]{:S(2)}, u32[]{:S(2)}) collective-permute-start(bf16[1080,128]{1,0:T(8,128)(2,1)S(1)} %get-tuple-element.280), channel_id=1, source_target_pairs={{0,1},{1,0},{2,3},{3,2},{4,5},{5,4},{6,7},{7,6},{8,9},{9,8},{10,11... | collective-permute-start | bytes 829448 | tf_op jit(solution)/shard_map/ppermute | solution.py:299
  90.0 5.4 %collective-permute-start.20 = (bf16[128,1024]{1,0:T(8,128)(2,1)S(1)}, bf16[128,1024]{1,0:T(8,128)(2,1)S(1)}, u32[]{:S(2)}, u32[]{:S(2)}) collective-permute-start(bf16[128,1024]{1,0:T(8,128)(2,1)S(1)} %select_convert_fusion), channel_id=1, source_target_pairs={{0,2},{2,0},{4,6},{6,4},{8,10},{10,8},{12,14},{14,12},{16,18},{18,... | collective-permute-start | bytes 786440 | tf_op jit(solution)/shard_map/ppermute | solution.py:47
  90.1 6.8 %collective-permute-start.25 = (f32[1,64,128]{2,1,0:T(8,128)S(1)}, f32[1,64,128]{2,1,0:T(8,128)S(1)}, u32[]{:S(2)}, u32[]{:S(2)}) collective-permute-start(f32[1,64,128]{2,1,0:T(8,128)S(1)} %get-tuple-element.81), channel_id=1, source_target_pairs={{0,8},{2,10},{4,12},{6,14},{8,0},{10,2},{12,4},{14,6},{16,24},{18,... | collective-permute-start | bytes 98312 | tf_op jit(solution)/shard_map/ppermute | solution.py:47
  91.3 5.6 %collective-permute-start.24 = (f32[1,64,128]{2,1,0:T(8,128)S(1)}, f32[1,64,128]{2,1,0:T(8,128)S(1)}, u32[]{:S(2)}, u32[]{:S(2)}) collective-permute-start(f32[1,64,128]{2,1,0:T(8,128)S(1)} %get-tuple-element.224), channel_id=1, source_target_pairs={{0,16},{2,18},{4,20},{6,22},{8,24},{10,26},{12,28},{14,30},{16,0},... | collective-permute-start | bytes 98312 | tf_op jit(solution)/shard_map/ppermute | solution.py:47
  93.1 5.7 %collective-permute-start.23 = (f32[1,64,128]{2,1,0:T(8,128)S(1)}, f32[1,64,128]{2,1,0:T(8,128)S(1)}, u32[]{:S(2)}, u32[]{:S(2)}) collective-permute-start(f32[1,64,128]{2,1,0:T(8,128)S(1)} %get-tuple-element.225), channel_id=1, source_target_pairs={{0,24},{2,26},{4,28},{6,30},{8,16},{10,18},{12,20},{14,22},{16,8},... | collective-permute-start | bytes 98312 | tf_op jit(solution)/shard_map/ppermute | solution.py:47
  94.7 6.4 %collective-permute-start.26 = (bf16[128,512]{1,0:T(8,128)(2,1)S(1)}, bf16[128,512]{1,0:T(8,128)(2,1)S(1)}, u32[]{:S(2)}, u32[]{:S(2)}) collective-permute-start(bf16[128,512]{1,0:T(8,128)(2,1)S(1)} %select_convert_fusion.5), channel_id=1, source_target_pairs={{0,4},{2,6},{4,0},{6,2},{8,12},{10,14},{12,8},{14,10},{16,20},{18,... | collective-permute-start | bytes 393224 | tf_op jit(solution)/shard_map/ppermute | solution.py:47
  95.5 10.8 %collective-permute-start.28 = (bf16[128,512]{1,0:T(8,128)(2,1)S(1)}, bf16[128,512]{1,0:T(8,128)(2,1)S(1)}, u32[]{:S(2)}, u32[]{:S(2)}) collective-permute-start(bf16[128,512]{1,0:T(8,128)(2,1)S(1)} %select_convert_fusion.4), channel_id=1, source_target_pairs={{0,4},{2,6},{4,0},{6,2},{8,12},{10,14},{12,8},{14,10},{16,20},{18,... | collective-permute-start | bytes 393224 | tf_op jit(solution)/shard_map/ppermute | solution.py:47
  101.1 8.2 %collective-permute-start.27 = (bf16[128,128]{1,0:T(8,128)(2,1)S(1)}, bf16[128,128]{1,0:T(8,128)(2,1)S(1)}, u32[]{:S(2)}, u32[]{:S(2)}) collective-permute-start(bf16[128,128]{1,0:T(8,128)(2,1)S(1)} %get-tuple-element.202), channel_id=1, source_target_pairs={{0,8},{2,10},{4,12},{6,14},{8,0},{10,2},{12,4},{14,6},{16,24},{18,... | collective-permute-start | bytes 98312 | tf_op jit(solution)/shard_map/ppermute | solution.py:47
  101.4 9.6 %collective-permute-start.29 = (bf16[128,128]{1,0:T(8,128)(2,1)S(1)}, bf16[128,128]{1,0:T(8,128)(2,1)S(1)}, u32[]{:S(2)}, u32[]{:S(2)}) collective-permute-start(bf16[128,128]{1,0:T(8,128)(2,1)S(1)} %select_convert_fusion.12), channel_id=1, source_target_pairs={{0,16},{2,18},{4,20},{6,22},{8,24},{10,26},{12,28},{14,30},{16,0},... | collective-permute-start | bytes 98312 | tf_op jit(solution)/shard_map/ppermute | solution.py:47
  104.0 7.0 %collective-permute-start.30 = (bf16[128,128]{1,0:T(8,128)(2,1)S(1)}, bf16[128,128]{1,0:T(8,128)(2,1)S(1)}, u32[]{:S(2)}, u32[]{:S(2)}) collective-permute-start(bf16[128,128]{1,0:T(8,128)(2,1)S(1)} %get-tuple-element.201), channel_id=1, source_target_pairs={{0,24},{2,26},{4,28},{6,30},{8,16},{10,18},{12,20},{14,22},{16,8},... | collective-permute-start | bytes 98312 | tf_op jit(solution)/shard_map/ppermute | solution.py:47
  106.5 4.5 %collective-permute-start.31 = (bf16[128,128]{1,0:T(8,128)(2,1)S(1)}, bf16[128,128]{1,0:T(8,128)(2,1)S(1)}, u32[]{:S(2)}, u32[]{:S(2)}) collective-permute-start(bf16[128,128]{1,0:T(8,128)(2,1)S(1)} %get-tuple-element.200), channel_id=1, source_target_pairs={{0,8},{2,10},{4,12},{6,14},{8,0},{10,2},{12,4},{14,6},{16,24},{18,... | collective-permute-start | bytes 98312 | tf_op jit(solution)/shard_map/ppermute | solution.py:47
  106.6 5.1 %collective-permute-start.32 = (bf16[128,128]{1,0:T(8,128)(2,1)S(1)}, bf16[128,128]{1,0:T(8,128)(2,1)S(1)}, u32[]{:S(2)}, u32[]{:S(2)}) collective-permute-start(bf16[128,128]{1,0:T(8,128)(2,1)S(1)} %get-tuple-element.199), channel_id=1, source_target_pairs={{0,16},{2,18},{4,20},{6,22},{8,24},{10,26},{12,28},{14,30},{16,0},... | collective-permute-start | bytes 98312 | tf_op jit(solution)/shard_map/ppermute | solution.py:47
  109.3 6.1 %collective-permute-start.33 = (bf16[128,128]{1,0:T(8,128)(2,1)S(1)}, bf16[128,128]{1,0:T(8,128)(2,1)S(1)}, u32[]{:S(2)}, u32[]{:S(2)}) collective-permute-start(bf16[128,128]{1,0:T(8,128)(2,1)S(1)} %select_convert_fusion.8), channel_id=1, source_target_pairs={{0,24},{2,26},{4,28},{6,30},{8,16},{10,18},{12,20},{14,22},{16,8},... | collective-permute-start | bytes 98312 | tf_op jit(solution)/shard_map/ppermute | solution.py:47
  115.7 6.3 %collective-permute-start.39 = (bf16[272,128]{1,0:T(8,128)(2,1)S(1)}, bf16[272,128]{1,0:T(8,128)(2,1)S(1)}, u32[]{:S(2)}, u32[]{:S(2)}) collective-permute-start(bf16[272,128]{1,0:T(8,128)(2,1)S(1)} %pad_maximum_fusion.27), channel_id=1, source_target_pairs={{0,24},{2,26},{4,28},{6,30},{8,16},{10,18},{12,20},{14,22},{16,8},... | collective-permute-start | bytes 208904 | tf_op jit(solution)/shard_map/ppermute | solution.py:47
  117.3 8.3 %collective-permute-start.40 = (bf16[272,128]{1,0:T(8,128)(2,1)S(1)}, bf16[272,128]{1,0:T(8,128)(2,1)S(1)}, u32[]{:S(2)}, u32[]{:S(2)}) collective-permute-start(bf16[272,128]{1,0:T(8,128)(2,1)S(1)} %pad_maximum_fusion.27), channel_id=1, source_target_pairs={{0,16},{2,18},{4,20},{6,22},{8,24},{10,26},{12,28},{14,30},{16,0},... | collective-permute-start | bytes 208904 | tf_op jit(solution)/shard_map/ppermute | solution.py:47
  117.3 8.3 %collective-permute-start.41 = (bf16[272,128]{1,0:T(8,128)(2,1)S(1)}, bf16[272,128]{1,0:T(8,128)(2,1)S(1)}, u32[]{:S(2)}, u32[]{:S(2)}) collective-permute-start(bf16[272,128]{1,0:T(8,128)(2,1)S(1)} %pad_maximum_fusion.27), channel_id=1, source_target_pairs={{0,8},{2,10},{4,12},{6,14},{8,0},{10,2},{12,4},{14,6},{16,24},{18,... | collective-permute-start | bytes 208904 | tf_op jit(solution)/shard_map/ppermute | solution.py:47
  120.2 6.3 %collective-permute-start.34 = (f32[4,2,2,16,128]{4,3,1,0,2:T(8,128)S(1)}, f32[4,2,2,16,128]{4,3,1,0,2:T(8,128)S(1)}, u32[]{:S(2)}, u32[]{:S(2)}) collective-permute-start(f32[4,2,2,16,128]{4,3,1,0,2:T(8,128)S(1)} %fusion.21), channel_id=1, source_target_pairs={{0,4},{2,6},{4,0},{6,2},{8,12},{10,14},{12,8},{14,10},{16,20},{18,... | collective-permute-start | bytes 393224 | tf_op jit(solution)/shard_map/ppermute | solution.py:47
  125.7 10.5 %copy-start.3 = (f32[16,4096]{1,0:T(8,128)S(1)}, f32[16,4096]{1,0:T(8,128)}, u32[]{:S(2)}) copy-start(f32[16,4096]{1,0:T(8,128)} %coefficients.1) | copy-start | bytes 786436
  125.8 8.6 %collective-permute-start.42 = (bf16[144,512]{1,0:T(8,128)(2,1)S(1)}, bf16[144,512]{1,0:T(8,128)(2,1)S(1)}, u32[]{:S(2)}, u32[]{:S(2)}) collective-permute-start(bf16[144,512]{1,0:T(8,128)(2,1)S(1)} %slice.894), channel_id=1, source_target_pairs={{0,4},{2,6},{4,0},{6,2},{8,12},{10,14},{12,8},{14,10},{16,20},{18,... | collective-permute-start | bytes 442376 | tf_op jit(solution)/shard_map/ppermute | solution.py:47
  126.6 6.1 %collective-permute-start.35 = (f32[2,2,2,16,128]{4,3,1,2,0:T(8,128)S(1)}, f32[2,2,2,16,128]{4,3,1,2,0:T(8,128)S(1)}, u32[]{:S(2)}, u32[]{:S(2)}) collective-permute-start(f32[2,2,2,16,128]{4,3,1,2,0:T(8,128)S(1)} %get-tuple-element.198), channel_id=1, source_target_pairs={{0,24},{2,26},{4,28},{6,30},{8,16},{10,18},{12,20},{14,22},{16,8},... | collective-permute-start | bytes 196616 | tf_op jit(solution)/shard_map/ppermute | solution.py:47
  128.3 5.8 %collective-permute-start.36 = (f32[2,2,2,16,128]{4,3,1,2,0:T(8,128)S(1)}, f32[2,2,2,16,128]{4,3,1,2,0:T(8,128)S(1)}, u32[]{:S(2)}, u32[]{:S(2)}) collective-permute-start(f32[2,2,2,16,128]{4,3,1,2,0:T(8,128)S(1)} %get-tuple-element.197), channel_id=1, source_target_pairs={{0,16},{2,18},{4,20},{6,22},{8,24},{10,26},{12,28},{14,30},{16,0},... | collective-permute-start | bytes 196616 | tf_op jit(solution)/shard_map/ppermute | solution.py:47
  128.3 5.8 %collective-permute-start.37 = (f32[2,2,2,16,128]{4,3,1,2,0:T(8,128)S(1)}, f32[2,2,2,16,128]{4,3,1,2,0:T(8,128)S(1)}, u32[]{:S(2)}, u32[]{:S(2)}) collective-permute-start(f32[2,2,2,16,128]{4,3,1,2,0:T(8,128)S(1)} %get-tuple-element.72), channel_id=1, source_target_pairs={{0,8},{2,10},{4,12},{6,14},{8,0},{10,2},{12,4},{14,6},{16,24},{18,... | collective-permute-start | bytes 196616 | tf_op jit(solution)/shard_map/ppermute | solution.py:47
  131.1 7.0 %collective-permute-start.45 = (bf16[128,512]{1,0:T(8,128)(2,1)S(1)}, bf16[128,512]{1,0:T(8,128)(2,1)S(1)}, u32[]{:S(2)}, u32[]{:S(2)}) collective-permute-start(bf16[128,512]{1,0:T(8,128)(2,1)S(1)} %pad_maximum_fusion.17), channel_id=1, source_target_pairs={{0,4},{2,6},{4,0},{6,2},{8,12},{10,14},{12,8},{14,10},{16,20},{18,... | collective-permute-start | bytes 393224 | tf_op jit(solution)/shard_map/ppermute | solution.py:47
  134.3 1.4 collective-permute-start.38
  134.4 1.8 %collective-permute-start.43 = (bf16[144,1024]{1,0:T(8,128)(2,1)S(1)}, bf16[144,1024]{1,0:T(8,128)(2,1)S(1)}, u32[]{:S(2)}, u32[]{:S(2)}) collective-permute-start(bf16[144,1024]{1,0:T(8,128)(2,1)S(1)} %pad_maximum_fusion.8), channel_id=1, source_target_pairs={{0,2},{2,0},{4,6},{6,4},{8,10},{10,8},{12,14},{14,12},{16,18},{18,... | collective-permute-start | bytes 884744 | tf_op jit(solution)/shard_map/ppermute | solution.py:47
  138.2 2.6 %collective-permute-start.46 = (bf16[128,1024]{1,0:T(8,128)(2,1)S(1)}, bf16[128,1024]{1,0:T(8,128)(2,1)S(1)}, u32[]{:S(2)}, u32[]{:S(2)}) collective-permute-start(bf16[128,1024]{1,0:T(8,128)(2,1)S(1)} %pad_maximum_fusion.13), channel_id=1, source_target_pairs={{0,2},{2,0},{4,6},{6,4},{8,10},{10,8},{12,14},{14,12},{16,18},{18,... | collective-permute-start | bytes 786440 | tf_op jit(solution)/shard_map/ppermute | solution.py:47
  139.3 9.5 %collective-permute-start.44 = (bf16[1080,128]{1,0:T(8,128)(2,1)S(1)}, bf16[1080,128]{1,0:T(8,128)(2,1)S(1)}, u32[]{:S(2)}, u32[]{:S(2)}) collective-permute-start(bf16[1080,128]{1,0:T(8,128)(2,1)S(1)} %get-tuple-element.286), channel_id=1, source_target_pairs={{0,1},{1,0},{2,3},{3,2},{4,5},{5,4},{6,7},{7,6},{8,9},{9,8},{10,11... | collective-permute-start | bytes 829448 | tf_op jit(solution)/shard_map/ppermute | solution.py:299
  142.6 11.3 %collective-permute-start.47 = (bf16[1080,128]{1,0:T(8,128)(2,1)S(1)}, bf16[1080,128]{1,0:T(8,128)(2,1)S(1)}, u32[]{:S(2)}, u32[]{:S(2)}) collective-permute-start(bf16[1080,128]{1,0:T(8,128)(2,1)S(1)} %get-tuple-element.284), channel_id=1, source_target_pairs={{0,1},{1,0},{2,3},{3,2},{4,5},{5,4},{6,7},{7,6},{8,9},{9,8},{10,11... | collective-permute-start | bytes 829448 | tf_op jit(solution)/shard_map/ppermute | solution.py:299

commit v3 on v2

--- a/solution.py
+++ b/solution.py
@@ -1,3 +1,5 @@
+import functools
+
 import jax
 import jax.numpy as jnp
 from jax import lax
@@ -24,7 +26,8 @@
 class Stage:
     def __init__(self, size, radix, stride):
         self.size, self.radix, self.stride = size, radix, stride
-        self.digit = (lax.axis_index("samp") // stride) % radix
+        digit = (lax.axis_index("samp") // stride) % radix
+        self.mine = [digit == d for d in range(radix)]
 
     def partner(self, digit, step):
         if self.radix & (self.radix - 1) == 0:
@@ -46,6 +49,13 @@
     def send(self, value, step):
         return lax.ppermute(value, "samp", self.pairs(step))
 
+    def by_digit(self, values):
+        value = values[0]
+        for d in range(1, self.radix):
+            if values[d] is not value:
+                value = jnp.where(self.mine[d], values[d], value)
+        return value
+
 
 def stages(size):
     out, stride = [], 1
@@ -55,11 +65,8 @@
     return out
 
 
-def pick(parts, index):
-    value = parts[0]
-    for i in range(1, len(parts)):
-        value = jnp.where(index == i, parts[i], value)
-    return value
+def pick(parts, stage, step):
+    return stage.by_digit([parts[stage.partner(d, step)] for d in range(stage.radix)])
 
 
 def split_cols(value, radix):
@@ -69,13 +76,8 @@
 
 def ordered(stage, own, received):
     by_step = [own] + received
-    out = []
-    for digit in range(stage.radix):
-        value = by_step[0]
-        for step in range(1, stage.radix):
-            value = jnp.where(stage.source(stage.digit, step) == digit, by_step[step], value)
-        out.append(value)
-    return out
+    step_of = [{stage.source(d, step): step for step in range(stage.radix)} for d in range(stage.radix)]
+    return [stage.by_digit([by_step[step_of[d][o]] for d in range(stage.radix)]) for o in range(stage.radix)]
 
 
 def rounded_to_bf16(value):
@@ -86,7 +88,7 @@
     out = []
     for _ in range(terms):
         top = rounded_to_bf16(value)
-        out.append(top.astype(BF16))
+        out.append(top)
         value = value - top
     return out
 
@@ -96,8 +98,8 @@
 
 
 def send_parts(stage, parts):
-    own = pick(parts, stage.digit)
-    sent = [pick(parts, stage.partner(stage.digit, step)) for step in range(1, stage.radix)]
+    own = pick(parts, stage, 0)
+    sent = [pick(parts, stage, step) for step in range(1, stage.radix)]
     return own, [stage.send(sent[step - 1], step) for step in range(1, stage.radix)]
 
 
@@ -110,17 +112,19 @@
     return jnp.concatenate(ordered(stage, value, received), axis=-1)
 
 
-def pad_rows(rows):
-    return jnp.pad(rows, ((0, -rows.shape[0] % 16), (0, 0)))
+def stack_rows(rows):
+    height = -(-len(rows) // 16) * 16
+    at = lax.broadcasted_iota(jnp.int32, (height, rows[0].shape[0]), 0)
+    out = jnp.zeros(at.shape, F32)
+    for i, row in enumerate(rows):
+        out = jnp.where(at == i, row[None, :], out)
+    return out.astype(BF16)
 
 
 def sum_rows(resid_sum, width):
-    size = resid_sum.shape[0]
-    fit = min(width, size)
-    rows = [
-        jnp.pad(row.reshape(-1, fit), ((0, 0), (0, width - fit))) for row in split_bf16(resid_sum, 3)
-    ]
-    return jnp.concatenate(rows, axis=0)
+    fit = min(width, resid_sum.shape[0])
+    rows = [term.reshape(-1, fit)[i] for term in split_bf16(resid_sum, 3) for i in range(resid_sum.shape[0] // fit)]
+    return [jnp.pad(row, (0, width - fit)) for row in rows]
 
 
 def read_sums(rows, width, size):
@@ -132,27 +136,27 @@
     size, width = partial.shape[0], partial.shape[1] // stage.radix
     parts = split_cols(partial, stage.radix)
     sums = sum_rows(resid_sum, width)
-    n_sum = sums.shape[0]
+    n_sum = len(sums)
     stat_parts = None if stats is None else split_cols(stats, stage.radix)
     rider_parts = None if riders is None else split_cols(riders, stage.radix)
     sent, arrived = [], []
     for step in range(1, stage.radix):
-        to = stage.partner(stage.digit, step)
         extra = sums
         if stats is not None:
-            extra = jnp.concatenate([sums] + split_bf16(pick(stat_parts, to), 2), axis=0)
-        message = [pick(parts, to).astype(BF16), pad_rows(extra)]
+            terms = split_bf16(pick(stat_parts, stage, step), 2)
+            extra = sums + [term[i] for term in terms for i in range(stats.shape[0])]
+        message = [pick(parts, stage, step).astype(BF16), stack_rows(extra)]
         n_extra = message[1].shape[0]
         if riders is not None:
-            message.append(pick(rider_parts, to))
+            message.append(pick(rider_parts, stage, step))
         sent.append(jnp.concatenate(message, axis=0))
         arrived.append(stage.send(sent[-1], step))
 
     def finish(gate=(), members=None):
-        partials, resid_sums, ridden = [pick(parts, stage.digit)], [resid_sum], []
+        partials, resid_sums, ridden = [pick(parts, stage, 0)], [resid_sum], []
         if stats is not None:
             n_stats = stats.shape[0]
-            members = [pick(stat_parts, stage.digit)]
+            members = [pick(stat_parts, stage, 0)]
         for message in arrived:
             message = after(message, *gate)
             partials.append(message[:size].astype(F32))
@@ -169,7 +173,7 @@
             total = total + (s - sum_mean)[:, None] * ((m[0] - count_mean) / samples)[None, :]
         merged = None
         if riders is not None:
-            merged = jnp.concatenate(ordered(stage, pick(rider_parts, stage.digit), ridden), axis=0)
+            merged = jnp.concatenate(ordered(stage, pick(rider_parts, stage, 0), ridden), axis=0)
         return (total, sum(resid_sums), merged), members
 
     return sent, finish
@@ -177,10 +181,8 @@
 
 def sum_stage(stage, partial):
     parts = split_cols(partial, stage.radix)
-    own = pick(parts, stage.digit)
-    sent = [
-        pick(parts, stage.partner(stage.digit, step)).astype(BF16) for step in range(1, stage.radix)
-    ]
+    own = pick(parts, stage, 0)
+    sent = [pick(parts, stage, step).astype(BF16) for step in range(1, stage.radix)]
     arrived = [stage.send(sent[step - 1], step) for step in range(1, stage.radix)]
 
     def finish(gate=()):
@@ -190,6 +192,7 @@
 
 
 TILES = 4
+BLOCK_LIMIT = 46
 GROUP = 64
 
 
@@ -215,30 +218,23 @@
     return counts, twos
 
 
-def head_kernel(
-    colors, genotypes, residual, coefficients, partial, stats, resid_sum, olds, blocks, resid, sems, resid_sem, old_sems
-):
+def head_kernel(colors, genotypes, residual, partial, stats, resid_sum, chosen, blocks, sems):
     samples, phenotypes = residual.shape
     width = BS // TILES
 
     def copy(r, t):
-        at = pl.multiple_of(colors[r, 0] * BS + t * width, width)
+        at = pl.multiple_of(colors[r] * BS + t * width, width)
         return pltpu.make_async_copy(
             genotypes.at[:, pl.ds(at, width)], blocks.at[r, :, pl.ds(t * width, width)], sems.at[r, t]
         )
 
-    def old_copy(r):
-        at = pl.multiple_of(colors[r, 0] * BS, BS)
-        return pltpu.make_async_copy(coefficients.at[:, pl.ds(at, BS)], olds.at[r], old_sems.at[r])
-
-    resid_copy = pltpu.make_async_copy(residual, resid, resid_sem)
-    resid_copy.start()
     for r in range(ROUNDS):
         for t in range(TILES):
             copy(r, t).start()
-        old_copy(r).start()
-    resid_copy.wait()
-    rounded = resid[...].astype(BF16)
+    chosen[...] = jnp.zeros_like(chosen)
+    for r in range(ROUNDS):
+        chosen[r : r + 1, :] = jnp.full((1, chosen.shape[1]), colors[r], jnp.int32)
+    rounded = residual[...].astype(BF16)
     sums = jnp.sum(rounded.astype(F32), axis=0, keepdims=True)
     resid_sum[...] = sums
     column = jnp.broadcast_to(jnp.transpose(jnp.broadcast_to(sums, (8, phenotypes)))[:, :1], (phenotypes, width))
@@ -255,37 +251,31 @@
                     rounded, values, (((0,), (0,)), ((), ())), preferred_element_type=F32
                 )
                 partial[:, here] = product - column * (counts * (1.0 / samples))
-        old_copy(r).wait()
-
-
-def head(colors, genotypes, residual, coefficients):
+
+
+def head(colors, genotypes, residual):
     samples, phenotypes = residual.shape
-    rows_own = coefficients.shape[0]
     whole = pl.BlockSpec(memory_space=pltpu.VMEM)
-    far = pl.BlockSpec(memory_space=pltpu.HBM)
     return pl.pallas_call(
         head_kernel,
         out_shape=[
             jax.ShapeDtypeStruct((phenotypes, BS), F32),
             jax.ShapeDtypeStruct((2 * ROUNDS, BS), F32),
             jax.ShapeDtypeStruct((1, phenotypes), F32),
-            jax.ShapeDtypeStruct((ROUNDS, rows_own, BS), F32),
+            jax.ShapeDtypeStruct((8, 128), jnp.int32),
         ],
-        in_specs=[pl.BlockSpec(memory_space=pltpu.SMEM), far, far, far],
+        in_specs=[pl.BlockSpec(memory_space=pltpu.SMEM), pl.BlockSpec(memory_space=pltpu.HBM), whole],
         out_specs=[whole] * 4,
         scratch_shapes=[
             pltpu.VMEM((ROUNDS, samples, BS), BF16),
-            pltpu.VMEM((samples, phenotypes), F32),
             pltpu.SemaphoreType.DMA((ROUNDS, TILES)),
-            pltpu.SemaphoreType.DMA,
-            pltpu.SemaphoreType.DMA((ROUNDS,)),
         ],
         cost_estimate=pl.CostEstimate(
             flops=4 * samples * phenotypes * BS, bytes_accessed=4 * samples * BS, transcendentals=0
         ),
         compiler_params=pltpu.CompilerParams(vmem_limit_bytes=50 * 1024 * 1024),
         name="head",
-    )(colors, genotypes, residual, coefficients)
+    )(colors, genotypes, residual)
 
 
 def over_var(value):
@@ -302,9 +292,33 @@
     return value, other
 
 
-def chosen_block(genotypes, block, gate):
-    genotypes = after(genotypes, gate)
-    return lax.optimization_barrier(lax.dynamic_slice_in_dim(genotypes, block * BS, BS, 1))
+def block_kernel(r, colors, genotypes, block, sems):
+    width = BS // TILES
+    copies = []
+    for t in range(TILES):
+        at = pl.multiple_of(colors[r] * BS + t * width, width)
+        copies.append(
+            pltpu.make_async_copy(
+                genotypes.at[:, pl.ds(at, width)], block.at[:, pl.ds(t * width, width)], sems.at[t]
+            )
+        )
+    for copy in copies:
+        copy.start()
+    for copy in copies:
+        copy.wait()
+
+
+def chosen_block(colors, genotypes, r, gate):
+    samples = genotypes.shape[0]
+    return pl.pallas_call(
+        functools.partial(block_kernel, r),
+        out_shape=jax.ShapeDtypeStruct((samples, BS), BF16),
+        in_specs=[pl.BlockSpec(memory_space=pltpu.SMEM), pl.BlockSpec(memory_space=pltpu.HBM)],
+        out_specs=pl.BlockSpec(memory_space=pltpu.VMEM),
+        scratch_shapes=[pltpu.SemaphoreType.DMA((TILES,))],
+        cost_estimate=pl.CostEstimate(flops=10**9, bytes_accessed=2 * samples * BS, transcendentals=0),
+        compiler_params=pltpu.CompilerParams(vmem_limit_bytes=BLOCK_LIMIT * 1024 * 1024),
+    )(after(colors, gate), genotypes)
 
 
 def descent(genotypes, residual, coefficients, penalty, colors):
@@ -318,23 +332,43 @@
     top = len(early) - 1
     chunks = 2 if phenotypes % 256 == 0 else 1
     size = phenotypes // chunks
-    chosen = colors[:, 0]
-
-    partial, stats, resid_sum, olds = head(colors, genotypes, residual, coefficients)
+    n_blocks = genotypes.shape[1] // BS
+    colors = colors[:, 0]
+
+    first = jnp.int32(0)
+    for stage in all_stages:
+        digit = sum(d * mine.astype(jnp.int32) for d, mine in enumerate(stage.mine))
+        first = first * stage.radix + digit
+    first = [(first * width + block * BS).astype(jnp.uint32) for block in range(n_blocks)]
+    mine = [stage.mine for stage in all_stages]
+    genotypes, first, mine = lax.optimization_barrier((genotypes, first, mine))
+    for stage, flags in zip(all_stages, mine):
+        stage.mine = flags
+
+    partial, stats, resid_sum, chosen = head(colors, genotypes, residual)
     partial_chunks = [partial[c * size : (c + 1) * size] for c in range(chunks)]
     sum_chunks = [resid_sum[0, c * size : (c + 1) * size] for c in range(chunks)]
-    values = []
-
-    first = jnp.int32(0)
-    for stage in all_stages:
-        first = first * stage.radix + stage.digit
-    first = first * width
+    chosen = [chosen[r : r + 1, :1] for r in range(ROUNDS)]
+
+    def of_block(array, r):
+        parts = split_cols(array, n_blocks)
+        value = parts[0]
+        for block in range(1, n_blocks):
+            value = jnp.where(chosen[r] == block, parts[block], value)
+        return value
+
+    olds = [of_block(coefficients, r) for r in range(ROUNDS)]
 
     def weights(r, gate):
-        part = lax.dynamic_slice_in_dim(after(penalty, gate), chosen[r] * BS + first, width, 0)
-        return lax.optimization_barrier(part)
-
-    riders = [None] * (chunks - 1) + [jnp.concatenate(split_bf16(olds[0], 2), axis=0)]
+        held = after(penalty, gate)
+        parts = [lax.dynamic_slice(held, (at,), (width,)) for at in first]
+        parts = lax.optimization_barrier(parts)
+        value = parts[0][None, :]
+        for block in range(1, n_blocks):
+            value = jnp.where(chosen[r] == block, parts[block][None, :], value)
+        return value[0]
+
+    riders = [None] * (chunks - 1) + [jnp.concatenate(split_bf16(olds[0], 2), axis=0).astype(BF16)]
     states = list(zip(partial_chunks, sum_chunks, riders))
     moments, samples = stats, local_samples
     sent_top, end_top, ends, members, gate = [], [], [], [None] * len(all_stages), ()
@@ -365,7 +399,7 @@
     old = jnp.sum(riders.astype(F32).reshape(samp, 2, rows_own, width), axis=1).reshape(phenotypes, width)
     ahead = sent_top[-1]
     weight = weights(0, ahead[0])
-    values = [None] + [chosen_block(genotypes, chosen[r], ahead[0]) for r in range(1, ROUNDS)]
+    values = [None] + [chosen_block(colors, genotypes, r, ahead[0]) for r in range(1, ROUNDS)]
     old_later = jnp.stack([after(olds[r], *ahead) for r in range(1, ROUNDS)])
     for i in range(top):
         parts = send_parts(early[i], split_cols(old_later, early[i].radix))
@@ -412,12 +446,11 @@
         news.append(new)
         change = (new - old).astype(BF16)
         means_sent = [mean] if r else [moments[2 * i] / total_samples for i in range(ROUNDS)]
-        rows = [row[None, :] for sent in means_sent for row in split_bf16(sent, 3)]
-        rows = pad_rows(jnp.concatenate(rows, axis=0))
+        rows = stack_rows([row for sent in means_sent for row in split_bf16(sent, 3)])
         lead = rows.shape[0]
         message = jnp.concatenate([rows, change], axis=0)
         if r == 0:
-            values[0] = chosen_block(genotypes, chosen[0], message)
+            values[0] = chosen_block(colors, genotypes, 0, message)
             old_parts = send_parts(early[top], split_cols(old_later, early[top].radix))
         gathered = gather_stage(message, last)
         cuts = [0] + [lead + size * (c + 1) for c in range(chunks)]
@@ -467,7 +500,7 @@
     home = home.reshape(samp, ROUNDS, rows_own, width)
     new_rows = [jnp.concatenate([home[s, r] for s in range(samp)], axis=-1) for r in range(ROUNDS)]
     out = []
-    for block in range(genotypes.shape[1] // BS):
+    for block in range(n_blocks):
         piece = coefficients[:, block * BS : (block + 1) * BS]
         for r in range(ROUNDS):
             piece = jnp.where(chosen[r] == block, new_rows[r], piece)

time: 156 us -> 156 us (level)
  local copies, waits for them, and re-layouts: 13.8 us -> 4.3 us
  waiting for transfers between devices: 53 us -> 59.8 us
  Pallas kernels: 5.52 us -> 11.2 us
  other arithmetic: 11 us -> 7.49 us
  starting transfers between devices: 55.2 us -> 57.2 us
    ppermute x44, waiting for transfers between devices: 28.7 us -> 36.3 us  [send(): return lax.ppermute(value, 'samp', self.pairs(step))]
    pallas_call x0 -> x2, Pallas kernels: none -> 5.7 us  [chosen_block(): pl.pallas_call(functools.partial(block_kernel, r), out_shape=jax.ShapeDty...]
    dynamic_slice x4 -> x2, local copies, waits for them, and re-layouts: 7.16 us -> 1.59 us  [weights(): parts = [lax.dynamic_slice(held, (at,), (width,)) for at in first]]
    add x6, other arithmetic: 2.77 us -> 0.92 us  [finish(): total + (s - sum_mean)[:, None] * ((m[0] - count_mean) / samples)[None, :]]
    ppermute x44, starting transfers between devices: 50 us -> 51.8 us  [send(): return lax.ppermute(value, 'samp', self.pairs(step))]
  transfers between devices with their start and end apart: 48 -> 48, of which waited for: 21 -> 24; matrix products, arithmetic and copies ran while one was open for 16% -> 10% of each run, Pallas kernels for 0% -> 4%
where the time goes in v3:
time: 156 us; the launch traced here: 155 us
  waiting for transfers between devices  59.8 us (38%)
  starting transfers between devices  57.2 us (37%)
  Pallas kernels  11.2 us (7%)
  matrix products  9.34 us (6%)
  other arithmetic  7.49 us (5%)
  between operations  6.13 us (4%)
  local copies, waits for them, and re-layouts  4.3 us (3%)
    ppermute x44, starting transfers between devices, send(): return lax.ppermute(value, 'samp', self.pairs(step))  51.8 us
    ppermute x44, waiting for transfers between devices, send(): return lax.ppermute(value, 'samp', self.pairs(step))  36.3 us
    ppermute x4, waiting for transfers between devices, over_var(): lax.ppermute(value.astype(BF16), 'var', [(i, i ^ step) for i in range(siz...  23.5 us
    dot_general x4, matrix products, descent(): lax.dot_general(values[r], piece, (((1,), (1,)), ((), ())), preferred_ele...  5.95 us
    pallas_call x2, Pallas kernels, chosen_block(): pl.pallas_call(functools.partial(block_kernel, r), out_shape=jax.ShapeDty...  5.7 us
    pallas_call x1, Pallas kernels, head(): pl.pallas_call(head_kernel, out_shape=[jax.ShapeDtypeStruct((phenotypes,...  5.5 us
    ppermute x4, starting transfers between devices, over_var(): lax.ppermute(value.astype(BF16), 'var', [(i, i ^ step) for i in range(siz...  5.43 us
  transfers between devices with their start and end apart: 48, of which 24 were waited for; matrix products, arithmetic and copies ran while one was open for 10% of the time, Pallas kernels for 4%

profile of v3, /device:TPU:0, one launch (start us, length us, event | category | flops | bytes accessed | tf_op | source)
XLA Modules:
  0.0 155.4 jit_solution(987449235784639195)
XLA Ops:
  0.9 1.2 copy-done
  2.1 0.7 copy-done.2
  2.8 5.5 %head.1 = (f32[256,2048]{1,0:T(8,128)S(1)}, f32[4,2048]{1,0:T(4,128)S(1)}, f32[1,256]{1,0:T(1,128)S(1)}, s32[8,128]{1,0:T(8,128)S(1)}) custom-call(s32[2]{0:T(128)S(1)} %bitcast.436, bf16[1080,4096]{1,0:T(8,128)(2,1)} %genotypes.2, f32[1080,256]{1,0:T(8,128)S(1)} %copy-done), custom_call_target="tpu_custom_call" | custom-call | flops 2264924160 | bytes 8847360 | tf_op jit(solution)/shard_map/head/pallas_call | solution.py:259
  11.9 3.0 %collective-permute-start.2 = (bf16[144,512]{1,0:T(8,128)(2,1)S(1)}, bf16[144,512]{1,0:T(8,128)(2,1)S(1)}, u32[]{:S(2)}, u32[]{:S(2)}) collective-permute-start(bf16[144,512]{1,0:T(8,128)(2,1)S(1)} %pad_maximum_fusion.20), channel_id=1, source_target_pairs={{0,4},{2,6},{4,0},{6,2},{8,12},{10,14},{12,8},{14,10},{16,20},{18,... | collective-permute-start | bytes 442376 | tf_op jit(solution)/shard_map/ppermute | solution.py:50
  15.4 0.7 collective-permute-start.4
  16.2 0.8 fusion.83
  17.0 2.7 %collective-permute-done.2 = bf16[144,512]{1,0:T(8,128)(2,1)S(1)} collective-permute-done((bf16[144,512]{1,0:T(8,128)(2,1)S(1)}, bf16[144,512]{1,0:T(8,128)(2,1)S(1)}, u32[]{:S(2)}, u32[]{:S(2)}) %collective-permute-start.2) | collective-permute-done | bytes 147488 | tf_op jit(solution)/shard_map/ppermute | solution.py:50
  20.2 3.2 %collective-permute-start.5 = (bf16[144,128]{1,0:T(8,128)(2,1)S(1)}, bf16[144,128]{1,0:T(8,128)(2,1)S(1)}, u32[]{:S(2)}, u32[]{:S(2)}) collective-permute-start(bf16[144,128]{1,0:T(8,128)(2,1)S(1)} %pad_maximum_fusion.38), channel_id=1, source_target_pairs={{0,16},{2,18},{4,20},{6,22},{8,24},{10,26},{12,28},{14,30},{16,0},... | collective-permute-start | bytes 110600 | tf_op jit(solution)/shard_map/ppermute | solution.py:50
  23.5 1.6 %collective-permute-start.3 = (bf16[144,128]{1,0:T(8,128)(2,1)S(1)}, bf16[144,128]{1,0:T(8,128)(2,1)S(1)}, u32[]{:S(2)}, u32[]{:S(2)}) collective-permute-start(bf16[144,128]{1,0:T(8,128)(2,1)S(1)} %pad_maximum_fusion.37), channel_id=1, source_target_pairs={{0,8},{2,10},{4,12},{6,14},{8,0},{10,2},{12,4},{14,6},{16,24},{18,... | collective-permute-start | bytes 110600 | tf_op jit(solution)/shard_map/ppermute | solution.py:50
  25.7 2.2 %collective-permute-done.3 = bf16[144,128]{1,0:T(8,128)(2,1)S(1)} collective-permute-done((bf16[144,128]{1,0:T(8,128)(2,1)S(1)}, bf16[144,128]{1,0:T(8,128)(2,1)S(1)}, u32[]{:S(2)}, u32[]{:S(2)}) %collective-permute-start.3) | collective-permute-done | bytes 36896 | tf_op jit(solution)/shard_map/ppermute | solution.py:50
  27.9 3.1 %collective-permute-done.6 = bf16[144,128]{1,0:T(8,128)(2,1)S(1)} collective-permute-done((bf16[144,128]{1,0:T(8,128)(2,1)S(1)}, bf16[144,128]{1,0:T(8,128)(2,1)S(1)}, u32[]{:S(2)}, u32[]{:S(2)}) %collective-permute-start.6) | collective-permute-done | bytes 36896 | tf_op jit(solution)/shard_map/ppermute | solution.py:50
  32.0 3.9 %collective-permute-start.9 = (bf16[272,128]{1,0:T(8,128)(2,1)S(1)}, bf16[272,128]{1,0:T(8,128)(2,1)S(1)}, u32[]{:S(2)}, u32[]{:S(2)}) collective-permute-start(bf16[272,128]{1,0:T(8,128)(2,1)S(1)} %get-tuple-element.299), channel_id=1, source_target_pairs={{0,8},{2,10},{4,12},{6,14},{8,0},{10,2},{12,4},{14,6},{16,24},{18,... | collective-permute-start | bytes 208904 | tf_op jit(solution)/shard_map/ppermute | solution.py:50
  35.9 1.4 collective-permute-done.7
  37.4 1.1 collective-permute-done.8
  38.5 1.1 collective-permute-done.9
  40.0 1.2 collective-permute-start.12
  41.2 1.7 %collective-permute-start.11 = (bf16[272,128]{1,0:T(8,128)(2,1)S(1)}, bf16[272,128]{1,0:T(8,128)(2,1)S(1)}, u32[]{:S(2)}, u32[]{:S(2)}) collective-permute-start(bf16[272,128]{1,0:T(8,128)(2,1)S(1)} %pad_maximum_fusion.31), channel_id=1, source_target_pairs={{0,16},{2,18},{4,20},{6,22},{8,24},{10,26},{12,28},{14,30},{16,0},... | collective-permute-start | bytes 208904 | tf_op jit(solution)/shard_map/ppermute | solution.py:50
  43.0 1.5 collective-permute-start.10
  47.2 1.9 %collective-permute-done.10 = bf16[272,128]{1,0:T(8,128)(2,1)S(1)} collective-permute-done((bf16[272,128]{1,0:T(8,128)(2,1)S(1)}, bf16[272,128]{1,0:T(8,128)(2,1)S(1)}, u32[]{:S(2)}, u32[]{:S(2)}) %collective-permute-start.10) | collective-permute-done | bytes 69664 | tf_op jit(solution)/shard_map/ppermute | solution.py:50
  49.2 1.6 %collective-permute-start.14 = (bf16[144,512]{1,0:T(8,128)(2,1)S(1)}, bf16[144,512]{1,0:T(8,128)(2,1)S(1)}, u32[]{:S(2)}, u32[]{:S(2)}) collective-permute-start(bf16[144,512]{1,0:T(8,128)(2,1)S(1)} %pad_maximum_fusion.17), channel_id=1, source_target_pairs={{0,4},{2,6},{4,0},{6,2},{8,12},{10,14},{12,8},{14,10},{16,20},{18,... | collective-permute-start | bytes 442376 | tf_op jit(solution)/shard_map/ppermute | solution.py:50
  50.9 3.6 %collective-permute-done.14 = bf16[144,512]{1,0:T(8,128)(2,1)S(1)} collective-permute-done((bf16[144,512]{1,0:T(8,128)(2,1)S(1)}, bf16[144,512]{1,0:T(8,128)(2,1)S(1)}, u32[]{:S(2)}, u32[]{:S(2)}) %collective-permute-start.14) | collective-permute-done | bytes 147488 | tf_op jit(solution)/shard_map/ppermute | solution.py:50
  54.6 2.8 %shard_map.69 = bf16[1080,2048]{1,0:T(8,128)(2,1)S(1)} custom-call(s32[2]{0:T(128)S(1)} %bitcast.437, bf16[1080,4096]{1,0:T(8,128)(2,1)} %genotypes.2), custom_call_target="tpu_custom_call" | custom-call | flops 1000000000 | bytes 4423680 | tf_op jit(solution)/shard_map/pallas_call | solution.py:313
  57.4 2.8 %shard_map.68 = bf16[1080,2048]{1,0:T(8,128)(2,1)S(1)} custom-call(s32[2]{0:T(128)S(1)} %bitcast.438, bf16[1080,4096]{1,0:T(8,128)(2,1)} %genotypes.2), custom_call_target="tpu_custom_call" | custom-call | flops 1000000000 | bytes 4423680 | tf_op jit(solution)/shard_map/pallas_call | solution.py:313
  60.3 1.6 %collective-permute-start.13 = (bf16[128,512]{1,0:T(8,128)(2,1)S(1)}, bf16[128,512]{1,0:T(8,128)(2,1)S(1)}, u32[]{:S(2)}, u32[]{:S(2)}) collective-permute-start(bf16[128,512]{1,0:T(8,128)(2,1)S(1)} %pad_maximum_fusion.23), channel_id=1, source_target_pairs={{0,4},{2,6},{4,0},{6,2},{8,12},{10,14},{12,8},{14,10},{16,20},{18,... | collective-permute-start | bytes 393224 | tf_op jit(solution)/shard_map/ppermute | solution.py:50
  62.3 1.4 fusion.92
  63.7 2.6 %collective-permute-done.13 = bf16[128,512]{1,0:T(8,128)(2,1)S(1)} collective-permute-done((bf16[128,512]{1,0:T(8,128)(2,1)S(1)}, bf16[128,512]{1,0:T(8,128)(2,1)S(1)}, u32[]{:S(2)}, u32[]{:S(2)}) %collective-permute-start.13) | collective-permute-done | bytes 131104 | tf_op jit(solution)/shard_map/ppermute | solution.py:50
  66.4 1.6 %collective-permute-start.18 = (bf16[1080,128]{1,0:T(8,128)(2,1)S(1)}, bf16[1080,128]{1,0:T(8,128)(2,1)S(1)}, u32[]{:S(2)}, u32[]{:S(2)}) collective-permute-start(bf16[1080,128]{1,0:T(8,128)(2,1)S(1)} %get-tuple-element.361), channel_id=1, source_target_pairs={{0,1},{1,0},{2,3},{3,2},{4,5},{5,4},{6,7},{7,6},{8,9},{9,8},{10,11... | collective-permute-start | bytes 829448 | tf_op jit(solution)/shard_map/ppermute | solution.py:289
  68.0 1.6 %collective-permute-start.22 = (f32[1,32,512]{2,1,0:T(8,128)S(1)}, f32[1,32,512]{2,1,0:T(8,128)S(1)}, u32[]{:S(2)}, u32[]{:S(2)}) collective-permute-start(f32[1,32,512]{2,1,0:T(8,128)S(1)} %broadcast_select_fusion.29), channel_id=1, source_target_pairs={{0,4},{2,6},{4,0},{6,2},{8,12},{10,14},{12,8},{14,10},{16,20},{18,... | collective-permute-start | bytes 196616 | tf_op jit(solution)/shard_map/ppermute | solution.py:50
  70.0 5.5 %collective-permute-done.18 = bf16[1080,128]{1,0:T(8,128)(2,1)S(1)} collective-permute-done((bf16[1080,128]{1,0:T(8,128)(2,1)S(1)}, bf16[1080,128]{1,0:T(8,128)(2,1)S(1)}, u32[]{:S(2)}, u32[]{:S(2)}) %collective-permute-start.18) | collective-permute-done | bytes 276512 | tf_op jit(solution)/shard_map/ppermute | solution.py:289
  75.7 1.2 convolution_subtract_fusion.5
  77.1 1.6 %fusion.91 = (bf16[1080,128]{1,0:T(8,128)(2,1)S(1)}, f32[1080,128]{1,0:T(8,128)S(1)}) fusion(f32[128]{0:T(128)S(1)} %convolution_reduce_fusion.2, bf16[1080,2048]{1,0:T(8,128)(2,1)S(1)} %shard_map.68, bf16[128,1024]{1,0:T(8,128)(2,1)S(1)} %get-tuple-element.169, bf16[128,1024]{1,0:T(8,128)(2,1)S(1)} %get-tuple-element.168), kind=kOutput, calls=%fused_computation.492 | convolution fusion | flops 567556096 | bytes 5777920 | tf_op jit(solution)/shard_map/dot_general | solution.py:476
  78.7 1.6 %collective-permute-start.17 = (bf16[1080,128]{1,0:T(8,128)(2,1)S(1)}, bf16[1080,128]{1,0:T(8,128)(2,1)S(1)}, u32[]{:S(2)}, u32[]{:S(2)}) collective-permute-start(bf16[1080,128]{1,0:T(8,128)(2,1)S(1)} %get-tuple-element.359), channel_id=1, source_target_pairs={{0,1},{1,0},{2,3},{3,2},{4,5},{5,4},{6,7},{7,6},{8,9},{9,8},{10,11... | collective-permute-start | bytes 829448 | tf_op jit(solution)/shard_map/ppermute | solution.py:289
  80.5 7.3 %collective-permute-done.17 = bf16[1080,128]{1,0:T(8,128)(2,1)S(1)} collective-permute-done((bf16[1080,128]{1,0:T(8,128)(2,1)S(1)}, bf16[1080,128]{1,0:T(8,128)(2,1)S(1)}, u32[]{:S(2)}, u32[]{:S(2)}) %collective-permute-start.17) | collective-permute-done | bytes 276512 | tf_op jit(solution)/shard_map/ppermute | solution.py:289
  88.0 1.2 convolution_subtract_fusion.4
  89.4 1.6 %collective-permute-start.23 = (f32[1,64,128]{2,1,0:T(8,128)S(1)}, f32[1,64,128]{2,1,0:T(8,128)S(1)}, u32[]{:S(2)}, u32[]{:S(2)}) collective-permute-start(f32[1,64,128]{2,1,0:T(8,128)S(1)} %get-tuple-element.105), channel_id=1, source_target_pairs={{0,24},{2,26},{4,28},{6,30},{8,16},{10,18},{12,20},{14,22},{16,8},... | collective-permute-start | bytes 98312 | tf_op jit(solution)/shard_map/ppermute | solution.py:50
  91.1 2.9 %collective-permute-start.24 = (f32[1,64,128]{2,1,0:T(8,128)S(1)}, f32[1,64,128]{2,1,0:T(8,128)S(1)}, u32[]{:S(2)}, u32[]{:S(2)}) collective-permute-start(f32[1,64,128]{2,1,0:T(8,128)S(1)} %get-tuple-element.260), channel_id=1, source_target_pairs={{0,16},{2,18},{4,20},{6,22},{8,24},{10,26},{12,28},{14,30},{16,0},... | collective-permute-start | bytes 98312 | tf_op jit(solution)/shard_map/ppermute | solution.py:50
  93.9 1.5 collective-permute-start.26
  96.2 4.1 %collective-permute-done.26 = bf16[128,512]{1,0:T(8,128)(2,1)S(1)} collective-permute-done((bf16[128,512]{1,0:T(8,128)(2,1)S(1)}, bf16[128,512]{1,0:T(8,128)(2,1)S(1)}, u32[]{:S(2)}, u32[]{:S(2)}) %collective-permute-start.26) | collective-permute-done | bytes 131104 | tf_op jit(solution)/shard_map/ppermute | solution.py:50
  100.5 0.8 fusion.82
  101.3 1.5 collective-permute-start.30
  102.8 2.9 %collective-permute-start.29 = (bf16[128,128]{1,0:T(8,128)(2,1)S(1)}, bf16[128,128]{1,0:T(8,128)(2,1)S(1)}, u32[]{:S(2)}, u32[]{:S(2)}) collective-permute-start(bf16[128,128]{1,0:T(8,128)(2,1)S(1)} %get-tuple-element.237), channel_id=1, source_target_pairs={{0,16},{2,18},{4,20},{6,22},{8,24},{10,26},{12,28},{14,30},{16,0},... | collective-permute-start | bytes 98312 | tf_op jit(solution)/shard_map/ppermute | solution.py:50
  105.9 2.0 %collective-permute-start.31 = (bf16[128,128]{1,0:T(8,128)(2,1)S(1)}, bf16[128,128]{1,0:T(8,128)(2,1)S(1)}, u32[]{:S(2)}, u32[]{:S(2)}) collective-permute-start(bf16[128,128]{1,0:T(8,128)(2,1)S(1)} %get-tuple-element.233), channel_id=1, source_target_pairs={{0,8},{2,10},{4,12},{6,14},{8,0},{10,2},{12,4},{14,6},{16,24},{18,... | collective-permute-start | bytes 98312 | tf_op jit(solution)/shard_map/ppermute | solution.py:50
  107.9 2.3 %collective-permute-start.33 = (bf16[128,128]{1,0:T(8,128)(2,1)S(1)}, bf16[128,128]{1,0:T(8,128)(2,1)S(1)}, u32[]{:S(2)}, u32[]{:S(2)}) collective-permute-start(bf16[128,128]{1,0:T(8,128)(2,1)S(1)} %get-tuple-element.234), channel_id=1, source_target_pairs={{0,24},{2,26},{4,28},{6,30},{8,16},{10,18},{12,20},{14,22},{16,8},... | collective-permute-start | bytes 98312 | tf_op jit(solution)/shard_map/ppermute | solution.py:50
  110.7 3.1 %collective-permute-done.33 = bf16[128,128]{1,0:T(8,128)(2,1)S(1)} collective-permute-done((bf16[128,128]{1,0:T(8,128)(2,1)S(1)}, bf16[128,128]{1,0:T(8,128)(2,1)S(1)}, u32[]{:S(2)}, u32[]{:S(2)}) %collective-permute-start.33) | collective-permute-done | bytes 32800 | tf_op jit(solution)/shard_map/ppermute | solution.py:50
  114.0 2.9 %collective-permute-start.40 = (bf16[272,128]{1,0:T(8,128)(2,1)S(1)}, bf16[272,128]{1,0:T(8,128)(2,1)S(1)}, u32[]{:S(2)}, u32[]{:S(2)}) collective-permute-start(bf16[272,128]{1,0:T(8,128)(2,1)S(1)} %pad_maximum_fusion.32), channel_id=1, source_target_pairs={{0,16},{2,18},{4,20},{6,22},{8,24},{10,26},{12,28},{14,30},{16,0},... | collective-permute-start | bytes 208904 | tf_op jit(solution)/shard_map/ppermute | solution.py:50
  117.0 1.4 collective-permute-start.39
  118.5 1.6 %collective-permute-start.34 = (f32[4,2,2,16,128]{4,3,1,0,2:T(8,128)S(1)}, f32[4,2,2,16,128]{4,3,1,0,2:T(8,128)S(1)}, u32[]{:S(2)}, u32[]{:S(2)}) collective-permute-start(f32[4,2,2,16,128]{4,3,1,0,2:T(8,128)S(1)} %fusion.8), channel_id=1, source_target_pairs={{0,4},{2,6},{4,0},{6,2},{8,12},{10,14},{12,8},{14,10},{16,20},{18,... | collective-permute-start | bytes 393224 | tf_op jit(solution)/shard_map/ppermute | solution.py:50
  120.1 3.8 %collective-permute-done.39 = bf16[272,128]{1,0:T(8,128)(2,1)S(1)} collective-permute-done((bf16[272,128]{1,0:T(8,128)(2,1)S(1)}, bf16[272,128]{1,0:T(8,128)(2,1)S(1)}, u32[]{:S(2)}, u32[]{:S(2)}) %collective-permute-start.39) | collective-permute-done | bytes 69664 | tf_op jit(solution)/shard_map/ppermute | solution.py:50
  124.0 1.0 collective-permute-start.45
  125.1 2.0 %collective-permute-start.35 = (f32[2,2,2,16,128]{4,3,1,2,0:T(8,128)S(1)}, f32[2,2,2,16,128]{4,3,1,2,0:T(8,128)S(1)}, u32[]{:S(2)}, u32[]{:S(2)}) collective-permute-start(f32[2,2,2,16,128]{4,3,1,2,0:T(8,128)S(1)} %get-tuple-element.96), channel_id=1, source_target_pairs={{0,24},{2,26},{4,28},{6,30},{8,16},{10,18},{12,20},{14,22},{16,8},... | collective-permute-start | bytes 196616 | tf_op jit(solution)/shard_map/ppermute | solution.py:50
  127.1 1.2 collective-permute-start.37
  128.3 1.3 collective-permute-start.36
  129.7 1.2 collective-permute-start.42
  131.3 0.7 collective-permute-done.37
  131.9 2.3 %collective-permute-done.36 = f32[2,2,2,16,128]{4,3,1,2,0:T(8,128)S(1)} collective-permute-done((f32[2,2,2,16,128]{4,3,1,2,0:T(8,128)S(1)}, f32[2,2,2,16,128]{4,3,1,2,0:T(8,128)S(1)}, u32[]{:S(2)}, u32[]{:S(2)}) %collective-permute-start.36) | collective-permute-done | bytes 65568 | tf_op jit(solution)/shard_map/ppermute | solution.py:50
  135.0 0.7 collective-permute-done.38
  137.0 1.4 fusion.94
  138.7 0.7 pad_maximum_fusion.14
  139.4 1.5 collective-permute-start.44
  141.3 1.4 fusion.93
  142.8 0.7 collective-permute-start.47
  143.5 5.4 %collective-permute-done.44 = bf16[1080,128]{1,0:T(8,128)(2,1)S(1)} collective-permute-done((bf16[1080,128]{1,0:T(8,128)(2,1)S(1)}, bf16[1080,128]{1,0:T(8,128)(2,1)S(1)}, u32[]{:S(2)}, u32[]{:S(2)}) %collective-permute-start.44) | collective-permute-done | bytes 276512 | tf_op jit(solution)/shard_map/ppermute | solution.py:289
  149.0 5.2 %collective-permute-done.47 = bf16[1080,128]{1,0:T(8,128)(2,1)S(1)} collective-permute-done((bf16[1080,128]{1,0:T(8,128)(2,1)S(1)}, bf16[1080,128]{1,0:T(8,128)(2,1)S(1)}, u32[]{:S(2)}, u32[]{:S(2)}) %collective-permute-start.47) | collective-permute-done | bytes 276512 | tf_op jit(solution)/shard_map/ppermute | solution.py:289
  154.4 1.1 pad_maximum_fusion
  (268 shorter events, 12.4 us)
Async XLA Ops:
  0.9 1.2 copy-start
  2.1 0.7 copy-start.2
  2.8 8.3 %copy-start.4 = (f32[16,4096]{1,0:T(8,128)S(1)}, f32[16,4096]{1,0:T(8,128)}, u32[]{:S(2)}) copy-start(f32[16,4096]{1,0:T(8,128)} %param.7) | copy-start | bytes 786436
  8.6 2.7 %collective-permute-start.1 = (bf16[144,1024]{1,0:T(8,128)(2,1)S(1)}, bf16[144,1024]{1,0:T(8,128)(2,1)S(1)}, u32[]{:S(2)}, u32[]{:S(2)}) collective-permute-start(bf16[144,1024]{1,0:T(8,128)(2,1)S(1)} %pad_maximum_fusion.8), channel_id=1, source_target_pairs={{0,2},{2,0},{4,6},{6,4},{8,10},{10,8},{12,14},{14,12},{16,18},{18,... | collective-permute-start | bytes 884744 | tf_op jit(solution)/shard_map/ppermute | solution.py:50
  11.2 3.7 %collective-permute-start = (bf16[176,1024]{1,0:T(8,128)(2,1)S(1)}, bf16[176,1024]{1,0:T(8,128)(2,1)S(1)}, u32[]{:S(2)}, u32[]{:S(2)}) collective-permute-start(bf16[176,1024]{1,0:T(8,128)(2,1)S(1)} %pad_maximum_fusion.3), channel_id=1, source_target_pairs={{0,2},{2,0},{4,6},{6,4},{8,10},{10,8},{12,14},{14,12},{16,18},{18,... | collective-permute-start | bytes 1081352 | tf_op jit(solution)/shard_map/ppermute | solution.py:50
  11.9 7.7 %collective-permute-start.2 = (bf16[144,512]{1,0:T(8,128)(2,1)S(1)}, bf16[144,512]{1,0:T(8,128)(2,1)S(1)}, u32[]{:S(2)}, u32[]{:S(2)}) collective-permute-start(bf16[144,512]{1,0:T(8,128)(2,1)S(1)} %pad_maximum_fusion.20), channel_id=1, source_target_pairs={{0,4},{2,6},{4,0},{6,2},{8,12},{10,14},{12,8},{14,10},{16,20},{18,... | collective-permute-start | bytes 442376 | tf_op jit(solution)/shard_map/ppermute | solution.py:50
  15.4 9.9 %collective-permute-start.4 = (bf16[208,512]{1,0:T(8,128)(2,1)S(1)}, bf16[208,512]{1,0:T(8,128)(2,1)S(1)}, u32[]{:S(2)}, u32[]{:S(2)}) collective-permute-start(bf16[208,512]{1,0:T(8,128)(2,1)S(1)} %pad_maximum_fusion.16), channel_id=1, source_target_pairs={{0,4},{2,6},{4,0},{6,2},{8,12},{10,14},{12,8},{14,10},{16,20},{18,... | collective-permute-start | bytes 638984 | tf_op jit(solution)/shard_map/ppermute | solution.py:50
  20.2 7.7 %collective-permute-start.5 = (bf16[144,128]{1,0:T(8,128)(2,1)S(1)}, bf16[144,128]{1,0:T(8,128)(2,1)S(1)}, u32[]{:S(2)}, u32[]{:S(2)}) collective-permute-start(bf16[144,128]{1,0:T(8,128)(2,1)S(1)} %pad_maximum_fusion.38), channel_id=1, source_target_pairs={{0,16},{2,18},{4,20},{6,22},{8,24},{10,26},{12,28},{14,30},{16,0},... | collective-permute-start | bytes 110600 | tf_op jit(solution)/shard_map/ppermute | solution.py:50
  23.5 4.4 %collective-permute-start.3 = (bf16[144,128]{1,0:T(8,128)(2,1)S(1)}, bf16[144,128]{1,0:T(8,128)(2,1)S(1)}, u32[]{:S(2)}, u32[]{:S(2)}) collective-permute-start(bf16[144,128]{1,0:T(8,128)(2,1)S(1)} %pad_maximum_fusion.37), channel_id=1, source_target_pairs={{0,8},{2,10},{4,12},{6,14},{8,0},{10,2},{12,4},{14,6},{16,24},{18,... | collective-permute-start | bytes 110600 | tf_op jit(solution)/shard_map/ppermute | solution.py:50
  25.2 5.8 %collective-permute-start.6 = (bf16[144,128]{1,0:T(8,128)(2,1)S(1)}, bf16[144,128]{1,0:T(8,128)(2,1)S(1)}, u32[]{:S(2)}, u32[]{:S(2)}) collective-permute-start(bf16[144,128]{1,0:T(8,128)(2,1)S(1)} %pad_maximum_fusion.39), channel_id=1, source_target_pairs={{0,24},{2,26},{4,28},{6,30},{8,16},{10,18},{12,20},{14,22},{16,8},... | collective-permute-start | bytes 110600 | tf_op jit(solution)/shard_map/ppermute | solution.py:50
  31.1 6.3 %collective-permute-start.7 = (bf16[272,128]{1,0:T(8,128)(2,1)S(1)}, bf16[272,128]{1,0:T(8,128)(2,1)S(1)}, u32[]{:S(2)}, u32[]{:S(2)}) collective-permute-start(bf16[272,128]{1,0:T(8,128)(2,1)S(1)} %get-tuple-element.297), channel_id=1, source_target_pairs={{0,24},{2,26},{4,28},{6,30},{8,16},{10,18},{12,20},{14,22},{16,8},... | collective-permute-start | bytes 208904 | tf_op jit(solution)/shard_map/ppermute | solution.py:50
  31.8 6.7 %collective-permute-start.8 = (bf16[272,128]{1,0:T(8,128)(2,1)S(1)}, bf16[272,128]{1,0:T(8,128)(2,1)S(1)}, u32[]{:S(2)}, u32[]{:S(2)}) collective-permute-start(bf16[272,128]{1,0:T(8,128)(2,1)S(1)} %get-tuple-element.298), channel_id=1, source_target_pairs={{0,16},{2,18},{4,20},{6,22},{8,24},{10,26},{12,28},{14,30},{16,0},... | collective-permute-start | bytes 208904 | tf_op jit(solution)/shard_map/ppermute | solution.py:50
  32.0 7.6 %collective-permute-start.9 = (bf16[272,128]{1,0:T(8,128)(2,1)S(1)}, bf16[272,128]{1,0:T(8,128)(2,1)S(1)}, u32[]{:S(2)}, u32[]{:S(2)}) collective-permute-start(bf16[272,128]{1,0:T(8,128)(2,1)S(1)} %get-tuple-element.299), channel_id=1, source_target_pairs={{0,8},{2,10},{4,12},{6,14},{8,0},{10,2},{12,4},{14,6},{16,24},{18,... | collective-permute-start | bytes 208904 | tf_op jit(solution)/shard_map/ppermute | solution.py:50
  40.0 7.1 %collective-permute-start.12 = (bf16[272,128]{1,0:T(8,128)(2,1)S(1)}, bf16[272,128]{1,0:T(8,128)(2,1)S(1)}, u32[]{:S(2)}, u32[]{:S(2)}) collective-permute-start(bf16[272,128]{1,0:T(8,128)(2,1)S(1)} %pad_maximum_fusion.31), channel_id=1, source_target_pairs={{0,8},{2,10},{4,12},{6,14},{8,0},{10,2},{12,4},{14,6},{16,24},{18,... | collective-permute-start | bytes 208904 | tf_op jit(solution)/shard_map/ppermute | solution.py:50
  41.2 6.0 %collective-permute-start.11 = (bf16[272,128]{1,0:T(8,128)(2,1)S(1)}, bf16[272,128]{1,0:T(8,128)(2,1)S(1)}, u32[]{:S(2)}, u32[]{:S(2)}) collective-permute-start(bf16[272,128]{1,0:T(8,128)(2,1)S(1)} %pad_maximum_fusion.31), channel_id=1, source_target_pairs={{0,16},{2,18},{4,20},{6,22},{8,24},{10,26},{12,28},{14,30},{16,0},... | collective-permute-start | bytes 208904 | tf_op jit(solution)/shard_map/ppermute | solution.py:50
  43.0 6.1 %collective-permute-start.10 = (bf16[272,128]{1,0:T(8,128)(2,1)S(1)}, bf16[272,128]{1,0:T(8,128)(2,1)S(1)}, u32[]{:S(2)}, u32[]{:S(2)}) collective-permute-start(bf16[272,128]{1,0:T(8,128)(2,1)S(1)} %pad_maximum_fusion.31), channel_id=1, source_target_pairs={{0,24},{2,26},{4,28},{6,30},{8,16},{10,18},{12,20},{14,22},{16,8},... | collective-permute-start | bytes 208904 | tf_op jit(solution)/shard_map/ppermute | solution.py:50
  49.2 5.2 %collective-permute-start.14 = (bf16[144,512]{1,0:T(8,128)(2,1)S(1)}, bf16[144,512]{1,0:T(8,128)(2,1)S(1)}, u32[]{:S(2)}, u32[]{:S(2)}) collective-permute-start(bf16[144,512]{1,0:T(8,128)(2,1)S(1)} %pad_maximum_fusion.17), channel_id=1, source_target_pairs={{0,4},{2,6},{4,0},{6,2},{8,12},{10,14},{12,8},{14,10},{16,20},{18,... | collective-permute-start | bytes 442376 | tf_op jit(solution)/shard_map/ppermute | solution.py:50
  50.8 6.6 %collective-permute-start.21 = (f32[1,16,1024]{2,1,0:T(8,128)S(1)}, f32[1,16,1024]{2,1,0:T(8,128)S(1)}, u32[]{:S(2)}, u32[]{:S(2)}) collective-permute-start(f32[1,16,1024]{2,1,0:T(8,128)S(1)} %slice_select_fusion.3), channel_id=1, source_target_pairs={{0,2},{2,0},{4,6},{6,4},{8,10},{10,8},{12,14},{14,12},{16,18},{18,... | collective-permute-start | bytes 196616 | tf_op jit(solution)/shard_map/ppermute | solution.py:50
  54.5 3.0 %copy-start.3 = (s32[2,1]{0,1:T(1,128)S(1)}, s32[2,1]{0,1:T(1,128)}, u32[]{:S(2)}) copy-start(s32[2,1]{0,1:T(1,128)} %param.9) | copy-start | bytes 28
  54.5 7.4 %collective-permute-start.15 = (bf16[144,1024]{1,0:T(8,128)(2,1)S(1)}, bf16[144,1024]{1,0:T(8,128)(2,1)S(1)}, u32[]{:S(2)}, u32[]{:S(2)}) collective-permute-start(bf16[144,1024]{1,0:T(8,128)(2,1)S(1)} %pad_maximum_fusion.9), channel_id=1, source_target_pairs={{0,2},{2,0},{4,6},{6,4},{8,10},{10,8},{12,14},{14,12},{16,18},{18,... | collective-permute-start | bytes 884744 | tf_op jit(solution)/shard_map/ppermute | solution.py:50
  60.3 6.0 %collective-permute-start.13 = (bf16[128,512]{1,0:T(8,128)(2,1)S(1)}, bf16[128,512]{1,0:T(8,128)(2,1)S(1)}, u32[]{:S(2)}, u32[]{:S(2)}) collective-permute-start(bf16[128,512]{1,0:T(8,128)(2,1)S(1)} %pad_maximum_fusion.23), channel_id=1, source_target_pairs={{0,4},{2,6},{4,0},{6,2},{8,12},{10,14},{12,8},{14,10},{16,20},{18,... | collective-permute-start | bytes 393224 | tf_op jit(solution)/shard_map/ppermute | solution.py:50
  62.3 13.2 %copy-start.1 = (f32[1080,256]{1,0:T(8,128)S(1)}, f32[1080,256]{1,0:T(8,128)}, u32[]{:S(2)}) copy-start(f32[1080,256]{1,0:T(8,128)} %residual.1) | copy-start | bytes 3317764
  66.3 3.3 %collective-permute-start.16 = (bf16[128,1024]{1,0:T(8,128)(2,1)S(1)}, bf16[128,1024]{1,0:T(8,128)(2,1)S(1)}, u32[]{:S(2)}, u32[]{:S(2)}) collective-permute-start(bf16[128,1024]{1,0:T(8,128)(2,1)S(1)} %pad_maximum_fusion.12), channel_id=1, source_target_pairs={{0,2},{2,0},{4,6},{6,4},{8,10},{10,8},{12,14},{14,12},{16,18},{18,... | collective-permute-start | bytes 786440 | tf_op jit(solution)/shard_map/ppermute | solution.py:50
  66.4 9.1 %collective-permute-start.18 = (bf16[1080,128]{1,0:T(8,128)(2,1)S(1)}, bf16[1080,128]{1,0:T(8,128)(2,1)S(1)}, u32[]{:S(2)}, u32[]{:S(2)}) collective-permute-start(bf16[1080,128]{1,0:T(8,128)(2,1)S(1)} %get-tuple-element.361), channel_id=1, source_target_pairs={{0,1},{1,0},{2,3},{3,2},{4,5},{5,4},{6,7},{7,6},{8,9},{9,8},{10,11... | collective-permute-start | bytes 829448 | tf_op jit(solution)/shard_map/ppermute | solution.py:289
  68.0 10.7 %collective-permute-start.22 = (f32[1,32,512]{2,1,0:T(8,128)S(1)}, f32[1,32,512]{2,1,0:T(8,128)S(1)}, u32[]{:S(2)}, u32[]{:S(2)}) collective-permute-start(f32[1,32,512]{2,1,0:T(8,128)S(1)} %broadcast_select_fusion.29), channel_id=1, source_target_pairs={{0,4},{2,6},{4,0},{6,2},{8,12},{10,14},{12,8},{14,10},{16,20},{18,... | collective-permute-start | bytes 196616 | tf_op jit(solution)/shard_map/ppermute | solution.py:50
  77.0 3.3 %collective-permute-start.19 = (bf16[128,1024]{1,0:T(8,128)(2,1)S(1)}, bf16[128,1024]{1,0:T(8,128)(2,1)S(1)}, u32[]{:S(2)}, u32[]{:S(2)}) collective-permute-start(bf16[128,1024]{1,0:T(8,128)(2,1)S(1)} %select_convert_fusion.1), channel_id=1, source_target_pairs={{0,2},{2,0},{4,6},{6,4},{8,10},{10,8},{12,14},{14,12},{16,18},{18,... | collective-permute-start | bytes 786440 | tf_op jit(solution)/shard_map/ppermute | solution.py:50
  78.7 9.1 %collective-permute-start.17 = (bf16[1080,128]{1,0:T(8,128)(2,1)S(1)}, bf16[1080,128]{1,0:T(8,128)(2,1)S(1)}, u32[]{:S(2)}, u32[]{:S(2)}) collective-permute-start(bf16[1080,128]{1,0:T(8,128)(2,1)S(1)} %get-tuple-element.359), channel_id=1, source_target_pairs={{0,1},{1,0},{2,3},{3,2},{4,5},{5,4},{6,7},{7,6},{8,9},{9,8},{10,11... | collective-permute-start | bytes 829448 | tf_op jit(solution)/shard_map/ppermute | solution.py:289
  89.3 6.1 %collective-permute-start.20 = (bf16[128,1024]{1,0:T(8,128)(2,1)S(1)}, bf16[128,1024]{1,0:T(8,128)(2,1)S(1)}, u32[]{:S(2)}, u32[]{:S(2)}) collective-permute-start(bf16[128,1024]{1,0:T(8,128)(2,1)S(1)} %select_convert_fusion), channel_id=1, source_target_pairs={{0,2},{2,0},{4,6},{6,4},{8,10},{10,8},{12,14},{14,12},{16,18},{18,... | collective-permute-start | bytes 786440 | tf_op jit(solution)/shard_map/ppermute | solution.py:50
  89.4 11.0 %collective-permute-start.23 = (f32[1,64,128]{2,1,0:T(8,128)S(1)}, f32[1,64,128]{2,1,0:T(8,128)S(1)}, u32[]{:S(2)}, u32[]{:S(2)}) collective-permute-start(f32[1,64,128]{2,1,0:T(8,128)S(1)} %get-tuple-element.105), channel_id=1, source_target_pairs={{0,24},{2,26},{4,28},{6,30},{8,16},{10,18},{12,20},{14,22},{16,8},... | collective-permute-start | bytes 98312 | tf_op jit(solution)/shard_map/ppermute | solution.py:50
  91.0 9.4 %collective-permute-start.25 = (f32[1,64,128]{2,1,0:T(8,128)S(1)}, f32[1,64,128]{2,1,0:T(8,128)S(1)}, u32[]{:S(2)}, u32[]{:S(2)}) collective-permute-start(f32[1,64,128]{2,1,0:T(8,128)S(1)} %get-tuple-element.259), channel_id=1, source_target_pairs={{0,8},{2,10},{4,12},{6,14},{8,0},{10,2},{12,4},{14,6},{16,24},{18,... | collective-permute-start | bytes 98312 | tf_op jit(solution)/shard_map/ppermute | solution.py:50
  91.1 9.3 %collective-permute-start.24 = (f32[1,64,128]{2,1,0:T(8,128)S(1)}, f32[1,64,128]{2,1,0:T(8,128)S(1)}, u32[]{:S(2)}, u32[]{:S(2)}) collective-permute-start(f32[1,64,128]{2,1,0:T(8,128)S(1)} %get-tuple-element.260), channel_id=1, source_target_pairs={{0,16},{2,18},{4,20},{6,22},{8,24},{10,26},{12,28},{14,30},{16,0},... | collective-permute-start | bytes 98312 | tf_op jit(solution)/shard_map/ppermute | solution.py:50
  93.9 6.4 %collective-permute-start.26 = (bf16[128,512]{1,0:T(8,128)(2,1)S(1)}, bf16[128,512]{1,0:T(8,128)(2,1)S(1)}, u32[]{:S(2)}, u32[]{:S(2)}) collective-permute-start(bf16[128,512]{1,0:T(8,128)(2,1)S(1)} %select_convert_fusion.5), channel_id=1, source_target_pairs={{0,4},{2,6},{4,0},{6,2},{8,12},{10,14},{12,8},{14,10},{16,20},{18,... | collective-permute-start | bytes 393224 | tf_op jit(solution)/shard_map/ppermute | solution.py:50
  95.6 10.1 %collective-permute-start.28 = (bf16[128,512]{1,0:T(8,128)(2,1)S(1)}, bf16[128,512]{1,0:T(8,128)(2,1)S(1)}, u32[]{:S(2)}, u32[]{:S(2)}) collective-permute-start(bf16[128,512]{1,0:T(8,128)(2,1)S(1)} %select_convert_fusion.4), channel_id=1, source_target_pairs={{0,4},{2,6},{4,0},{6,2},{8,12},{10,14},{12,8},{14,10},{16,20},{18,... | collective-permute-start | bytes 393224 | tf_op jit(solution)/shard_map/ppermute | solution.py:50
  101.3 6.7 %collective-permute-start.30 = (bf16[128,128]{1,0:T(8,128)(2,1)S(1)}, bf16[128,128]{1,0:T(8,128)(2,1)S(1)}, u32[]{:S(2)}, u32[]{:S(2)}) collective-permute-start(bf16[128,128]{1,0:T(8,128)(2,1)S(1)} %get-tuple-element.235), channel_id=1, source_target_pairs={{0,24},{2,26},{4,28},{6,30},{8,16},{10,18},{12,20},{14,22},{16,8},... | collective-permute-start | bytes 98312 | tf_op jit(solution)/shard_map/ppermute | solution.py:50
  102.8 7.5 %collective-permute-start.27 = (bf16[128,128]{1,0:T(8,128)(2,1)S(1)}, bf16[128,128]{1,0:T(8,128)(2,1)S(1)}, u32[]{:S(2)}, u32[]{:S(2)}) collective-permute-start(bf16[128,128]{1,0:T(8,128)(2,1)S(1)} %get-tuple-element.236), channel_id=1, source_target_pairs={{0,8},{2,10},{4,12},{6,14},{8,0},{10,2},{12,4},{14,6},{16,24},{18,... | collective-permute-start | bytes 98312 | tf_op jit(solution)/shard_map/ppermute | solution.py:50
  102.8 7.4 %collective-permute-start.29 = (bf16[128,128]{1,0:T(8,128)(2,1)S(1)}, bf16[128,128]{1,0:T(8,128)(2,1)S(1)}, u32[]{:S(2)}, u32[]{:S(2)}) collective-permute-start(bf16[128,128]{1,0:T(8,128)(2,1)S(1)} %get-tuple-element.237), channel_id=1, source_target_pairs={{0,16},{2,18},{4,20},{6,22},{8,24},{10,26},{12,28},{14,30},{16,0},... | collective-permute-start | bytes 98312 | tf_op jit(solution)/shard_map/ppermute | solution.py:50
  105.8 4.9 %collective-permute-start.32 = (bf16[128,128]{1,0:T(8,128)(2,1)S(1)}, bf16[128,128]{1,0:T(8,128)(2,1)S(1)}, u32[]{:S(2)}, u32[]{:S(2)}) collective-permute-start(bf16[128,128]{1,0:T(8,128)(2,1)S(1)} %get-tuple-element.232), channel_id=1, source_target_pairs={{0,16},{2,18},{4,20},{6,22},{8,24},{10,26},{12,28},{14,30},{16,0},... | collective-permute-start | bytes 98312 | tf_op jit(solution)/shard_map/ppermute | solution.py:50
  105.9 4.8 %collective-permute-start.31 = (bf16[128,128]{1,0:T(8,128)(2,1)S(1)}, bf16[128,128]{1,0:T(8,128)(2,1)S(1)}, u32[]{:S(2)}, u32[]{:S(2)}) collective-permute-start(bf16[128,128]{1,0:T(8,128)(2,1)S(1)} %get-tuple-element.233), channel_id=1, source_target_pairs={{0,8},{2,10},{4,12},{6,14},{8,0},{10,2},{12,4},{14,6},{16,24},{18,... | collective-permute-start | bytes 98312 | tf_op jit(solution)/shard_map/ppermute | solution.py:50
  107.9 5.8 %collective-permute-start.33 = (bf16[128,128]{1,0:T(8,128)(2,1)S(1)}, bf16[128,128]{1,0:T(8,128)(2,1)S(1)}, u32[]{:S(2)}, u32[]{:S(2)}) collective-permute-start(bf16[128,128]{1,0:T(8,128)(2,1)S(1)} %get-tuple-element.234), channel_id=1, source_target_pairs={{0,24},{2,26},{4,28},{6,30},{8,16},{10,18},{12,20},{14,22},{16,8},... | collective-permute-start | bytes 98312 | tf_op jit(solution)/shard_map/ppermute | solution.py:50
  114.0 6.1 %collective-permute-start.41 = (bf16[272,128]{1,0:T(8,128)(2,1)S(1)}, bf16[272,128]{1,0:T(8,128)(2,1)S(1)}, u32[]{:S(2)}, u32[]{:S(2)}) collective-permute-start(bf16[272,128]{1,0:T(8,128)(2,1)S(1)} %pad_maximum_fusion.32), channel_id=1, source_target_pairs={{0,8},{2,10},{4,12},{6,14},{8,0},{10,2},{12,4},{14,6},{16,24},{18,... | collective-permute-start | bytes 208904 | tf_op jit(solution)/shard_map/ppermute | solution.py:50
  114.0 6.0 %collective-permute-start.40 = (bf16[272,128]{1,0:T(8,128)(2,1)S(1)}, bf16[272,128]{1,0:T(8,128)(2,1)S(1)}, u32[]{:S(2)}, u32[]{:S(2)}) collective-permute-start(bf16[272,128]{1,0:T(8,128)(2,1)S(1)} %pad_maximum_fusion.32), channel_id=1, source_target_pairs={{0,16},{2,18},{4,20},{6,22},{8,24},{10,26},{12,28},{14,30},{16,0},... | collective-permute-start | bytes 208904 | tf_op jit(solution)/shard_map/ppermute | solution.py:50
  117.0 6.9 %collective-permute-start.39 = (bf16[272,128]{1,0:T(8,128)(2,1)S(1)}, bf16[272,128]{1,0:T(8,128)(2,1)S(1)}, u32[]{:S(2)}, u32[]{:S(2)}) collective-permute-start(bf16[272,128]{1,0:T(8,128)(2,1)S(1)} %pad_maximum_fusion.32), channel_id=1, source_target_pairs={{0,24},{2,26},{4,28},{6,30},{8,16},{10,18},{12,20},{14,22},{16,8},... | collective-permute-start | bytes 208904 | tf_op jit(solution)/shard_map/ppermute | solution.py:50
  118.5 6.5 %collective-permute-start.34 = (f32[4,2,2,16,128]{4,3,1,0,2:T(8,128)S(1)}, f32[4,2,2,16,128]{4,3,1,0,2:T(8,128)S(1)}, u32[]{:S(2)}, u32[]{:S(2)}) collective-permute-start(f32[4,2,2,16,128]{4,3,1,0,2:T(8,128)S(1)} %fusion.8), channel_id=1, source_target_pairs={{0,4},{2,6},{4,0},{6,2},{8,12},{10,14},{12,8},{14,10},{16,20},{18,... | collective-permute-start | bytes 393224 | tf_op jit(solution)/shard_map/ppermute | solution.py:50
  124.0 14.4 %collective-permute-start.45 = (bf16[128,512]{1,0:T(8,128)(2,1)S(1)}, bf16[128,512]{1,0:T(8,128)(2,1)S(1)}, u32[]{:S(2)}, u32[]{:S(2)}) collective-permute-start(bf16[128,512]{1,0:T(8,128)(2,1)S(1)} %pad_maximum_fusion.21), channel_id=1, source_target_pairs={{0,4},{2,6},{4,0},{6,2},{8,12},{10,14},{12,8},{14,10},{16,20},{18,... | collective-permute-start | bytes 393224 | tf_op jit(solution)/shard_map/ppermute | solution.py:50
  125.1 6.2 %collective-permute-start.35 = (f32[2,2,2,16,128]{4,3,1,2,0:T(8,128)S(1)}, f32[2,2,2,16,128]{4,3,1,2,0:T(8,128)S(1)}, u32[]{:S(2)}, u32[]{:S(2)}) collective-permute-start(f32[2,2,2,16,128]{4,3,1,2,0:T(8,128)S(1)} %get-tuple-element.96), channel_id=1, source_target_pairs={{0,24},{2,26},{4,28},{6,30},{8,16},{10,18},{12,20},{14,22},{16,8},... | collective-permute-start | bytes 196616 | tf_op jit(solution)/shard_map/ppermute | solution.py:50
  127.1 4.8 %collective-permute-start.37 = (f32[2,2,2,16,128]{4,3,1,2,0:T(8,128)S(1)}, f32[2,2,2,16,128]{4,3,1,2,0:T(8,128)S(1)}, u32[]{:S(2)}, u32[]{:S(2)}) collective-permute-start(f32[2,2,2,16,128]{4,3,1,2,0:T(8,128)S(1)} %get-tuple-element.227), channel_id=1, source_target_pairs={{0,8},{2,10},{4,12},{6,14},{8,0},{10,2},{12,4},{14,6},{16,24},{18,... | collective-permute-start | bytes 196616 | tf_op jit(solution)/shard_map/ppermute | solution.py:50
  128.3 5.9 %collective-permute-start.36 = (f32[2,2,2,16,128]{4,3,1,2,0:T(8,128)S(1)}, f32[2,2,2,16,128]{4,3,1,2,0:T(8,128)S(1)}, u32[]{:S(2)}, u32[]{:S(2)}) collective-permute-start(f32[2,2,2,16,128]{4,3,1,2,0:T(8,128)S(1)} %get-tuple-element.228), channel_id=1, source_target_pairs={{0,16},{2,18},{4,20},{6,22},{8,24},{10,26},{12,28},{14,30},{16,0},... | collective-permute-start | bytes 196616 | tf_op jit(solution)/shard_map/ppermute | solution.py:50
  129.7 5.2 %collective-permute-start.42 = (bf16[144,512]{1,0:T(8,128)(2,1)S(1)}, bf16[144,512]{1,0:T(8,128)(2,1)S(1)}, u32[]{:S(2)}, u32[]{:S(2)}) collective-permute-start(bf16[144,512]{1,0:T(8,128)(2,1)S(1)} %slice.1056), channel_id=1, source_target_pairs={{0,4},{2,6},{4,0},{6,2},{8,12},{10,14},{12,8},{14,10},{16,20},{18,... | collective-permute-start | bytes 442376 | tf_op jit(solution)/shard_map/ppermute | solution.py:50
  134.3 1.4 collective-permute-start.38
  135.0 1.6 %collective-permute-start.43 = (bf16[144,1024]{1,0:T(8,128)(2,1)S(1)}, bf16[144,1024]{1,0:T(8,128)(2,1)S(1)}, u32[]{:S(2)}, u32[]{:S(2)}) collective-permute-start(bf16[144,1024]{1,0:T(8,128)(2,1)S(1)} %pad_maximum_fusion.10), channel_id=1, source_target_pairs={{0,2},{2,0},{4,6},{6,4},{8,10},{10,8},{12,14},{14,12},{16,18},{18,... | collective-permute-start | bytes 884744 | tf_op jit(solution)/shard_map/ppermute | solution.py:50
  138.5 2.4 %collective-permute-start.46 = (bf16[128,1024]{1,0:T(8,128)(2,1)S(1)}, bf16[128,1024]{1,0:T(8,128)(2,1)S(1)}, u32[]{:S(2)}, u32[]{:S(2)}) collective-permute-start(bf16[128,1024]{1,0:T(8,128)(2,1)S(1)} %pad_maximum_fusion.15), channel_id=1, source_target_pairs={{0,2},{2,0},{4,6},{6,4},{8,10},{10,8},{12,14},{14,12},{16,18},{18,... | collective-permute-start | bytes 786440 | tf_op jit(solution)/shard_map/ppermute | solution.py:50
  139.4 9.5 %collective-permute-start.44 = (bf16[1080,128]{1,0:T(8,128)(2,1)S(1)}, bf16[1080,128]{1,0:T(8,128)(2,1)S(1)}, u32[]{:S(2)}, u32[]{:S(2)}) collective-permute-start(bf16[1080,128]{1,0:T(8,128)(2,1)S(1)} %get-tuple-element.365), channel_id=1, source_target_pairs={{0,1},{1,0},{2,3},{3,2},{4,5},{5,4},{6,7},{7,6},{8,9},{9,8},{10,11... | collective-permute-start | bytes 829448 | tf_op jit(solution)/shard_map/ppermute | solution.py:289
  142.8 11.5 %collective-permute-start.47 = (bf16[1080,128]{1,0:T(8,128)(2,1)S(1)}, bf16[1080,128]{1,0:T(8,128)(2,1)S(1)}, u32[]{:S(2)}, u32[]{:S(2)}) collective-permute-start(bf16[1080,128]{1,0:T(8,128)(2,1)S(1)} %get-tuple-element.363), channel_id=1, source_target_pairs={{0,1},{1,0},{2,3},{3,2},{4,5},{5,4},{6,7},{7,6},{8,9},{9,8},{10,11... | collective-permute-start | bytes 829448 | tf_op jit(solution)/shard_map/ppermute | solution.py:289

commit v4 on v3

--- a/solution.py
+++ b/solution.py
@@ -486,9 +486,9 @@
         own, other = pending[c]
         residuals[c] = residuals[c] - (own + other)
 
-    home = [new.reshape([stage.radix for stage in reversed(all_stages)] + [rows_own, width]) for new in news]
+    home = [new.astype(BF16).reshape([stage.radix for stage in reversed(all_stages)] + [rows_own, width]) for new in news]
     home = jnp.stack(home, axis=len(all_stages))
-    steps = [(top, 1, []), (top + 1, 1, [])] + [
+    steps = [(top, 1, pieces[-1:]), (top + 1, 1, [])] + [
         (i, len(all_stages) - 1 - i, []) for i in reversed(range(top))
     ]
     for i, axis, gate in steps:
@@ -498,7 +498,7 @@
     found = list(range(top)) + [top + 1, top]
     home = jnp.transpose(home, [found.index(i) for i in range(len(found))] + [len(found) + j for j in range(3)])
     home = home.reshape(samp, ROUNDS, rows_own, width)
-    new_rows = [jnp.concatenate([home[s, r] for s in range(samp)], axis=-1) for r in range(ROUNDS)]
+    new_rows = [jnp.concatenate([home[s, r] for s in range(samp)], axis=-1).astype(F32) for r in range(ROUNDS)]
     out = []
     for block in range(n_blocks):
         piece = coefficients[:, block * BS : (block + 1) * BS]

time: 156 us -> 159 us (1.019)
  waiting for transfers between devices: 59.8 us -> 62.4 us
    ppermute x44, waiting for transfers between devices: 36.3 us -> 38.9 us  [send(): return lax.ppermute(value, 'samp', self.pairs(step))]
  transfers between devices with their start and end apart: 48 -> 48, of which waited for: 24 -> 21; matrix products, arithmetic and copies ran while one was open for 10% -> 10% of each run, Pallas kernels for 4% -> 4%
where the time goes in v4:
time: 159 us; the launch traced here: 158 us
  waiting for transfers between devices  62.4 us (39%)
  starting transfers between devices  57.4 us (36%)
  Pallas kernels  11.2 us (7%)
  matrix products  9.33 us (6%)
  other arithmetic  7.4 us (5%)
  between operations  6.08 us (4%)
  local copies, waits for them, and re-layouts  4.37 us (3%)
    ppermute x44, starting transfers between devices, send(): return lax.ppermute(value, 'samp', self.pairs(step))  52 us
    ppermute x44, waiting for transfers between devices, send(): return lax.ppermute(value, 'samp', self.pairs(step))  38.9 us
    ppermute x4, waiting for transfers between devices, over_var(): lax.ppermute(value.astype(BF16), 'var', [(i, i ^ step) for i in range(siz...  23.5 us
    dot_general x4, matrix products, descent(): lax.dot_general(values[r], piece, (((1,), (1,)), ((), ())), preferred_ele...  5.94 us
    pallas_call x2, Pallas kernels, chosen_block(): pl.pallas_call(functools.partial(block_kernel, r), out_shape=jax.ShapeDty...  5.7 us
    pallas_call x1, Pallas kernels, head(): pl.pallas_call(head_kernel, out_shape=[jax.ShapeDtypeStruct((phenotypes,...  5.5 us
    ppermute x4, starting transfers between devices, over_var(): lax.ppermute(value.astype(BF16), 'var', [(i, i ^ step) for i in range(siz...  5.44 us
  transfers between devices with their start and end apart: 48, of which 21 were waited for; matrix products, arithmetic and copies ran while one was open for 10% of the time, Pallas kernels for 4%

profile of v4, /device:TPU:0, one launch (start us, length us, event | category | flops | bytes accessed | tf_op | source)
XLA Modules:
  0.0 158.2 jit_solution(10889721780924306800)
XLA Ops:
  0.9 1.2 copy-done
  2.1 0.7 copy-done.2
  2.8 5.5 %head.1 = (f32[256,2048]{1,0:T(8,128)S(1)}, f32[4,2048]{1,0:T(4,128)S(1)}, f32[1,256]{1,0:T(1,128)S(1)}, s32[8,128]{1,0:T(8,128)S(1)}) custom-call(s32[2]{0:T(128)S(1)} %bitcast.438, bf16[1080,4096]{1,0:T(8,128)(2,1)} %genotypes.2, f32[1080,256]{1,0:T(8,128)S(1)} %copy-done), custom_call_target="tpu_custom_call" | custom-call | flops 2264924160 | bytes 8847360 | tf_op jit(solution)/shard_map/head/pallas_call | solution.py:259
  11.9 3.0 %collective-permute-start.2 = (bf16[144,512]{1,0:T(8,128)(2,1)S(1)}, bf16[144,512]{1,0:T(8,128)(2,1)S(1)}, u32[]{:S(2)}, u32[]{:S(2)}) collective-permute-start(bf16[144,512]{1,0:T(8,128)(2,1)S(1)} %pad_maximum_fusion.21), channel_id=1, source_target_pairs={{0,4},{2,6},{4,0},{6,2},{8,12},{10,14},{12,8},{14,10},{16,20},{18,... | collective-permute-start | bytes 442376 | tf_op jit(solution)/shard_map/ppermute | solution.py:50
  15.4 0.7 collective-permute-start.4
  16.2 0.8 fusion.82
  17.0 2.7 %collective-permute-done.2 = bf16[144,512]{1,0:T(8,128)(2,1)S(1)} collective-permute-done((bf16[144,512]{1,0:T(8,128)(2,1)S(1)}, bf16[144,512]{1,0:T(8,128)(2,1)S(1)}, u32[]{:S(2)}, u32[]{:S(2)}) %collective-permute-start.2) | collective-permute-done | bytes 147488 | tf_op jit(solution)/shard_map/ppermute | solution.py:50
  20.2 3.2 %collective-permute-start.5 = (bf16[144,128]{1,0:T(8,128)(2,1)S(1)}, bf16[144,128]{1,0:T(8,128)(2,1)S(1)}, u32[]{:S(2)}, u32[]{:S(2)}) collective-permute-start(bf16[144,128]{1,0:T(8,128)(2,1)S(1)} %pad_maximum_fusion.39), channel_id=1, source_target_pairs={{0,16},{2,18},{4,20},{6,22},{8,24},{10,26},{12,28},{14,30},{16,0},... | collective-permute-start | bytes 110600 | tf_op jit(solution)/shard_map/ppermute | solution.py:50
  23.5 1.6 %collective-permute-start.3 = (bf16[144,128]{1,0:T(8,128)(2,1)S(1)}, bf16[144,128]{1,0:T(8,128)(2,1)S(1)}, u32[]{:S(2)}, u32[]{:S(2)}) collective-permute-start(bf16[144,128]{1,0:T(8,128)(2,1)S(1)} %pad_maximum_fusion.38), channel_id=1, source_target_pairs={{0,8},{2,10},{4,12},{6,14},{8,0},{10,2},{12,4},{14,6},{16,24},{18,... | collective-permute-start | bytes 110600 | tf_op jit(solution)/shard_map/ppermute | solution.py:50
  25.7 2.2 %collective-permute-done.3 = bf16[144,128]{1,0:T(8,128)(2,1)S(1)} collective-permute-done((bf16[144,128]{1,0:T(8,128)(2,1)S(1)}, bf16[144,128]{1,0:T(8,128)(2,1)S(1)}, u32[]{:S(2)}, u32[]{:S(2)}) %collective-permute-start.3) | collective-permute-done | bytes 36896 | tf_op jit(solution)/shard_map/ppermute | solution.py:50
  27.9 3.1 %collective-permute-done.6 = bf16[144,128]{1,0:T(8,128)(2,1)S(1)} collective-permute-done((bf16[144,128]{1,0:T(8,128)(2,1)S(1)}, bf16[144,128]{1,0:T(8,128)(2,1)S(1)}, u32[]{:S(2)}, u32[]{:S(2)}) %collective-permute-start.6) | collective-permute-done | bytes 36896 | tf_op jit(solution)/shard_map/ppermute | solution.py:50
  32.0 3.9 %collective-permute-start.9 = (bf16[272,128]{1,0:T(8,128)(2,1)S(1)}, bf16[272,128]{1,0:T(8,128)(2,1)S(1)}, u32[]{:S(2)}, u32[]{:S(2)}) collective-permute-start(bf16[272,128]{1,0:T(8,128)(2,1)S(1)} %get-tuple-element.301), channel_id=1, source_target_pairs={{0,8},{2,10},{4,12},{6,14},{8,0},{10,2},{12,4},{14,6},{16,24},{18,... | collective-permute-start | bytes 208904 | tf_op jit(solution)/shard_map/ppermute | solution.py:50
  35.9 1.4 collective-permute-done.7
  37.4 1.1 collective-permute-done.8
  38.5 1.1 collective-permute-done.9
  40.0 1.2 collective-permute-start.12
  41.2 1.7 %collective-permute-start.11 = (bf16[272,128]{1,0:T(8,128)(2,1)S(1)}, bf16[272,128]{1,0:T(8,128)(2,1)S(1)}, u32[]{:S(2)}, u32[]{:S(2)}) collective-permute-start(bf16[272,128]{1,0:T(8,128)(2,1)S(1)} %pad_maximum_fusion.32), channel_id=1, source_target_pairs={{0,16},{2,18},{4,20},{6,22},{8,24},{10,26},{12,28},{14,30},{16,0},... | collective-permute-start | bytes 208904 | tf_op jit(solution)/shard_map/ppermute | solution.py:50
  43.0 1.5 collective-permute-start.10
  45.8 1.4 collective-permute-done.11
  47.2 1.9 %collective-permute-done.10 = bf16[272,128]{1,0:T(8,128)(2,1)S(1)} collective-permute-done((bf16[272,128]{1,0:T(8,128)(2,1)S(1)}, bf16[272,128]{1,0:T(8,128)(2,1)S(1)}, u32[]{:S(2)}, u32[]{:S(2)}) %collective-permute-start.10) | collective-permute-done | bytes 69664 | tf_op jit(solution)/shard_map/ppermute | solution.py:50
  49.2 1.6 collective-permute-start.14
  50.9 3.6 %collective-permute-done.14 = bf16[144,512]{1,0:T(8,128)(2,1)S(1)} collective-permute-done((bf16[144,512]{1,0:T(8,128)(2,1)S(1)}, bf16[144,512]{1,0:T(8,128)(2,1)S(1)}, u32[]{:S(2)}, u32[]{:S(2)}) %collective-permute-start.14) | collective-permute-done | bytes 147488 | tf_op jit(solution)/shard_map/ppermute | solution.py:50
  54.6 2.8 %shard_map.69 = bf16[1080,2048]{1,0:T(8,128)(2,1)S(1)} custom-call(s32[2]{0:T(128)S(1)} %bitcast.439, bf16[1080,4096]{1,0:T(8,128)(2,1)} %genotypes.2), custom_call_target="tpu_custom_call" | custom-call | flops 1000000000 | bytes 4423680 | tf_op jit(solution)/shard_map/pallas_call | solution.py:313
  57.4 2.8 %shard_map.68 = bf16[1080,2048]{1,0:T(8,128)(2,1)S(1)} custom-call(s32[2]{0:T(128)S(1)} %bitcast.440, bf16[1080,4096]{1,0:T(8,128)(2,1)} %genotypes.2), custom_call_target="tpu_custom_call" | custom-call | flops 1000000000 | bytes 4423680 | tf_op jit(solution)/shard_map/pallas_call | solution.py:313
  60.3 1.6 collective-permute-start.13
  62.3 1.4 fusion.91
  63.7 2.6 %collective-permute-done.13 = bf16[128,512]{1,0:T(8,128)(2,1)S(1)} collective-permute-done((bf16[128,512]{1,0:T(8,128)(2,1)S(1)}, bf16[128,512]{1,0:T(8,128)(2,1)S(1)}, u32[]{:S(2)}, u32[]{:S(2)}) %collective-permute-start.13) | collective-permute-done | bytes 131104 | tf_op jit(solution)/shard_map/ppermute | solution.py:50
  66.4 1.6 %collective-permute-start.18 = (bf16[1080,128]{1,0:T(8,128)(2,1)S(1)}, bf16[1080,128]{1,0:T(8,128)(2,1)S(1)}, u32[]{:S(2)}, u32[]{:S(2)}) collective-permute-start(bf16[1080,128]{1,0:T(8,128)(2,1)S(1)} %get-tuple-element.363), channel_id=1, source_target_pairs={{0,1},{1,0},{2,3},{3,2},{4,5},{5,4},{6,7},{7,6},{8,9},{9,8},{10,11... | collective-permute-start | bytes 829448 | tf_op jit(solution)/shard_map/ppermute | solution.py:289
  68.0 1.6 collective-permute-start.22
  70.0 5.5 %collective-permute-done.18 = bf16[1080,128]{1,0:T(8,128)(2,1)S(1)} collective-permute-done((bf16[1080,128]{1,0:T(8,128)(2,1)S(1)}, bf16[1080,128]{1,0:T(8,128)(2,1)S(1)}, u32[]{:S(2)}, u32[]{:S(2)}) %collective-permute-start.18) | collective-permute-done | bytes 276512 | tf_op jit(solution)/shard_map/ppermute | solution.py:289
  75.7 1.2 convolution_subtract_fusion.5
  77.1 1.6 %fusion.90 = (bf16[1080,128]{1,0:T(8,128)(2,1)S(1)}, f32[1080,128]{1,0:T(8,128)S(1)}) fusion(f32[128]{0:T(128)S(1)} %convolution_reduce_fusion.2, bf16[1080,2048]{1,0:T(8,128)(2,1)S(1)} %shard_map.68, bf16[128,1024]{1,0:T(8,128)(2,1)S(1)} %get-tuple-element.167, bf16[128,1024]{1,0:T(8,128)(2,1)S(1)} %get-tuple-element.166), kind=kOutput, calls=%fused_computation.495 | convolution fusion | flops 567556096 | bytes 5777920 | tf_op jit(solution)/shard_map/dot_general | solution.py:476
  78.7 1.6 %collective-permute-start.17 = (bf16[1080,128]{1,0:T(8,128)(2,1)S(1)}, bf16[1080,128]{1,0:T(8,128)(2,1)S(1)}, u32[]{:S(2)}, u32[]{:S(2)}) collective-permute-start(bf16[1080,128]{1,0:T(8,128)(2,1)S(1)} %get-tuple-element.361), channel_id=1, source_target_pairs={{0,1},{1,0},{2,3},{3,2},{4,5},{5,4},{6,7},{7,6},{8,9},{9,8},{10,11... | collective-permute-start | bytes 829448 | tf_op jit(solution)/shard_map/ppermute | solution.py:289
  80.5 7.3 %collective-permute-done.17 = bf16[1080,128]{1,0:T(8,128)(2,1)S(1)} collective-permute-done((bf16[1080,128]{1,0:T(8,128)(2,1)S(1)}, bf16[1080,128]{1,0:T(8,128)(2,1)S(1)}, u32[]{:S(2)}, u32[]{:S(2)}) %collective-permute-start.17) | collective-permute-done | bytes 276512 | tf_op jit(solution)/shard_map/ppermute | solution.py:289
  88.0 1.2 convolution_subtract_fusion.4
  89.4 1.6 %collective-permute-start.23 = (f32[1,64,128]{2,1,0:T(8,128)S(1)}, f32[1,64,128]{2,1,0:T(8,128)S(1)}, u32[]{:S(2)}, u32[]{:S(2)}) collective-permute-start(f32[1,64,128]{2,1,0:T(8,128)S(1)} %get-tuple-element.105), channel_id=1, source_target_pairs={{0,24},{2,26},{4,28},{6,30},{8,16},{10,18},{12,20},{14,22},{16,8},... | collective-permute-start | bytes 98312 | tf_op jit(solution)/shard_map/ppermute | solution.py:50
  91.1 2.8 %collective-permute-start.24 = (f32[1,64,128]{2,1,0:T(8,128)S(1)}, f32[1,64,128]{2,1,0:T(8,128)S(1)}, u32[]{:S(2)}, u32[]{:S(2)}) collective-permute-start(f32[1,64,128]{2,1,0:T(8,128)S(1)} %get-tuple-element.262), channel_id=1, source_target_pairs={{0,16},{2,18},{4,20},{6,22},{8,24},{10,26},{12,28},{14,30},{16,0},... | collective-permute-start | bytes 98312 | tf_op jit(solution)/shard_map/ppermute | solution.py:50
  93.9 1.5 collective-permute-start.26
  95.6 0.6 collective-permute-start.28
  96.2 4.1 %collective-permute-done.26 = bf16[128,512]{1,0:T(8,128)(2,1)S(1)} collective-permute-done((bf16[128,512]{1,0:T(8,128)(2,1)S(1)}, bf16[128,512]{1,0:T(8,128)(2,1)S(1)}, u32[]{:S(2)}, u32[]{:S(2)}) %collective-permute-start.26) | collective-permute-done | bytes 131104 | tf_op jit(solution)/shard_map/ppermute | solution.py:50
  100.5 0.8 fusion.81
  101.3 1.5 collective-permute-start.30
  102.8 2.9 %collective-permute-start.29 = (bf16[128,128]{1,0:T(8,128)(2,1)S(1)}, bf16[128,128]{1,0:T(8,128)(2,1)S(1)}, u32[]{:S(2)}, u32[]{:S(2)}) collective-permute-start(bf16[128,128]{1,0:T(8,128)(2,1)S(1)} %get-tuple-element.198), channel_id=1, source_target_pairs={{0,16},{2,18},{4,20},{6,22},{8,24},{10,26},{12,28},{14,30},{16,0},... | collective-permute-start | bytes 98312 | tf_op jit(solution)/shard_map/ppermute | solution.py:50
  105.9 2.0 %collective-permute-start.31 = (bf16[128,128]{1,0:T(8,128)(2,1)S(1)}, bf16[128,128]{1,0:T(8,128)(2,1)S(1)}, u32[]{:S(2)}, u32[]{:S(2)}) collective-permute-start(bf16[128,128]{1,0:T(8,128)(2,1)S(1)} %get-tuple-element.194), channel_id=1, source_target_pairs={{0,8},{2,10},{4,12},{6,14},{8,0},{10,2},{12,4},{14,6},{16,24},{18,... | collective-permute-start | bytes 98312 | tf_op jit(solution)/shard_map/ppermute | solution.py:50
  107.9 2.3 %collective-permute-start.33 = (bf16[128,128]{1,0:T(8,128)(2,1)S(1)}, bf16[128,128]{1,0:T(8,128)(2,1)S(1)}, u32[]{:S(2)}, u32[]{:S(2)}) collective-permute-start(bf16[128,128]{1,0:T(8,128)(2,1)S(1)} %get-tuple-element.195), channel_id=1, source_target_pairs={{0,24},{2,26},{4,28},{6,30},{8,16},{10,18},{12,20},{14,22},{16,8},... | collective-permute-start | bytes 98312 | tf_op jit(solution)/shard_map/ppermute | solution.py:50
  110.6 3.1 %collective-permute-done.33 = bf16[128,128]{1,0:T(8,128)(2,1)S(1)} collective-permute-done((bf16[128,128]{1,0:T(8,128)(2,1)S(1)}, bf16[128,128]{1,0:T(8,128)(2,1)S(1)}, u32[]{:S(2)}, u32[]{:S(2)}) %collective-permute-start.33) | collective-permute-done | bytes 32800 | tf_op jit(solution)/shard_map/ppermute | solution.py:50
  114.0 2.9 %collective-permute-start.36 = (bf16[272,128]{1,0:T(8,128)(2,1)S(1)}, bf16[272,128]{1,0:T(8,128)(2,1)S(1)}, u32[]{:S(2)}, u32[]{:S(2)}) collective-permute-start(bf16[272,128]{1,0:T(8,128)(2,1)S(1)} %pad_maximum_fusion.33), channel_id=1, source_target_pairs={{0,16},{2,18},{4,20},{6,22},{8,24},{10,26},{12,28},{14,30},{16,0},... | collective-permute-start | bytes 208904 | tf_op jit(solution)/shard_map/ppermute | solution.py:50
  117.0 1.4 collective-permute-start.35
  118.5 1.6 collective-permute-start.34
  120.0 3.4 %collective-permute-done.35 = bf16[272,128]{1,0:T(8,128)(2,1)S(1)} collective-permute-done((bf16[272,128]{1,0:T(8,128)(2,1)S(1)}, bf16[272,128]{1,0:T(8,128)(2,1)S(1)}, u32[]{:S(2)}, u32[]{:S(2)}) %collective-permute-start.35) | collective-permute-done | bytes 69664 | tf_op jit(solution)/shard_map/ppermute | solution.py:50
  123.6 1.7 %collective-permute-start.38 = (bf16[2,2,2,16,128]{4,3,1,2,0:T(8,128)(2,1)S(1)}, bf16[2,2,2,16,128]{4,3,1,2,0:T(8,128)(2,1)S(1)}, u32[]{:S(2)}, u32[]{:S(2)}) collective-permute-start(bf16[2,2,2,16,128]{4,3,1,2,0:T(8,128)(2,1)S(1)} %get-tuple-element.98), channel_id=1, source_target_pairs={{0,24},{2,26},{4,28},{6,30},{8,16},{10,18},{12,20},{14,22},{16,8},... | collective-permute-start | bytes 98312 | tf_op jit(solution)/shard_map/ppermute | solution.py:50
  125.4 2.7 %collective-permute-start.39 = (bf16[2,2,2,16,128]{4,3,1,2,0:T(8,128)(2,1)S(1)}, bf16[2,2,2,16,128]{4,3,1,2,0:T(8,128)(2,1)S(1)}, u32[]{:S(2)}, u32[]{:S(2)}) collective-permute-start(bf16[2,2,2,16,128]{4,3,1,2,0:T(8,128)(2,1)S(1)} %get-tuple-element.254), channel_id=1, source_target_pairs={{0,16},{2,18},{4,20},{6,22},{8,24},{10,26},{12,28},{14,30},{16,0},... | collective-permute-start | bytes 98312 | tf_op jit(solution)/shard_map/ppermute | solution.py:50
  129.4 1.6 collective-permute-start.45
  131.2 0.8 collective-permute-start.42
  132.7 4.9 %collective-permute-done.42 = bf16[144,512]{1,0:T(8,128)(2,1)S(1)} collective-permute-done((bf16[144,512]{1,0:T(8,128)(2,1)S(1)}, bf16[144,512]{1,0:T(8,128)(2,1)S(1)}, u32[]{:S(2)}, u32[]{:S(2)}) %collective-permute-start.42) | collective-permute-done | bytes 147488 | tf_op jit(solution)/shard_map/ppermute | solution.py:50
  137.8 1.5 collective-permute-done.43
  139.8 1.4 fusion.93
  141.5 0.7 pad_maximum_fusion.12
  142.2 1.5 collective-permute-start.44
  144.1 1.4 fusion.92
  145.5 0.7 collective-permute-start.47
  146.3 5.4 %collective-permute-done.44 = bf16[1080,128]{1,0:T(8,128)(2,1)S(1)} collective-permute-done((bf16[1080,128]{1,0:T(8,128)(2,1)S(1)}, bf16[1080,128]{1,0:T(8,128)(2,1)S(1)}, u32[]{:S(2)}, u32[]{:S(2)}) %collective-permute-start.44) | collective-permute-done | bytes 276512 | tf_op jit(solution)/shard_map/ppermute | solution.py:289
  151.8 5.2 %collective-permute-done.47 = bf16[1080,128]{1,0:T(8,128)(2,1)S(1)} collective-permute-done((bf16[1080,128]{1,0:T(8,128)(2,1)S(1)}, bf16[1080,128]{1,0:T(8,128)(2,1)S(1)}, u32[]{:S(2)}, u32[]{:S(2)}) %collective-permute-start.47) | collective-permute-done | bytes 276512 | tf_op jit(solution)/shard_map/ppermute | solution.py:289
  157.1 1.1 pad_maximum_fusion
  (267 shorter events, 10.7 us)
Async XLA Ops:
  0.9 1.2 copy-start
  2.1 0.7 copy-start.2
  2.8 8.3 %copy-start.4 = (f32[16,4096]{1,0:T(8,128)S(1)}, f32[16,4096]{1,0:T(8,128)}, u32[]{:S(2)}) copy-start(f32[16,4096]{1,0:T(8,128)} %param.7) | copy-start | bytes 786436
  8.6 2.7 %collective-permute-start.1 = (bf16[144,1024]{1,0:T(8,128)(2,1)S(1)}, bf16[144,1024]{1,0:T(8,128)(2,1)S(1)}, u32[]{:S(2)}, u32[]{:S(2)}) collective-permute-start(bf16[144,1024]{1,0:T(8,128)(2,1)S(1)} %pad_maximum_fusion.8), channel_id=1, source_target_pairs={{0,2},{2,0},{4,6},{6,4},{8,10},{10,8},{12,14},{14,12},{16,18},{18,... | collective-permute-start | bytes 884744 | tf_op jit(solution)/shard_map/ppermute | solution.py:50
  11.2 3.7 %collective-permute-start = (bf16[176,1024]{1,0:T(8,128)(2,1)S(1)}, bf16[176,1024]{1,0:T(8,128)(2,1)S(1)}, u32[]{:S(2)}, u32[]{:S(2)}) collective-permute-start(bf16[176,1024]{1,0:T(8,128)(2,1)S(1)} %pad_maximum_fusion.3), channel_id=1, source_target_pairs={{0,2},{2,0},{4,6},{6,4},{8,10},{10,8},{12,14},{14,12},{16,18},{18,... | collective-permute-start | bytes 1081352 | tf_op jit(solution)/shard_map/ppermute | solution.py:50
  11.9 7.7 %collective-permute-start.2 = (bf16[144,512]{1,0:T(8,128)(2,1)S(1)}, bf16[144,512]{1,0:T(8,128)(2,1)S(1)}, u32[]{:S(2)}, u32[]{:S(2)}) collective-permute-start(bf16[144,512]{1,0:T(8,128)(2,1)S(1)} %pad_maximum_fusion.21), channel_id=1, source_target_pairs={{0,4},{2,6},{4,0},{6,2},{8,12},{10,14},{12,8},{14,10},{16,20},{18,... | collective-permute-start | bytes 442376 | tf_op jit(solution)/shard_map/ppermute | solution.py:50
  15.4 9.9 %collective-permute-start.4 = (bf16[208,512]{1,0:T(8,128)(2,1)S(1)}, bf16[208,512]{1,0:T(8,128)(2,1)S(1)}, u32[]{:S(2)}, u32[]{:S(2)}) collective-permute-start(bf16[208,512]{1,0:T(8,128)(2,1)S(1)} %pad_maximum_fusion.14), channel_id=1, source_target_pairs={{0,4},{2,6},{4,0},{6,2},{8,12},{10,14},{12,8},{14,10},{16,20},{18,... | collective-permute-start | bytes 638984 | tf_op jit(solution)/shard_map/ppermute | solution.py:50
  20.2 7.7 %collective-permute-start.5 = (bf16[144,128]{1,0:T(8,128)(2,1)S(1)}, bf16[144,128]{1,0:T(8,128)(2,1)S(1)}, u32[]{:S(2)}, u32[]{:S(2)}) collective-permute-start(bf16[144,128]{1,0:T(8,128)(2,1)S(1)} %pad_maximum_fusion.39), channel_id=1, source_target_pairs={{0,16},{2,18},{4,20},{6,22},{8,24},{10,26},{12,28},{14,30},{16,0},... | collective-permute-start | bytes 110600 | tf_op jit(solution)/shard_map/ppermute | solution.py:50
  23.5 4.4 %collective-permute-start.3 = (bf16[144,128]{1,0:T(8,128)(2,1)S(1)}, bf16[144,128]{1,0:T(8,128)(2,1)S(1)}, u32[]{:S(2)}, u32[]{:S(2)}) collective-permute-start(bf16[144,128]{1,0:T(8,128)(2,1)S(1)} %pad_maximum_fusion.38), channel_id=1, source_target_pairs={{0,8},{2,10},{4,12},{6,14},{8,0},{10,2},{12,4},{14,6},{16,24},{18,... | collective-permute-start | bytes 110600 | tf_op jit(solution)/shard_map/ppermute | solution.py:50
  25.2 5.8 %collective-permute-start.6 = (bf16[144,128]{1,0:T(8,128)(2,1)S(1)}, bf16[144,128]{1,0:T(8,128)(2,1)S(1)}, u32[]{:S(2)}, u32[]{:S(2)}) collective-permute-start(bf16[144,128]{1,0:T(8,128)(2,1)S(1)} %pad_maximum_fusion.40), channel_id=1, source_target_pairs={{0,24},{2,26},{4,28},{6,30},{8,16},{10,18},{12,20},{14,22},{16,8},... | collective-permute-start | bytes 110600 | tf_op jit(solution)/shard_map/ppermute | solution.py:50
  31.1 6.3 %collective-permute-start.7 = (bf16[272,128]{1,0:T(8,128)(2,1)S(1)}, bf16[272,128]{1,0:T(8,128)(2,1)S(1)}, u32[]{:S(2)}, u32[]{:S(2)}) collective-permute-start(bf16[272,128]{1,0:T(8,128)(2,1)S(1)} %get-tuple-element.299), channel_id=1, source_target_pairs={{0,24},{2,26},{4,28},{6,30},{8,16},{10,18},{12,20},{14,22},{16,8},... | collective-permute-start | bytes 208904 | tf_op jit(solution)/shard_map/ppermute | solution.py:50
  31.8 6.7 %collective-permute-start.8 = (bf16[272,128]{1,0:T(8,128)(2,1)S(1)}, bf16[272,128]{1,0:T(8,128)(2,1)S(1)}, u32[]{:S(2)}, u32[]{:S(2)}) collective-permute-start(bf16[272,128]{1,0:T(8,128)(2,1)S(1)} %get-tuple-element.300), channel_id=1, source_target_pairs={{0,16},{2,18},{4,20},{6,22},{8,24},{10,26},{12,28},{14,30},{16,0},... | collective-permute-start | bytes 208904 | tf_op jit(solution)/shard_map/ppermute | solution.py:50
  32.0 7.6 %collective-permute-start.9 = (bf16[272,128]{1,0:T(8,128)(2,1)S(1)}, bf16[272,128]{1,0:T(8,128)(2,1)S(1)}, u32[]{:S(2)}, u32[]{:S(2)}) collective-permute-start(bf16[272,128]{1,0:T(8,128)(2,1)S(1)} %get-tuple-element.301), channel_id=1, source_target_pairs={{0,8},{2,10},{4,12},{6,14},{8,0},{10,2},{12,4},{14,6},{16,24},{18,... | collective-permute-start | bytes 208904 | tf_op jit(solution)/shard_map/ppermute | solution.py:50
  40.0 5.8 %collective-permute-start.12 = (bf16[272,128]{1,0:T(8,128)(2,1)S(1)}, bf16[272,128]{1,0:T(8,128)(2,1)S(1)}, u32[]{:S(2)}, u32[]{:S(2)}) collective-permute-start(bf16[272,128]{1,0:T(8,128)(2,1)S(1)} %pad_maximum_fusion.32), channel_id=1, source_target_pairs={{0,8},{2,10},{4,12},{6,14},{8,0},{10,2},{12,4},{14,6},{16,24},{18,... | collective-permute-start | bytes 208904 | tf_op jit(solution)/shard_map/ppermute | solution.py:50
  41.2 6.0 %collective-permute-start.11 = (bf16[272,128]{1,0:T(8,128)(2,1)S(1)}, bf16[272,128]{1,0:T(8,128)(2,1)S(1)}, u32[]{:S(2)}, u32[]{:S(2)}) collective-permute-start(bf16[272,128]{1,0:T(8,128)(2,1)S(1)} %pad_maximum_fusion.32), channel_id=1, source_target_pairs={{0,16},{2,18},{4,20},{6,22},{8,24},{10,26},{12,28},{14,30},{16,0},... | collective-permute-start | bytes 208904 | tf_op jit(solution)/shard_map/ppermute | solution.py:50
  43.0 6.1 %collective-permute-start.10 = (bf16[272,128]{1,0:T(8,128)(2,1)S(1)}, bf16[272,128]{1,0:T(8,128)(2,1)S(1)}, u32[]{:S(2)}, u32[]{:S(2)}) collective-permute-start(bf16[272,128]{1,0:T(8,128)(2,1)S(1)} %pad_maximum_fusion.32), channel_id=1, source_target_pairs={{0,24},{2,26},{4,28},{6,30},{8,16},{10,18},{12,20},{14,22},{16,8},... | collective-permute-start | bytes 208904 | tf_op jit(solution)/shard_map/ppermute | solution.py:50
  49.2 5.2 %collective-permute-start.14 = (bf16[144,512]{1,0:T(8,128)(2,1)S(1)}, bf16[144,512]{1,0:T(8,128)(2,1)S(1)}, u32[]{:S(2)}, u32[]{:S(2)}) collective-permute-start(bf16[144,512]{1,0:T(8,128)(2,1)S(1)} %pad_maximum_fusion.18), channel_id=1, source_target_pairs={{0,4},{2,6},{4,0},{6,2},{8,12},{10,14},{12,8},{14,10},{16,20},{18,... | collective-permute-start | bytes 442376 | tf_op jit(solution)/shard_map/ppermute | solution.py:50
  50.8 6.6 %collective-permute-start.21 = (f32[1,16,1024]{2,1,0:T(8,128)S(1)}, f32[1,16,1024]{2,1,0:T(8,128)S(1)}, u32[]{:S(2)}, u32[]{:S(2)}) collective-permute-start(f32[1,16,1024]{2,1,0:T(8,128)S(1)} %slice_select_fusion.3), channel_id=1, source_target_pairs={{0,2},{2,0},{4,6},{6,4},{8,10},{10,8},{12,14},{14,12},{16,18},{18,... | collective-permute-start | bytes 196616 | tf_op jit(solution)/shard_map/ppermute | solution.py:50
  54.5 3.0 %copy-start.3 = (s32[2,1]{0,1:T(1,128)S(1)}, s32[2,1]{0,1:T(1,128)}, u32[]{:S(2)}) copy-start(s32[2,1]{0,1:T(1,128)} %param.9) | copy-start | bytes 28
  54.5 7.4 %collective-permute-start.15 = (bf16[144,1024]{1,0:T(8,128)(2,1)S(1)}, bf16[144,1024]{1,0:T(8,128)(2,1)S(1)}, u32[]{:S(2)}, u32[]{:S(2)}) collective-permute-start(bf16[144,1024]{1,0:T(8,128)(2,1)S(1)} %pad_maximum_fusion.9), channel_id=1, source_target_pairs={{0,2},{2,0},{4,6},{6,4},{8,10},{10,8},{12,14},{14,12},{16,18},{18,... | collective-permute-start | bytes 884744 | tf_op jit(solution)/shard_map/ppermute | solution.py:50
  60.3 6.0 %collective-permute-start.13 = (bf16[128,512]{1,0:T(8,128)(2,1)S(1)}, bf16[128,512]{1,0:T(8,128)(2,1)S(1)}, u32[]{:S(2)}, u32[]{:S(2)}) collective-permute-start(bf16[128,512]{1,0:T(8,128)(2,1)S(1)} %pad_maximum_fusion.23), channel_id=1, source_target_pairs={{0,4},{2,6},{4,0},{6,2},{8,12},{10,14},{12,8},{14,10},{16,20},{18,... | collective-permute-start | bytes 393224 | tf_op jit(solution)/shard_map/ppermute | solution.py:50
  62.3 13.2 %copy-start.1 = (f32[1080,256]{1,0:T(8,128)S(1)}, f32[1080,256]{1,0:T(8,128)}, u32[]{:S(2)}) copy-start(f32[1080,256]{1,0:T(8,128)} %residual.1) | copy-start | bytes 3317764
  66.3 3.3 %collective-permute-start.16 = (bf16[128,1024]{1,0:T(8,128)(2,1)S(1)}, bf16[128,1024]{1,0:T(8,128)(2,1)S(1)}, u32[]{:S(2)}, u32[]{:S(2)}) collective-permute-start(bf16[128,1024]{1,0:T(8,128)(2,1)S(1)} %pad_maximum_fusion.11), channel_id=1, source_target_pairs={{0,2},{2,0},{4,6},{6,4},{8,10},{10,8},{12,14},{14,12},{16,18},{18,... | collective-permute-start | bytes 786440 | tf_op jit(solution)/shard_map/ppermute | solution.py:50
  66.4 9.1 %collective-permute-start.18 = (bf16[1080,128]{1,0:T(8,128)(2,1)S(1)}, bf16[1080,128]{1,0:T(8,128)(2,1)S(1)}, u32[]{:S(2)}, u32[]{:S(2)}) collective-permute-start(bf16[1080,128]{1,0:T(8,128)(2,1)S(1)} %get-tuple-element.363), channel_id=1, source_target_pairs={{0,1},{1,0},{2,3},{3,2},{4,5},{5,4},{6,7},{7,6},{8,9},{9,8},{10,11... | collective-permute-start | bytes 829448 | tf_op jit(solution)/shard_map/ppermute | solution.py:289
  68.0 10.7 %collective-permute-start.22 = (f32[1,32,512]{2,1,0:T(8,128)S(1)}, f32[1,32,512]{2,1,0:T(8,128)S(1)}, u32[]{:S(2)}, u32[]{:S(2)}) collective-permute-start(f32[1,32,512]{2,1,0:T(8,128)S(1)} %broadcast_select_fusion.29), channel_id=1, source_target_pairs={{0,4},{2,6},{4,0},{6,2},{8,12},{10,14},{12,8},{14,10},{16,20},{18,... | collective-permute-start | bytes 196616 | tf_op jit(solution)/shard_map/ppermute | solution.py:50
  77.0 3.3 %collective-permute-start.19 = (bf16[128,1024]{1,0:T(8,128)(2,1)S(1)}, bf16[128,1024]{1,0:T(8,128)(2,1)S(1)}, u32[]{:S(2)}, u32[]{:S(2)}) collective-permute-start(bf16[128,1024]{1,0:T(8,128)(2,1)S(1)} %select_convert_fusion.1), channel_id=1, source_target_pairs={{0,2},{2,0},{4,6},{6,4},{8,10},{10,8},{12,14},{14,12},{16,18},{18,... | collective-permute-start | bytes 786440 | tf_op jit(solution)/shard_map/ppermute | solution.py:50
  78.7 9.1 %collective-permute-start.17 = (bf16[1080,128]{1,0:T(8,128)(2,1)S(1)}, bf16[1080,128]{1,0:T(8,128)(2,1)S(1)}, u32[]{:S(2)}, u32[]{:S(2)}) collective-permute-start(bf16[1080,128]{1,0:T(8,128)(2,1)S(1)} %get-tuple-element.361), channel_id=1, source_target_pairs={{0,1},{1,0},{2,3},{3,2},{4,5},{5,4},{6,7},{7,6},{8,9},{9,8},{10,11... | collective-permute-start | bytes 829448 | tf_op jit(solution)/shard_map/ppermute | solution.py:289
  89.3 6.1 %collective-permute-start.20 = (bf16[128,1024]{1,0:T(8,128)(2,1)S(1)}, bf16[128,1024]{1,0:T(8,128)(2,1)S(1)}, u32[]{:S(2)}, u32[]{:S(2)}) collective-permute-start(bf16[128,1024]{1,0:T(8,128)(2,1)S(1)} %select_convert_fusion), channel_id=1, source_target_pairs={{0,2},{2,0},{4,6},{6,4},{8,10},{10,8},{12,14},{14,12},{16,18},{18,... | collective-permute-start | bytes 786440 | tf_op jit(solution)/shard_map/ppermute | solution.py:50
  89.4 11.0 %collective-permute-start.23 = (f32[1,64,128]{2,1,0:T(8,128)S(1)}, f32[1,64,128]{2,1,0:T(8,128)S(1)}, u32[]{:S(2)}, u32[]{:S(2)}) collective-permute-start(f32[1,64,128]{2,1,0:T(8,128)S(1)} %get-tuple-element.105), channel_id=1, source_target_pairs={{0,24},{2,26},{4,28},{6,30},{8,16},{10,18},{12,20},{14,22},{16,8},... | collective-permute-start | bytes 98312 | tf_op jit(solution)/shard_map/ppermute | solution.py:50
  91.0 9.4 %collective-permute-start.25 = (f32[1,64,128]{2,1,0:T(8,128)S(1)}, f32[1,64,128]{2,1,0:T(8,128)S(1)}, u32[]{:S(2)}, u32[]{:S(2)}) collective-permute-start(f32[1,64,128]{2,1,0:T(8,128)S(1)} %get-tuple-element.261), channel_id=1, source_target_pairs={{0,8},{2,10},{4,12},{6,14},{8,0},{10,2},{12,4},{14,6},{16,24},{18,... | collective-permute-start | bytes 98312 | tf_op jit(solution)/shard_map/ppermute | solution.py:50
  91.1 9.3 %collective-permute-start.24 = (f32[1,64,128]{2,1,0:T(8,128)S(1)}, f32[1,64,128]{2,1,0:T(8,128)S(1)}, u32[]{:S(2)}, u32[]{:S(2)}) collective-permute-start(f32[1,64,128]{2,1,0:T(8,128)S(1)} %get-tuple-element.262), channel_id=1, source_target_pairs={{0,16},{2,18},{4,20},{6,22},{8,24},{10,26},{12,28},{14,30},{16,0},... | collective-permute-start | bytes 98312 | tf_op jit(solution)/shard_map/ppermute | solution.py:50
  93.9 6.4 %collective-permute-start.26 = (bf16[128,512]{1,0:T(8,128)(2,1)S(1)}, bf16[128,512]{1,0:T(8,128)(2,1)S(1)}, u32[]{:S(2)}, u32[]{:S(2)}) collective-permute-start(bf16[128,512]{1,0:T(8,128)(2,1)S(1)} %select_convert_fusion.5), channel_id=1, source_target_pairs={{0,4},{2,6},{4,0},{6,2},{8,12},{10,14},{12,8},{14,10},{16,20},{18,... | collective-permute-start | bytes 393224 | tf_op jit(solution)/shard_map/ppermute | solution.py:50
  95.6 10.1 %collective-permute-start.28 = (bf16[128,512]{1,0:T(8,128)(2,1)S(1)}, bf16[128,512]{1,0:T(8,128)(2,1)S(1)}, u32[]{:S(2)}, u32[]{:S(2)}) collective-permute-start(bf16[128,512]{1,0:T(8,128)(2,1)S(1)} %select_convert_fusion.4), channel_id=1, source_target_pairs={{0,4},{2,6},{4,0},{6,2},{8,12},{10,14},{12,8},{14,10},{16,20},{18,... | collective-permute-start | bytes 393224 | tf_op jit(solution)/shard_map/ppermute | solution.py:50
  101.3 6.7 %collective-permute-start.30 = (bf16[128,128]{1,0:T(8,128)(2,1)S(1)}, bf16[128,128]{1,0:T(8,128)(2,1)S(1)}, u32[]{:S(2)}, u32[]{:S(2)}) collective-permute-start(bf16[128,128]{1,0:T(8,128)(2,1)S(1)} %get-tuple-element.196), channel_id=1, source_target_pairs={{0,24},{2,26},{4,28},{6,30},{8,16},{10,18},{12,20},{14,22},{16,8},... | collective-permute-start | bytes 98312 | tf_op jit(solution)/shard_map/ppermute | solution.py:50
  102.8 7.4 %collective-permute-start.27 = (bf16[128,128]{1,0:T(8,128)(2,1)S(1)}, bf16[128,128]{1,0:T(8,128)(2,1)S(1)}, u32[]{:S(2)}, u32[]{:S(2)}) collective-permute-start(bf16[128,128]{1,0:T(8,128)(2,1)S(1)} %get-tuple-element.197), channel_id=1, source_target_pairs={{0,8},{2,10},{4,12},{6,14},{8,0},{10,2},{12,4},{14,6},{16,24},{18,... | collective-permute-start | bytes 98312 | tf_op jit(solution)/shard_map/ppermute | solution.py:50
  102.8 7.4 %collective-permute-start.29 = (bf16[128,128]{1,0:T(8,128)(2,1)S(1)}, bf16[128,128]{1,0:T(8,128)(2,1)S(1)}, u32[]{:S(2)}, u32[]{:S(2)}) collective-permute-start(bf16[128,128]{1,0:T(8,128)(2,1)S(1)} %get-tuple-element.198), channel_id=1, source_target_pairs={{0,16},{2,18},{4,20},{6,22},{8,24},{10,26},{12,28},{14,30},{16,0},... | collective-permute-start | bytes 98312 | tf_op jit(solution)/shard_map/ppermute | solution.py:50
  105.8 4.9 %collective-permute-start.32 = (bf16[128,128]{1,0:T(8,128)(2,1)S(1)}, bf16[128,128]{1,0:T(8,128)(2,1)S(1)}, u32[]{:S(2)}, u32[]{:S(2)}) collective-permute-start(bf16[128,128]{1,0:T(8,128)(2,1)S(1)} %get-tuple-element.193), channel_id=1, source_target_pairs={{0,16},{2,18},{4,20},{6,22},{8,24},{10,26},{12,28},{14,30},{16,0},... | collective-permute-start | bytes 98312 | tf_op jit(solution)/shard_map/ppermute | solution.py:50
  105.9 4.7 %collective-permute-start.31 = (bf16[128,128]{1,0:T(8,128)(2,1)S(1)}, bf16[128,128]{1,0:T(8,128)(2,1)S(1)}, u32[]{:S(2)}, u32[]{:S(2)}) collective-permute-start(bf16[128,128]{1,0:T(8,128)(2,1)S(1)} %get-tuple-element.194), channel_id=1, source_target_pairs={{0,8},{2,10},{4,12},{6,14},{8,0},{10,2},{12,4},{14,6},{16,24},{18,... | collective-permute-start | bytes 98312 | tf_op jit(solution)/shard_map/ppermute | solution.py:50
  107.9 5.8 %collective-permute-start.33 = (bf16[128,128]{1,0:T(8,128)(2,1)S(1)}, bf16[128,128]{1,0:T(8,128)(2,1)S(1)}, u32[]{:S(2)}, u32[]{:S(2)}) collective-permute-start(bf16[128,128]{1,0:T(8,128)(2,1)S(1)} %get-tuple-element.195), channel_id=1, source_target_pairs={{0,24},{2,26},{4,28},{6,30},{8,16},{10,18},{12,20},{14,22},{16,8},... | collective-permute-start | bytes 98312 | tf_op jit(solution)/shard_map/ppermute | solution.py:50
  114.0 6.1 %collective-permute-start.37 = (bf16[272,128]{1,0:T(8,128)(2,1)S(1)}, bf16[272,128]{1,0:T(8,128)(2,1)S(1)}, u32[]{:S(2)}, u32[]{:S(2)}) collective-permute-start(bf16[272,128]{1,0:T(8,128)(2,1)S(1)} %pad_maximum_fusion.33), channel_id=1, source_target_pairs={{0,8},{2,10},{4,12},{6,14},{8,0},{10,2},{12,4},{14,6},{16,24},{18,... | collective-permute-start | bytes 208904 | tf_op jit(solution)/shard_map/ppermute | solution.py:50
  114.0 6.0 %collective-permute-start.36 = (bf16[272,128]{1,0:T(8,128)(2,1)S(1)}, bf16[272,128]{1,0:T(8,128)(2,1)S(1)}, u32[]{:S(2)}, u32[]{:S(2)}) collective-permute-start(bf16[272,128]{1,0:T(8,128)(2,1)S(1)} %pad_maximum_fusion.33), channel_id=1, source_target_pairs={{0,16},{2,18},{4,20},{6,22},{8,24},{10,26},{12,28},{14,30},{16,0},... | collective-permute-start | bytes 208904 | tf_op jit(solution)/shard_map/ppermute | solution.py:50
  117.0 6.5 %collective-permute-start.35 = (bf16[272,128]{1,0:T(8,128)(2,1)S(1)}, bf16[272,128]{1,0:T(8,128)(2,1)S(1)}, u32[]{:S(2)}, u32[]{:S(2)}) collective-permute-start(bf16[272,128]{1,0:T(8,128)(2,1)S(1)} %pad_maximum_fusion.33), channel_id=1, source_target_pairs={{0,24},{2,26},{4,28},{6,30},{8,16},{10,18},{12,20},{14,22},{16,8},... | collective-permute-start | bytes 208904 | tf_op jit(solution)/shard_map/ppermute | solution.py:50
  118.5 5.1 %collective-permute-start.34 = (bf16[4,2,2,16,128]{4,3,1,0,2:T(8,128)(2,1)S(1)}, bf16[4,2,2,16,128]{4,3,1,0,2:T(8,128)(2,1)S(1)}, u32[]{:S(2)}, u32[]{:S(2)}) collective-permute-start(bf16[4,2,2,16,128]{4,3,1,0,2:T(8,128)(2,1)S(1)} %fusion.17), channel_id=1, source_target_pairs={{0,4},{2,6},{4,0},{6,2},{8,12},{10,14},{12,8},{14,10},{16,20},{18,... | collective-permute-start | bytes 196616 | tf_op jit(solution)/shard_map/ppermute | solution.py:50
  123.6 7.4 %collective-permute-start.38 = (bf16[2,2,2,16,128]{4,3,1,2,0:T(8,128)(2,1)S(1)}, bf16[2,2,2,16,128]{4,3,1,2,0:T(8,128)(2,1)S(1)}, u32[]{:S(2)}, u32[]{:S(2)}) collective-permute-start(bf16[2,2,2,16,128]{4,3,1,2,0:T(8,128)(2,1)S(1)} %get-tuple-element.98), channel_id=1, source_target_pairs={{0,24},{2,26},{4,28},{6,30},{8,16},{10,18},{12,20},{14,22},{16,8},... | collective-permute-start | bytes 98312 | tf_op jit(solution)/shard_map/ppermute | solution.py:50
  125.3 5.7 %collective-permute-start.40 = (bf16[2,2,2,16,128]{4,3,1,2,0:T(8,128)(2,1)S(1)}, bf16[2,2,2,16,128]{4,3,1,2,0:T(8,128)(2,1)S(1)}, u32[]{:S(2)}, u32[]{:S(2)}) collective-permute-start(bf16[2,2,2,16,128]{4,3,1,2,0:T(8,128)(2,1)S(1)} %get-tuple-element.253), channel_id=1, source_target_pairs={{0,8},{2,10},{4,12},{6,14},{8,0},{10,2},{12,4},{14,6},{16,24},{18,... | collective-permute-start | bytes 98312 | tf_op jit(solution)/shard_map/ppermute | solution.py:50
  125.4 5.6 %collective-permute-start.39 = (bf16[2,2,2,16,128]{4,3,1,2,0:T(8,128)(2,1)S(1)}, bf16[2,2,2,16,128]{4,3,1,2,0:T(8,128)(2,1)S(1)}, u32[]{:S(2)}, u32[]{:S(2)}) collective-permute-start(bf16[2,2,2,16,128]{4,3,1,2,0:T(8,128)(2,1)S(1)} %get-tuple-element.254), channel_id=1, source_target_pairs={{0,16},{2,18},{4,20},{6,22},{8,24},{10,26},{12,28},{14,30},{16,0},... | collective-permute-start | bytes 98312 | tf_op jit(solution)/shard_map/ppermute | solution.py:50
  129.4 11.8 %collective-permute-start.45 = (bf16[128,512]{1,0:T(8,128)(2,1)S(1)}, bf16[128,512]{1,0:T(8,128)(2,1)S(1)}, u32[]{:S(2)}, u32[]{:S(2)}) collective-permute-start(bf16[128,512]{1,0:T(8,128)(2,1)S(1)} %pad_maximum_fusion.22), channel_id=1, source_target_pairs={{0,4},{2,6},{4,0},{6,2},{8,12},{10,14},{12,8},{14,10},{16,20},{18,... | collective-permute-start | bytes 393224 | tf_op jit(solution)/shard_map/ppermute | solution.py:50
  131.1 1.3 collective-permute-start.41
  131.2 6.4 %collective-permute-start.42 = (bf16[144,512]{1,0:T(8,128)(2,1)S(1)}, bf16[144,512]{1,0:T(8,128)(2,1)S(1)}, u32[]{:S(2)}, u32[]{:S(2)}) collective-permute-start(bf16[144,512]{1,0:T(8,128)(2,1)S(1)} %pad_maximum_fusion.15), channel_id=1, source_target_pairs={{0,4},{2,6},{4,0},{6,2},{8,12},{10,14},{12,8},{14,10},{16,20},{18,... | collective-permute-start | bytes 442376 | tf_op jit(solution)/shard_map/ppermute | solution.py:50
  137.7 1.6 %collective-permute-start.43 = (bf16[144,1024]{1,0:T(8,128)(2,1)S(1)}, bf16[144,1024]{1,0:T(8,128)(2,1)S(1)}, u32[]{:S(2)}, u32[]{:S(2)}) collective-permute-start(bf16[144,1024]{1,0:T(8,128)(2,1)S(1)} %pad_maximum_fusion.10), channel_id=1, source_target_pairs={{0,2},{2,0},{4,6},{6,4},{8,10},{10,8},{12,14},{14,12},{16,18},{18,... | collective-permute-start | bytes 884744 | tf_op jit(solution)/shard_map/ppermute | solution.py:50
  141.3 2.5 %collective-permute-start.46 = (bf16[128,1024]{1,0:T(8,128)(2,1)S(1)}, bf16[128,1024]{1,0:T(8,128)(2,1)S(1)}, u32[]{:S(2)}, u32[]{:S(2)}) collective-permute-start(bf16[128,1024]{1,0:T(8,128)(2,1)S(1)} %pad_maximum_fusion.13), channel_id=1, source_target_pairs={{0,2},{2,0},{4,6},{6,4},{8,10},{10,8},{12,14},{14,12},{16,18},{18,... | collective-permute-start | bytes 786440 | tf_op jit(solution)/shard_map/ppermute | solution.py:50
  142.2 9.5 %collective-permute-start.44 = (bf16[1080,128]{1,0:T(8,128)(2,1)S(1)}, bf16[1080,128]{1,0:T(8,128)(2,1)S(1)}, u32[]{:S(2)}, u32[]{:S(2)}) collective-permute-start(bf16[1080,128]{1,0:T(8,128)(2,1)S(1)} %get-tuple-element.367), channel_id=1, source_target_pairs={{0,1},{1,0},{2,3},{3,2},{4,5},{5,4},{6,7},{7,6},{8,9},{9,8},{10,11... | collective-permute-start | bytes 829448 | tf_op jit(solution)/shard_map/ppermute | solution.py:289
  145.5 11.5 %collective-permute-start.47 = (bf16[1080,128]{1,0:T(8,128)(2,1)S(1)}, bf16[1080,128]{1,0:T(8,128)(2,1)S(1)}, u32[]{:S(2)}, u32[]{:S(2)}) collective-permute-start(bf16[1080,128]{1,0:T(8,128)(2,1)S(1)} %get-tuple-element.365), channel_id=1, source_target_pairs={{0,1},{1,0},{2,3},{3,2},{4,5},{5,4},{6,7},{7,6},{8,9},{9,8},{10,11... | collective-permute-start | bytes 829448 | tf_op jit(solution)/shard_map/ppermute | solution.py:289
